TPU v7x, 512 devices: a whole 4x8x8 slice. The times are simulated.
512 devices in a mesh: gx: 8 (over z), gy: 64 (over x, y, core).
Axes of the slice: x: 4, y: 8, z: 8, core: 2. Of those that a mesh axis runs over, the one named last changes fastest.
Arguments:
- right_side: float32 [4194304], P(('gx', 'gy')), may hold values from -60 to 60
- reaction: float32 [4194304], P(('gx', 'gy')), may hold values from 0.5 to 2
- cell_slots: int32 [125, 65536], P(None, ('gx', 'gy')), may hold values from 0 to 12543
- cell_level: int32 [65536], P(('gx', 'gy')), may hold values from 0 to 2
- con_masters: int32 [5, 131072], P(None, ('gx', 'gy')), may hold values from 0 to 12287
- con_rows: int32 [131072], P(('gx', 'gy')), may hold values from 0 to 9
- send_lists: int32 [8, 262144], P(None, ('gx', 'gy')), may hold values from 0 to 8191
Outputs:
- solution: float32 [4194304], P(('gx', 'gy'))
- residual: float32 [4194304], P(('gx', 'gy'))
Inputs may be any that keep to these rules, and one draw needn't show every extreme that they name: `cell_slots`: column block of rank d indexes d's local list: its 8192 owned unknowns, then 512 values from each of ranks d - 1, ..., d - 4, then from d + 1, ..., d + 4, then its 256 constrained values (rank d = 64 gx + gy). `cell_level`: A cell of level l has side 2^(-l). `con_masters`: slots among the same rank's owned and ghost values. `con_rows`: row of the interpolation table: 5 fine nodes on each half of a coarse edge. `send_lists`: row j of rank s lists s's owned unknowns that fill ghost block j of rank s + j + 1 (j < 4) or of rank s - (j - 3); rows without such a rank are unused.
All inputs are finite; a program needn't handle non-finite values.
Results may differ from a plain program's by a relative error of at most 0.0002.
Values sent between devices are 32-bit elements; how exact they have to be, the bound alone decides.
No kernel may reach another device: no remote copies, remote signals or barrier semaphores. Data moves between devices by JAX's collectives and lax.ppermute only.
A program may use at most 64 MiB of HBM per device.

v0:
```python
import jax
import jax.numpy as jnp
import numpy as np
from jax import lax
from jax.sharding import Mesh
from jax.sharding import PartitionSpec as P

ITERS = 3
GX_GY = ("gx", "gy_0", "gy_1", "gy_2")


def shifted(value, axis, steps):
    count = lax.axis_size(axis)
    initial, last = (max(0, -steps), min(count, count - steps))
    return lax.ppermute(value, axis, [(source, source + steps) for source in range(initial, last)])


def one_axis_at_a_time(x, axes):
    for axis in axes:
        x = lax.psum(x, axis)
    return x


def lagrange(node_list, points):
    node_count = len(node_list)
    values = np.ones((len(points), node_count))
    derivs = np.zeros((len(points), node_count))
    for basis_node in range(node_count):
        for other_node in range(node_count):
            if other_node != basis_node:
                values[:, basis_node] = (
                    values[:, basis_node]
                    * (points - node_list[other_node])
                    / (node_list[basis_node] - node_list[other_node])
                )
        for skipped in range(node_count):
            if skipped != basis_node:
                product_term = np.ones(len(points)) / (node_list[basis_node] - node_list[skipped])
                for other_node in range(node_count):
                    if other_node != basis_node and other_node != skipped:
                        product_term = (
                            product_term
                            * (points - node_list[other_node])
                            / (node_list[basis_node] - node_list[other_node])
                        )
                derivs[:, basis_node] = derivs[:, basis_node] + product_term
    return (values, derivs)


def tables():
    gll_offset = np.sqrt(3.0 / 7.0)
    lobatto = np.array([0.0, (1.0 - gll_offset) / 2.0, 0.5, (1.0 + gll_offset) / 2.0, 1.0])
    inner_point = np.sqrt(5.0 - 2.0 * np.sqrt(10.0 / 7.0)) / 3.0
    outer_point = np.sqrt(5.0 + 2.0 * np.sqrt(10.0 / 7.0)) / 3.0
    inner_weight = (322.0 + 13.0 * np.sqrt(70.0)) / 900.0
    outer_weight = (322.0 - 13.0 * np.sqrt(70.0)) / 900.0
    points = np.array([-outer_point, -inner_point, 0.0, inner_point, outer_point])
    gauss_weights = np.array(
        [outer_weight, inner_weight, 128.0 / 225.0, inner_weight, outer_weight]
    )
    points = (points + 1.0) / 2.0
    gauss_weights = gauss_weights / 2.0
    shapes, slopes = lagrange(lobatto, points)
    fine_points = np.concatenate([lobatto / 2.0, (1.0 + lobatto) / 2.0])
    interp, unused_slopes = lagrange(lobatto, fine_points)
    quad_weights = np.kron(gauss_weights, np.kron(gauss_weights, gauss_weights))
    grad_x = np.kron(slopes, np.kron(shapes, shapes))
    grad_y = np.kron(shapes, np.kron(slopes, shapes))
    grad_z = np.kron(shapes, np.kron(shapes, slopes))
    stiffness = np.zeros((125, 125))
    for gradient in (grad_x, grad_y, grad_z):
        stiffness = stiffness + gradient.T @ (quad_weights[:, None] * gradient)
    return (jnp.asarray(interp, jnp.float32), jnp.asarray(stiffness, jnp.float32))


def cell_laplace(cell_values, cell_scale, stiffness):
    product = jnp.dot(
        stiffness, cell_values, precision=lax.Precision.HIGHEST, preferred_element_type=jnp.float32
    )
    return product * cell_scale[None, :]


def local_apply(own_values, ghosts, slot_map, cell_scale, masters, weights, stiffness):
    local_list = jnp.concatenate([own_values, ghosts.reshape(-1)])
    picked = local_list[masters]
    resolved = jnp.sum(weights * picked, axis=0)
    full_list = jnp.concatenate([local_list, resolved])
    cell_values = full_list[slot_map]
    contrib = cell_laplace(cell_values, cell_scale, stiffness)
    summed = (
        jnp.zeros(full_list.shape, jnp.float32).at[slot_map.reshape(-1)].add(contrib.reshape(-1))
    )
    split_at = local_list.shape[0]
    spread = (
        summed[:split_at]
        .at[masters.reshape(-1)]
        .add((weights * summed[split_at:][None, :]).reshape(-1))
    )
    return spread


def on_device(right_side, reaction, cell_slots, cell_level, con_masters, con_rows, send_lists):
    interp, stiffness = tables()
    block_count = send_lists.shape[0]
    half_count = block_count // 2
    offsets = [neighbour + 1 for neighbour in range(half_count)] + [
        -(neighbour + 1) for neighbour in range(half_count)
    ]
    cell_scale = jnp.exp2(-cell_level.astype(jnp.float32))
    selector = (con_rows[None, :] == jnp.arange(10, dtype=jnp.int32)[:, None]).astype(jnp.float32)
    weights = jnp.dot(interp.T, selector, precision=lax.Precision.HIGHEST)
    own_count = right_side.shape[0]
    flat_lists = send_lists.reshape(-1)

    def carry_out(packed):
        return jnp.stack(
            [
                shifted(packed[neighbour], GX_GY, offsets[neighbour])
                for neighbour in range(block_count)
            ]
        )

    def carry_back(packed):
        return jnp.stack(
            [
                shifted(packed[neighbour], GX_GY, -offsets[neighbour])
                for neighbour in range(block_count)
            ]
        )

    def operate(vector):
        ghosts = carry_out(vector[send_lists])
        spread = local_apply(
            vector, ghosts, cell_slots, cell_scale, con_masters, weights, stiffness
        )
        returned = carry_back(spread[own_count:].reshape(block_count, -1))
        result = spread[:own_count] + reaction * vector
        return result.at[flat_lists].add(returned.reshape(-1))

    def paired_sums(vector, applied):
        return (
            one_axis_at_a_time(jnp.sum(vector * vector), GX_GY),
            one_axis_at_a_time(jnp.sum(vector * applied), GX_GY),
        )

    solution = jnp.zeros_like(right_side)
    residual = right_side
    applied = operate(residual)
    norm_now, product = paired_sums(residual, applied)
    step_size = norm_now / product
    direction = residual
    applied_dir = applied
    for iteration in range(ITERS):
        solution = solution + step_size * direction
        residual = residual - step_size * applied_dir
        if iteration + 1 < ITERS:
            applied = operate(residual)
            norm_next, product = paired_sums(residual, applied)
            beta_ratio = norm_next / norm_now
            step_size = norm_next / (product - beta_ratio * norm_next / step_size)
            direction = residual + beta_ratio * direction
            applied_dir = applied + beta_ratio * applied_dir
            norm_now = norm_next
    return (solution, residual)


def solution(mesh):
    torus = Mesh(mesh.devices.reshape(mesh.shape["gx"], 4, 8, 2), ("gx", "gy_0", "gy_1", "gy_2"))
    placed = (
        P(GX_GY),
        P(GX_GY),
        P(None, GX_GY),
        P(GX_GY),
        P(None, GX_GY),
        P(GX_GY),
        P(None, GX_GY),
    )
    return jax.shard_map(
        on_device, mesh=torus, in_specs=placed, out_specs=(P(GX_GY), P(GX_GY)), check_vma=False
    )
```

profile of v0, /device:TPU:1, one launch (start us, length us, event | category | flops | bytes accessed | tf_op | source)
XLA Modules:
  0.0 1038.3 jit_solution(5382295155196519492)
XLA Ops:
  2.1 23.0 %gather_fusion = f32[4096]{0:T(1024)S(1)} fusion(f32[8192]{0:T(1024)S(1)} %copy-done, s32[4096]{0:T(1024)S(1)} %broadcast_clamp_fusion), kind=kCustom, calls=%fused_computation | custom fusion | bytes 49152 | tf_op jit(solution)/shard_map/gather | solution.py:132
  29.1 8.7 collective-permute-start.4
  37.8 6.4 collective-permute-start.3
  57.4 7.1 gather_fusion.1
  65.4 82.3 %gather_fusion.2 = f32[16000]{0:T(1024)S(1)} fusion(f32[12544]{0:T(1024)S(1)} %pad_maximum_fusion, s32[16384]{0:T(1024)S(1)} %pad_clamp_fusion), kind=kCustom, calls=%fused_computation.2 | custom fusion | bytes 192000 | tf_op jit(solution)/shard_map/gather | solution.py:88
  148.1 85.1 %scatter_custom_fusion = f32[12544]{0:T(1024)S(1)} fusion(s32[16000]{0:T(1024)S(1)} %fusion.7, f32[16000]{0:T(1024)S(1)} %bitcast.115, f32[]{:T(128)} %constant.8.clone.1), kind=kCustom, calls=%fused_computation.59 | custom fusion | flops 16000 | bytes 50180 | tf_op jit(solution)/shard_map/scatter-add | solution.py:91
  233.3 7.4 scatter_fusion
  261.9 22.5 %scatter_fusion.1 = f32[8192]{0:T(1024)S(1)} fusion(f32[8192]{0:T(1024)S(1)} %slice_add_fusion.2, s32[4096]{0:T(1024)S(1)} %bitcast.101, f32[4096]{0:T(1024)S(1)} %bitcast.112), kind=kCustom, calls=%fused_computation.11 | custom fusion | flops 4096 | bytes 65536 | tf_op jit(solution)/shard_map/scatter-add | solution.py:138
  285.0 32.7 %all-reduce.5 = (f32[]{:T(128)}, f32[]{:T(128)}) all-reduce(f32[]{:T(128)} %get-tuple-element.7, f32[]{:T(128)} %get-tuple-element.6), channel_id=1, replica_groups=mesh['gx'=8,'gy_0'=4,'gy_1'=8,'gy_2'=2] {'gx'}, use_global_device_ids=true, to_apply=%region_1.0 | all-reduce | flops 2 | bytes 16 | tf_op jit(solution)/shard_map/psum | solution.py:20
  317.6 6.6 all-reduce.8
  324.2 16.9 %all-reduce.2 = (f32[]{:T(128)}, f32[]{:T(128)}) all-reduce(f32[]{:T(128)} %get-tuple-element.24, f32[]{:T(128)} %get-tuple-element.25), channel_id=1, replica_groups=mesh['gx'=8,'gy_0'=4,'gy_1'=8,'gy_2'=2] {'gy_1'}, use_global_device_ids=true, to_apply=%region_3.0 | all-reduce | flops 2 | bytes 16 | tf_op jit(solution)/shard_map/psum | solution.py:20
  341.1 10.0 all-reduce.11
  352.4 23.0 %gather_fusion.3 = f32[4096]{0:T(1024)S(1)} fusion(f32[8192]{0:T(1024)S(1)} %multiply_subtract_fusion.2, s32[4096]{0:T(1024)S(1)} %broadcast_clamp_fusion), kind=kCustom, calls=%fused_computation.3 | custom fusion | bytes 49152 | tf_op jit(solution)/shard_map/gather | solution.py:132
  400.8 7.1 gather_fusion.4
  408.0 82.3 %gather_fusion.5 = f32[16000]{0:T(1024)S(1)} fusion(f32[12544]{0:T(1024)S(1)} %pad_maximum_fusion.1, s32[16384]{0:T(1024)S(1)} %pad_clamp_fusion), kind=kCustom, calls=%fused_computation.5 | custom fusion | bytes 192000 | tf_op jit(solution)/shard_map/gather | solution.py:88
  490.7 85.1 %scatter_custom_fusion.3 = f32[12544]{0:T(1024)S(1)} fusion(s32[16000]{0:T(1024)S(1)} %fusion.7, f32[16000]{0:T(1024)S(1)} %bitcast.116, f32[]{:T(128)} %constant.8.clone.1), kind=kCustom, calls=%fused_computation.57 | custom fusion | flops 16000 | bytes 50180 | tf_op jit(solution)/shard_map/scatter-add | solution.py:91
  575.9 7.6 scatter_fusion.2
  605.4 22.5 %scatter_fusion.3 = f32[8192]{0:T(1024)S(1)} fusion(f32[8192]{0:T(1024)S(1)} %slice_add_fusion.1, s32[4096]{0:T(1024)S(1)} %bitcast.102, f32[4096]{0:T(1024)S(1)} %bitcast.113), kind=kCustom, calls=%fused_computation.14 | custom fusion | flops 4096 | bytes 65536 | tf_op jit(solution)/shard_map/scatter-add | solution.py:138
  628.6 25.6 %all-reduce.4 = (f32[]{:T(128)}, f32[]{:T(128)}) all-reduce(f32[]{:T(128)} %get-tuple-element.5, f32[]{:T(128)} %get-tuple-element.4), channel_id=1, replica_groups=mesh['gx'=8,'gy_0'=4,'gy_1'=8,'gy_2'=2] {'gx'}, use_global_device_ids=true, to_apply=%region_15.0 | all-reduce | flops 2 | bytes 16 | tf_op jit(solution)/shard_map/psum | solution.py:20
  654.2 6.7 all-reduce.7
  660.9 20.6 %all-reduce.1 = (f32[]{:T(128)}, f32[]{:T(128)}) all-reduce(f32[]{:T(128)} %get-tuple-element.22, f32[]{:T(128)} %get-tuple-element.23), channel_id=1, replica_groups=mesh['gx'=8,'gy_0'=4,'gy_1'=8,'gy_2'=2] {'gy_1'}, use_global_device_ids=true, to_apply=%region_17.0 | all-reduce | flops 2 | bytes 16 | tf_op jit(solution)/shard_map/psum | solution.py:20
  681.5 9.6 all-reduce.10
  695.7 23.0 %gather_fusion.6 = f32[4096]{0:T(1024)S(1)} fusion(f32[8192]{0:T(1024)S(1)} %multiply_subtract_fusion.1, s32[4096]{0:T(1024)S(1)} %broadcast_clamp_fusion), kind=kCustom, calls=%fused_computation.6 | custom fusion | bytes 49152 | tf_op jit(solution)/shard_map/gather | solution.py:132
  744.1 7.1 gather_fusion.7
  751.2 82.3 %gather_fusion.8 = f32[16000]{0:T(1024)S(1)} fusion(f32[12544]{0:T(1024)S(1)} %pad_maximum_fusion.2, s32[16384]{0:T(1024)S(1)} %pad_clamp_fusion), kind=kCustom, calls=%fused_computation.8 | custom fusion | bytes 192000 | tf_op jit(solution)/shard_map/gather | solution.py:88
  833.9 85.1 %scatter_custom_fusion.6 = f32[12544]{0:T(1024)S(1)} fusion(s32[16000]{0:T(1024)S(1)} %fusion.7, f32[16000]{0:T(1024)S(1)} %bitcast.114, f32[]{:T(128)} %constant.8.clone.1), kind=kCustom, calls=%fused_computation.55 | custom fusion | flops 16000 | bytes 50180 | tf_op jit(solution)/shard_map/scatter-add | solution.py:91
  919.1 7.4 scatter_fusion.4
  948.5 22.5 %scatter_fusion.5 = f32[8192]{0:T(1024)S(1)} fusion(f32[8192]{0:T(1024)S(1)} %slice_add_fusion, s32[4096]{0:T(1024)S(1)} %bitcast.103, f32[4096]{0:T(1024)S(1)} %bitcast.111), kind=kCustom, calls=%fused_computation.17 | custom fusion | flops 4096 | bytes 65536 | tf_op jit(solution)/shard_map/scatter-add | solution.py:138
  971.6 25.5 %all-reduce.3 = (f32[]{:T(128)}, f32[]{:T(128)}) all-reduce(f32[]{:T(128)} %get-tuple-element.3, f32[]{:T(128)} %get-tuple-element.2), channel_id=1, replica_groups=mesh['gx'=8,'gy_0'=4,'gy_1'=8,'gy_2'=2] {'gx'}, use_global_device_ids=true, to_apply=%region_29.0 | all-reduce | flops 2 | bytes 16 | tf_op jit(solution)/shard_map/psum | solution.py:20
  997.1 6.6 all-reduce.6
  1003.7 20.0 %all-reduce = (f32[]{:T(128)}, f32[]{:T(128)}) all-reduce(f32[]{:T(128)} %get-tuple-element.20, f32[]{:T(128)} %get-tuple-element.21), channel_id=1, replica_groups=mesh['gx'=8,'gy_0'=4,'gy_1'=8,'gy_2'=2] {'gy_1'}, use_global_device_ids=true, to_apply=%region_31.0 | all-reduce | flops 2 | bytes 16 | tf_op jit(solution)/shard_map/psum | solution.py:20
  1023.6 10.1 all-reduce.9
  (183 shorter events, 138.0 us)
Async XLA Ops:
  25.2 19.5 %collective-permute-start.7 = (f32[512]{0:T(512)S(1)}, f32[512]{0:T(512)S(1)}, u32[]{:S(2)}, u32[]{:S(2)}) collective-permute-start(f32[512]{0:T(512)S(1)} %get-tuple-element.74), channel_id=1, source_target_pairs={{4,0},{5,1},{6,2},{7,3},{8,4},{9,5},{10,6},{11,7},{12,8},{13,9},{1... | collective-permute-start | bytes 6152 | tf_op jit(solution)/shard_map/ppermute | solution.py:15
  26.5 24.4 %collective-permute-start.6 = (f32[512]{0:T(512)S(1)}, f32[512]{0:T(512)S(1)}, u32[]{:S(2)}, u32[]{:S(2)}) collective-permute-start(f32[512]{0:T(512)S(1)} %get-tuple-element.75), channel_id=1, source_target_pairs={{3,0},{4,1},{5,2},{6,3},{7,4},{8,5},{9,6},{10,7},{11,8},{12,9},{13... | collective-permute-start | bytes 6152 | tf_op jit(solution)/shard_map/ppermute | solution.py:15
  27.8 26.5 %collective-permute-start.5 = (f32[512]{0:T(512)S(1)}, f32[512]{0:T(512)S(1)}, u32[]{:S(2)}, u32[]{:S(2)}) collective-permute-start(f32[512]{0:T(512)S(1)} %get-tuple-element.76), channel_id=1, source_target_pairs={{2,0},{3,1},{4,2},{5,3},{6,4},{7,5},{8,6},{9,7},{10,8},{11,9},{12,... | collective-permute-start | bytes 6152 | tf_op jit(solution)/shard_map/ppermute | solution.py:15
  29.1 27.1 %collective-permute-start.4 = (f32[512]{0:T(512)S(1)}, f32[512]{0:T(512)S(1)}, u32[]{:S(2)}, u32[]{:S(2)}) collective-permute-start(f32[512]{0:T(512)S(1)} %get-tuple-element.77), channel_id=1, source_target_pairs={{1,0},{2,1},{3,2},{4,3},{5,4},{6,5},{7,6},{8,7},{9,8},{10,9},{11,1... | collective-permute-start | bytes 6152 | tf_op jit(solution)/shard_map/ppermute | solution.py:15
  37.8 18.4 %collective-permute-start.3 = (f32[512]{0:T(512)S(1)}, f32[512]{0:T(512)S(1)}, u32[]{:S(2)}, u32[]{:S(2)}) collective-permute-start(f32[512]{0:T(512)S(1)} %get-tuple-element.78), channel_id=1, source_target_pairs={{0,4},{1,5},{2,6},{3,7},{4,8},{5,9},{6,10},{7,11},{8,12},{9,13},{1... | collective-permute-start | bytes 6152 | tf_op jit(solution)/shard_map/ppermute | solution.py:15
  44.6 11.6 %collective-permute-start.2 = (f32[512]{0:T(512)S(1)}, f32[512]{0:T(512)S(1)}, u32[]{:S(2)}, u32[]{:S(2)}) collective-permute-start(f32[512]{0:T(512)S(1)} %get-tuple-element.79), channel_id=1, source_target_pairs={{0,3},{1,4},{2,5},{3,6},{4,7},{5,8},{6,9},{7,10},{8,11},{9,12},{10... | collective-permute-start | bytes 6152 | tf_op jit(solution)/shard_map/ppermute | solution.py:15
  240.8 13.1 %collective-permute-start.15 = (f32[512]{0:T(512)S(1)}, f32[512]{0:T(512)S(1)}, u32[]{:S(2)}, u32[]{:S(2)}) collective-permute-start(f32[512]{0:T(512)S(1)} %get-tuple-element.48), channel_id=1, source_target_pairs={{0,4},{1,5},{2,6},{3,7},{4,8},{5,9},{6,10},{7,11},{8,12},{9,13},{1... | collective-permute-start | bytes 6152 | tf_op jit(solution)/shard_map/ppermute | solution.py:15
  242.6 12.6 %collective-permute-start.14 = (f32[512]{0:T(512)S(1)}, f32[512]{0:T(512)S(1)}, u32[]{:S(2)}, u32[]{:S(2)}) collective-permute-start(f32[512]{0:T(512)S(1)} %get-tuple-element.49), channel_id=1, source_target_pairs={{0,3},{1,4},{2,5},{3,6},{4,7},{5,8},{6,9},{7,10},{8,11},{9,12},{10... | collective-permute-start | bytes 6152 | tf_op jit(solution)/shard_map/ppermute | solution.py:15
  248.2 8.4 collective-permute-start.13
  250.1 8.4 collective-permute-start.12
  375.5 12.6 %collective-permute-start.23 = (f32[512]{0:T(512)S(1)}, f32[512]{0:T(512)S(1)}, u32[]{:S(2)}, u32[]{:S(2)}) collective-permute-start(f32[512]{0:T(512)S(1)} %get-tuple-element.66), channel_id=1, source_target_pairs={{4,0},{5,1},{6,2},{7,3},{8,4},{9,5},{10,6},{11,7},{12,8},{13,9},{1... | collective-permute-start | bytes 6152 | tf_op jit(solution)/shard_map/ppermute | solution.py:15
  376.8 17.5 %collective-permute-start.22 = (f32[512]{0:T(512)S(1)}, f32[512]{0:T(512)S(1)}, u32[]{:S(2)}, u32[]{:S(2)}) collective-permute-start(f32[512]{0:T(512)S(1)} %get-tuple-element.67), channel_id=1, source_target_pairs={{3,0},{4,1},{5,2},{6,3},{7,4},{8,5},{9,6},{10,7},{11,8},{12,9},{13... | collective-permute-start | bytes 6152 | tf_op jit(solution)/shard_map/ppermute | solution.py:15
  378.1 19.6 %collective-permute-start.21 = (f32[512]{0:T(512)S(1)}, f32[512]{0:T(512)S(1)}, u32[]{:S(2)}, u32[]{:S(2)}) collective-permute-start(f32[512]{0:T(512)S(1)} %get-tuple-element.68), channel_id=1, source_target_pairs={{2,0},{3,1},{4,2},{5,3},{6,4},{7,5},{8,6},{9,7},{10,8},{11,9},{12,... | collective-permute-start | bytes 6152 | tf_op jit(solution)/shard_map/ppermute | solution.py:15
  379.4 20.4 %collective-permute-start.20 = (f32[512]{0:T(512)S(1)}, f32[512]{0:T(512)S(1)}, u32[]{:S(2)}, u32[]{:S(2)}) collective-permute-start(f32[512]{0:T(512)S(1)} %get-tuple-element.69), channel_id=1, source_target_pairs={{1,0},{2,1},{3,2},{4,3},{5,4},{6,5},{7,6},{8,7},{9,8},{10,9},{11,1... | collective-permute-start | bytes 6152 | tf_op jit(solution)/shard_map/ppermute | solution.py:15
  381.7 18.1 %collective-permute-start.19 = (f32[512]{0:T(512)S(1)}, f32[512]{0:T(512)S(1)}, u32[]{:S(2)}, u32[]{:S(2)}) collective-permute-start(f32[512]{0:T(512)S(1)} %get-tuple-element.70), channel_id=1, source_target_pairs={{0,4},{1,5},{2,6},{3,7},{4,8},{5,9},{6,10},{7,11},{8,12},{9,13},{1... | collective-permute-start | bytes 6152 | tf_op jit(solution)/shard_map/ppermute | solution.py:15
  388.1 11.7 %collective-permute-start.18 = (f32[512]{0:T(512)S(1)}, f32[512]{0:T(512)S(1)}, u32[]{:S(2)}, u32[]{:S(2)}) collective-permute-start(f32[512]{0:T(512)S(1)} %get-tuple-element.71), channel_id=1, source_target_pairs={{0,3},{1,4},{2,5},{3,6},{4,7},{5,8},{6,9},{7,10},{8,11},{9,12},{10... | collective-permute-start | bytes 6152 | tf_op jit(solution)/shard_map/ppermute | solution.py:15
  583.5 13.8 %collective-permute-start.31 = (f32[512]{0:T(512)S(1)}, f32[512]{0:T(512)S(1)}, u32[]{:S(2)}, u32[]{:S(2)}) collective-permute-start(f32[512]{0:T(512)S(1)} %get-tuple-element.40), channel_id=1, source_target_pairs={{0,4},{1,5},{2,6},{3,7},{4,8},{5,9},{6,10},{7,11},{8,12},{9,13},{1... | collective-permute-start | bytes 6152 | tf_op jit(solution)/shard_map/ppermute | solution.py:15
  585.4 13.2 %collective-permute-start.30 = (f32[512]{0:T(512)S(1)}, f32[512]{0:T(512)S(1)}, u32[]{:S(2)}, u32[]{:S(2)}) collective-permute-start(f32[512]{0:T(512)S(1)} %get-tuple-element.41), channel_id=1, source_target_pairs={{0,3},{1,4},{2,5},{3,6},{4,7},{5,8},{6,9},{7,10},{8,11},{9,12},{10... | collective-permute-start | bytes 6152 | tf_op jit(solution)/shard_map/ppermute | solution.py:15
  591.6 8.3 collective-permute-start.29
  593.6 8.3 collective-permute-start.28
  597.3 6.4 collective-permute-start.26
  718.7 12.6 %collective-permute-start.39 = (f32[512]{0:T(512)S(1)}, f32[512]{0:T(512)S(1)}, u32[]{:S(2)}, u32[]{:S(2)}) collective-permute-start(f32[512]{0:T(512)S(1)} %get-tuple-element.58), channel_id=1, source_target_pairs={{4,0},{5,1},{6,2},{7,3},{8,4},{9,5},{10,6},{11,7},{12,8},{13,9},{1... | collective-permute-start | bytes 6152 | tf_op jit(solution)/shard_map/ppermute | solution.py:15
  720.0 17.5 %collective-permute-start.38 = (f32[512]{0:T(512)S(1)}, f32[512]{0:T(512)S(1)}, u32[]{:S(2)}, u32[]{:S(2)}) collective-permute-start(f32[512]{0:T(512)S(1)} %get-tuple-element.59), channel_id=1, source_target_pairs={{3,0},{4,1},{5,2},{6,3},{7,4},{8,5},{9,6},{10,7},{11,8},{12,9},{13... | collective-permute-start | bytes 6152 | tf_op jit(solution)/shard_map/ppermute | solution.py:15
  721.3 19.6 %collective-permute-start.37 = (f32[512]{0:T(512)S(1)}, f32[512]{0:T(512)S(1)}, u32[]{:S(2)}, u32[]{:S(2)}) collective-permute-start(f32[512]{0:T(512)S(1)} %get-tuple-element.60), channel_id=1, source_target_pairs={{2,0},{3,1},{4,2},{5,3},{6,4},{7,5},{8,6},{9,7},{10,8},{11,9},{12,... | collective-permute-start | bytes 6152 | tf_op jit(solution)/shard_map/ppermute | solution.py:15
  722.6 20.4 %collective-permute-start.36 = (f32[512]{0:T(512)S(1)}, f32[512]{0:T(512)S(1)}, u32[]{:S(2)}, u32[]{:S(2)}) collective-permute-start(f32[512]{0:T(512)S(1)} %get-tuple-element.61), channel_id=1, source_target_pairs={{1,0},{2,1},{3,2},{4,3},{5,4},{6,5},{7,6},{8,7},{9,8},{10,9},{11,1... | collective-permute-start | bytes 6152 | tf_op jit(solution)/shard_map/ppermute | solution.py:15
  724.9 18.1 %collective-permute-start.35 = (f32[512]{0:T(512)S(1)}, f32[512]{0:T(512)S(1)}, u32[]{:S(2)}, u32[]{:S(2)}) collective-permute-start(f32[512]{0:T(512)S(1)} %get-tuple-element.62), channel_id=1, source_target_pairs={{0,4},{1,5},{2,6},{3,7},{4,8},{5,9},{6,10},{7,11},{8,12},{9,13},{1... | collective-permute-start | bytes 6152 | tf_op jit(solution)/shard_map/ppermute | solution.py:15
  731.3 11.7 %collective-permute-start.34 = (f32[512]{0:T(512)S(1)}, f32[512]{0:T(512)S(1)}, u32[]{:S(2)}, u32[]{:S(2)}) collective-permute-start(f32[512]{0:T(512)S(1)} %get-tuple-element.63), channel_id=1, source_target_pairs={{0,3},{1,4},{2,5},{3,6},{4,7},{5,8},{6,9},{7,10},{8,11},{9,12},{10... | collective-permute-start | bytes 6152 | tf_op jit(solution)/shard_map/ppermute | solution.py:15
  926.5 13.8 %collective-permute-start.47 = (f32[512]{0:T(512)S(1)}, f32[512]{0:T(512)S(1)}, u32[]{:S(2)}, u32[]{:S(2)}) collective-permute-start(f32[512]{0:T(512)S(1)} %get-tuple-element.32), channel_id=1, source_target_pairs={{0,4},{1,5},{2,6},{3,7},{4,8},{5,9},{6,10},{7,11},{8,12},{9,13},{1... | collective-permute-start | bytes 6152 | tf_op jit(solution)/shard_map/ppermute | solution.py:15
  928.4 13.2 %collective-permute-start.46 = (f32[512]{0:T(512)S(1)}, f32[512]{0:T(512)S(1)}, u32[]{:S(2)}, u32[]{:S(2)}) collective-permute-start(f32[512]{0:T(512)S(1)} %get-tuple-element.33), channel_id=1, source_target_pairs={{0,3},{1,4},{2,5},{3,6},{4,7},{5,8},{6,9},{7,10},{8,11},{9,12},{10... | collective-permute-start | bytes 6152 | tf_op jit(solution)/shard_map/ppermute | solution.py:15
  934.6 8.3 collective-permute-start.45
  936.6 8.3 collective-permute-start.44
  940.3 6.4 collective-permute-start.42
  (25 other events, 298.3 us)
where the time goes:
time: 1040 us
  other arithmetic  349 us (34%)
  local copies, waits for them, and re-layouts  339 us (33%)
  blocking collectives  191 us (18%)
  starting transfers between devices  133 us (13%)
  waiting for transfers between devices  13.3 us (1%)
  between operations  11.8 us (1%)
    scatter-add x3, other arithmetic, local_apply(): jnp.zeros(full_list.shape, jnp.float32).at[slot_map.reshape(-1)]  255 us
    gather x3, local copies, waits for them, and re-layouts, local_apply(): cell_values = full_list[slot_map]  247 us
    psum x12, blocking collectives, one_axis_at_a_time(): x = lax.psum(x, axis)  191 us
    ppermute x48, starting transfers between devices, shifted(): lax.ppermute(value, axis, [(source, source + steps) for source in range(i...  133 us
    gather x3, local copies, waits for them, and re-layouts, operate(): ghosts = carry_out(vector[send_lists])  69.1 us
    scatter-add x3, other arithmetic, operate(): return result.at[flat_lists].add(returned.reshape(-1))  67.4 us
    scatter-add x3, other arithmetic, local_apply(): spread = summed[:split_at].at[masters.reshape(-1)].add((weights * summed[...  22.4 us
    gather x6, local copies, waits for them, and re-layouts, local_apply(): picked = local_list[masters]  21.3 us
  transfers between devices with their start and end apart: 48, of which 12 were waited for; matrix products, arithmetic and copies ran while one was open for 0% of the time, Pallas kernels for 0%

commit v1 on v0

v1 whole, which is shorter than its diff:
```python
import jax
import jax.numpy as jnp
import numpy as np
from jax import lax
from jax.experimental import pallas as pl
from jax.experimental.pallas import tpu as pltpu
from jax.sharding import Mesh
from jax.sharding import PartitionSpec as P

F32 = jnp.float32
BF16 = jnp.bfloat16
I32 = jnp.int32
AXES = ("gx", "gy_0", "gy_1", "gy_2")
GROUP = ("gy_1", "gy_2")
REST = ("gx", "gy_0")
OFFSETS = (1, 2, 3, 4, -1, -2, -3, -4)
MEMBERS = 16
PARTS = 3
OWN_ROWS = 64
LOCAL_ROWS = 96
FULL_ROWS = 98
PAD_ROWS = 112


def lagrange(node_list, points):
    node_count = len(node_list)
    values = np.ones((len(points), node_count))
    derivs = np.zeros((len(points), node_count))
    for basis_node in range(node_count):
        for other_node in range(node_count):
            if other_node != basis_node:
                values[:, basis_node] = (
                    values[:, basis_node]
                    * (points - node_list[other_node])
                    / (node_list[basis_node] - node_list[other_node])
                )
        for skipped in range(node_count):
            if skipped != basis_node:
                product_term = np.ones(len(points)) / (node_list[basis_node] - node_list[skipped])
                for other_node in range(node_count):
                    if other_node != basis_node and other_node != skipped:
                        product_term = (
                            product_term
                            * (points - node_list[other_node])
                            / (node_list[basis_node] - node_list[other_node])
                        )
                derivs[:, basis_node] = derivs[:, basis_node] + product_term
    return (values, derivs)


def tables():
    gll_offset = np.sqrt(3.0 / 7.0)
    lobatto = np.array([0.0, (1.0 - gll_offset) / 2.0, 0.5, (1.0 + gll_offset) / 2.0, 1.0])
    inner_point = np.sqrt(5.0 - 2.0 * np.sqrt(10.0 / 7.0)) / 3.0
    outer_point = np.sqrt(5.0 + 2.0 * np.sqrt(10.0 / 7.0)) / 3.0
    inner_weight = (322.0 + 13.0 * np.sqrt(70.0)) / 900.0
    outer_weight = (322.0 - 13.0 * np.sqrt(70.0)) / 900.0
    points = np.array([-outer_point, -inner_point, 0.0, inner_point, outer_point])
    gauss_weights = np.array(
        [outer_weight, inner_weight, 128.0 / 225.0, inner_weight, outer_weight]
    )
    points = (points + 1.0) / 2.0
    gauss_weights = gauss_weights / 2.0
    shapes, slopes = lagrange(lobatto, points)
    fine_points = np.concatenate([lobatto / 2.0, (1.0 + lobatto) / 2.0])
    interp, unused_slopes = lagrange(lobatto, fine_points)
    quad_weights = np.kron(gauss_weights, np.kron(gauss_weights, gauss_weights))
    grad_x = np.kron(slopes, np.kron(shapes, shapes))
    grad_y = np.kron(shapes, np.kron(slopes, shapes))
    grad_z = np.kron(shapes, np.kron(shapes, slopes))
    stiffness = np.zeros((128, 128))
    for gradient in (grad_x, grad_y, grad_z):
        stiffness[:125, :125] += gradient.T @ (quad_weights[:, None] * gradient)
    interp_wide = np.zeros((8, 128))
    interp_wide[:5, :10] = interp.T
    return (jnp.asarray(interp_wide, F32), jnp.asarray(stiffness, F32))


def lane_pick(rows, lanes):
    return jnp.take_along_axis(rows, lanes, axis=1, mode="promise_in_bounds")


def pick(table, slots, first, last):
    row_of = lax.shift_right_logical(slots, 7)
    lane_of = lax.bitwise_and(slots, 127)
    picked = jnp.zeros(slots.shape, F32)
    for row in range(first, last):
        spread_row = jnp.broadcast_to(table[row : row + 1, :], slots.shape)
        picked = jnp.where(row_of == row, lane_pick(spread_row, lane_of), picked)
    return picked


def split(x):
    pieces = []
    for part in range(PARTS):
        piece = x.astype(BF16)
        pieces.append(piece)
        if part + 1 < PARTS:
            x = x - piece.astype(F32)
    return pieces


def scatter_add(total, slots, values, rows):
    count = slots.shape[1]
    row_of = lax.shift_right_logical(slots, 7).astype(F32).astype(BF16)
    lane_of = lax.bitwise_and(slots, 127).astype(F32).astype(BF16)
    row_ids = lax.broadcasted_iota(I32, (rows, count), 0).astype(F32).astype(BF16)
    lane_ids = lax.broadcasted_iota(I32, (128, count), 0).astype(F32).astype(BF16)
    row_hot = jnp.where(
        row_ids == jnp.broadcast_to(row_of, (rows, count)),
        jnp.ones((rows, count), BF16),
        jnp.zeros((rows, count), BF16),
    )
    lane_hot = lane_ids == jnp.broadcast_to(lane_of, (128, count))
    none = jnp.zeros((128, count), BF16)
    lane_values = jnp.concatenate(
        [
            jnp.where(lane_hot, jnp.broadcast_to(piece, (128, count)), none)
            for piece in split(values)
        ],
        axis=0,
    )
    return total + lax.dot_general(
        row_hot, lane_values, (((1,), (1,)), ((), ())), preferred_element_type=F32
    )


def folded(total):
    result = total[:, :128]
    for part in range(1, PARTS):
        result = result + total[:, 128 * part : 128 * part + 128]
    return result


def place_sends(place, sign, sends, pull):
    for member in range(MEMBERS):
        sends[member] = jnp.zeros(sends.shape[1:], F32)
    for block, offset in enumerate(OFFSETS):
        member = lax.bitwise_and(place + sign * offset, MEMBERS - 1)
        for quarter, row in enumerate(pull(block)):
            sends[member, quarter : quarter + 1, :] = row


def arrived(place, received, relayed, offset, quarter):
    position = place + offset
    member = lax.bitwise_and(position, MEMBERS - 1)
    outside = (position < 0) | (position >= MEMBERS)
    inner = received[member, quarter : quarter + 1, :]
    outer = relayed[lax.bitwise_and(member, 3), quarter : quarter + 1, :]
    return jnp.where(outside, outer, inner)


def pick_lists(place, vector, lists, sends):
    quarters = [
        pick(vector, lists[:, 128 * quarter : 128 * quarter + 128], 0, OWN_ROWS)
        for quarter in range(4)
    ]
    place_sends(
        place, 1, sends, lambda block: [quarter[block : block + 1, :] for quarter in quarters]
    )


def first_kernel(place_ref, vector, lists, sends):
    pick_lists(place_ref[0], vector, lists, sends)


def local_kernel(
    place_ref,
    vector,
    received,
    relayed,
    slots_in,
    level,
    masters_in,
    con_row,
    interp,
    stiffness,
    reaction,
    *rest,
):
    moments_of = rest[:-6]
    own, sends, table, slots, masters, cell_values = rest[-6:]
    place = place_ref[0]
    table[0:OWN_ROWS, :] = vector[...]
    for block, offset in enumerate(OFFSETS):
        for quarter in range(4):
            row = OWN_ROWS + 4 * block + quarter
            table[row : row + 1, :] = arrived(place, received, relayed, -offset, quarter)
    slots[120:128, :] = jnp.zeros((8, 128), I32)
    slots[0:125, :] = slots_in[...]
    masters[...] = jnp.zeros((8, 256), I32)
    masters[0:5, :] = masters_in[...]
    weights = []
    for half in range(2):
        lanes = slice(128 * half, 128 * half + 128)
        weight = lane_pick(interp[...], jnp.broadcast_to(con_row[:, lanes], (8, 128)))
        weights.append(weight)
        resolved = weight * pick(table, masters[:, lanes], 0, LOCAL_ROWS)
        table[LOCAL_ROWS + half : LOCAL_ROWS + half + 1, :] = jnp.sum(
            resolved, axis=0, keepdims=True
        )
    for group in range(16):
        cell_values[8 * group : 8 * group + 8, :] = pick(
            table, slots[8 * group : 8 * group + 8, :], 0, FULL_ROWS
        )
    products = jnp.dot(
        stiffness[...],
        cell_values[...],
        precision=lax.Precision.HIGHEST,
        preferred_element_type=F32,
    )
    products = products * jnp.exp2(-level[...].astype(F32))
    if moments_of:
        energy = jnp.sum(products * cell_values[...]) + jnp.sum(
            reaction[...] * vector[...] * vector[...]
        )
        vectors = [ref[...] for ref in moments_of] + [vector[...]]
        moments = [
            jnp.sum(vectors[degree // 2] * vectors[(degree + 1) // 2]) for degree in range(5)
        ] + [energy]
    cell_values[...] = products

    def cell_rows(step, total):
        base = pl.multiple_of(8 * step, 8)
        at = slots[pl.ds(base, 8), :]
        add = cell_values[pl.ds(base, 8), :]
        for row in range(0, 8, 2):
            total = scatter_add(
                total,
                jnp.concatenate([at[row : row + 1], at[row + 1 : row + 2]], axis=1),
                jnp.concatenate([add[row : row + 1], add[row + 1 : row + 2]], axis=1),
                PAD_ROWS,
            )
        return total

    summed = folded(
        lax.fori_loop(0, 16, cell_rows, jnp.zeros((PAD_ROWS, 128 * PARTS), F32))
    )
    total = jnp.zeros((PAD_ROWS, 128 * PARTS), F32)
    back = [
        weights[half]
        * jnp.broadcast_to(summed[LOCAL_ROWS + half : LOCAL_ROWS + half + 1, :], (8, 128))
        for half in range(2)
    ]
    for node in range(5):
        total = scatter_add(
            total,
            masters[node : node + 1, :],
            jnp.concatenate([part[node : node + 1, :] for part in back], axis=1),
            PAD_ROWS,
        )
    spread = summed + folded(total)
    own[...] = spread[0:OWN_ROWS, :] + reaction[...] * vector[...]

    def ghost_rows(block):
        first = OWN_ROWS + 4 * block
        return [spread[first + quarter : first + quarter + 1, :] for quarter in range(4)]

    place_sends(place, -1, sends, ghost_rows)
    if moments_of:
        lane = lax.broadcasted_iota(I32, (1, 128), 1)
        packed = jnp.zeros((1, 128), F32)
        for degree, moment in enumerate(moments):
            packed = jnp.where(lane == degree, moment, packed)
        for member in range(MEMBERS):
            sends[member, 4:5, :] = packed


def owner_kernel(place_ref, own, received, relayed, lists, vector, *sends):
    place = place_ref[0]
    total = jnp.zeros((OWN_ROWS, 128 * PARTS), F32)
    for block, offset in enumerate(OFFSETS):
        for half in range(2):
            lanes = slice(256 * half, 256 * half + 256)
            total = scatter_add(
                total,
                lists[block : block + 1, lanes],
                jnp.concatenate(
                    [
                        arrived(place, received, relayed, offset, 2 * half + quarter)
                        for quarter in range(2)
                    ],
                    axis=1,
                ),
                OWN_ROWS,
            )
    vector[...] = own[...] + folded(total)
    if sends:
        pick_lists(place, vector, lists, sends[0])


def last_kernel(moments_in, *refs):
    v = [ref[...] for ref in refs[:4]]
    solution, residual = refs[4:]
    sums = jnp.sum(moments_in[...], axis=0, keepdims=True)
    lane = lax.broadcasted_iota(I32, (1, 128), 1)
    mu = [
        jnp.sum(jnp.where(lane == degree, sums, 0.0), axis=1, keepdims=True)
        for degree in range(6)
    ]
    zero = jnp.zeros((1, 1), F32)
    one = jnp.ones((1, 1), F32)

    def form(p, q, shift):
        value = zero
        for i, left in enumerate(p):
            for k, right in enumerate(q):
                value = value + left * right * mu[i + k + shift]
        return value

    res = [one]
    direction = [one]
    sol = [zero]
    rr = mu[0]
    for iteration in range(3):
        step = rr / form(direction, direction, 1)
        applied = [zero] + direction
        sol = [
            (sol[i] if i < len(sol) else zero) + step * direction[i]
            for i in range(len(direction))
        ]
        res = [
            (res[i] if i < len(res) else zero) - step * applied[i] for i in range(len(applied))
        ]
        if iteration < 2:
            rr_next = form(res, res, 0)
            ratio = rr_next / rr
            direction = [
                res[i] + (ratio * direction[i] if i < len(direction) else zero)
                for i in range(len(res))
            ]
            rr = rr_next
    solution[...] = sol[0] * v[0] + sol[1] * v[1] + sol[2] * v[2]
    residual[...] = res[0] * v[0] + res[1] * v[1] + res[2] * v[2] + res[3] * v[3]


def relay_pairs():
    pairs = []
    for group in range(32):
        for member in range(4):
            if group + 1 < 32:
                source = MEMBERS * group + member
                pairs.append((source, source + MEMBERS))
            if group > 0:
                source = MEMBERS * group + 12 + member
                pairs.append((source, source - MEMBERS))
    return pairs


def on_device(right_side, reaction, cell_slots, cell_level, con_masters, con_rows, send_lists):
    interp, stiffness = tables()
    place = lax.axis_index(GROUP).astype(I32)
    place_ref = place.reshape(1)
    whole = pl.BlockSpec(memory_space=pltpu.VMEM)
    scalar = pl.BlockSpec(memory_space=pltpu.SMEM)
    tile = jax.ShapeDtypeStruct((OWN_ROWS, 128), F32)
    sends = jax.ShapeDtypeStruct((MEMBERS, 4, 128), F32)
    sends_wide = jax.ShapeDtypeStruct((MEMBERS, 8, 128), F32)
    vector = right_side.reshape(OWN_ROWS, 128)
    reaction = reaction.reshape(OWN_ROWS, 128)
    level = cell_level.reshape(1, 128)
    con_row = con_rows.reshape(1, 256)
    pairs = relay_pairs()

    def exchange(packed):
        received = lax.all_to_all(packed, GROUP, 0, 0)
        first = jnp.where(place < 4, 12, 0)
        relay = lax.dynamic_slice(received, (first, 0, 0), (4, 4, 128))
        return received, lax.ppermute(relay, AXES, pairs)

    packed = pl.pallas_call(
        first_kernel,
        out_shape=sends,
        in_specs=[scalar, whole, whole],
        out_specs=whole,
        name="first_lists",
    )(place_ref, vector, send_lists)
    vectors = [vector]
    for step in range(3):
        received, relayed = exchange(packed)
        last = step == 2
        extra = vectors[:2] if last else []
        own, packed = pl.pallas_call(
            local_kernel,
            out_shape=(tile, sends_wide if last else sends),
            in_specs=[scalar] + [whole] * (10 + len(extra)),
            out_specs=(whole, whole),
            scratch_shapes=[
                pltpu.VMEM((104, 128), F32),
                pltpu.VMEM((128, 128), I32),
                pltpu.VMEM((8, 256), I32),
                pltpu.VMEM((128, 128), F32),
            ],
            name="local_apply",
        )(
            place_ref,
            vectors[-1],
            received,
            relayed,
            cell_slots,
            level,
            con_masters,
            con_row,
            interp,
            stiffness,
            reaction,
            *extra,
        )
        received, relayed = exchange(packed)
        if last:
            group_sums = jnp.sum(received[:, 4, :], axis=0)
            moments = lax.all_to_all(
                jnp.broadcast_to(group_sums[None], (32, 128)), REST, 0, 0
            )
        outs = pl.pallas_call(
            owner_kernel,
            out_shape=(tile,) if last else (tile, sends),
            in_specs=[scalar] + [whole] * 4,
            out_specs=(whole,) if last else (whole, whole),
            name="owner_sum",
        )(place_ref, own, received, relayed, send_lists)
        vectors.append(outs[0])
        if not last:
            packed = outs[1]
    solution_rows, residual_rows = pl.pallas_call(
        last_kernel,
        out_shape=(tile, tile),
        in_specs=[whole] * 5,
        out_specs=(whole, whole),
        name="combine",
    )(moments, *vectors)
    return (solution_rows.reshape(-1), residual_rows.reshape(-1))


def solution(mesh):
    torus = Mesh(mesh.devices.reshape(mesh.shape["gx"], 4, 8, 2), AXES)
    placed = (
        P(AXES),
        P(AXES),
        P(None, AXES),
        P(AXES),
        P(None, AXES),
        P(AXES),
        P(None, AXES),
    )
    return jax.shard_map(
        on_device, mesh=torus, in_specs=placed, out_specs=(P(AXES), P(AXES)), check_vma=False
    )
```

time: 1040 us -> 182 us (0.17)
  other arithmetic: 349 us -> 0.03 us
  local copies, waits for them, and re-layouts: 339 us -> 4.78 us
  blocking collectives: 191 us -> 61.1 us
  starting transfers between devices: 133 us -> 57.2 us
  Pallas kernels: 0 us -> 42.7 us
  between operations: 11.8 us -> 0.73 us
    scatter-add x9 -> x0, other arithmetic: 345 us -> none  [the longest x3 255 us: local_apply(): jnp.zeros(full_list.shape, jnp.float32).at[slot_map.reshape(-1)]]
    gather x12 -> x0, local copies, waits for them, and re-layouts: 337 us -> none  [the longest x3 247 us: local_apply(): cell_values = full_list[slot_map]]
    psum x12 -> x0, blocking collectives: 191 us -> none  [one_axis_at_a_time(): x = lax.psum(x, axis)]
    ppermute x48 -> x6, starting transfers between devices: 133 us -> 19.6 us  [exchange(): return (received, lax.ppermute(relay, AXES, pairs))]
    all_to_all x0 -> x5, blocking collectives: none -> 61.1 us  [exchange(): received = lax.all_to_all(packed, GROUP, 0, 0)]
    pallas_call x0 -> x8, Pallas kernels: none -> 42.7 us  [the longest x3 31 us: on_device(): pl.pallas_call(local_kernel, out_shape=(tile, sends_wide if last else sen...]
    all_to_all x0 -> x2, starting transfers between devices: none -> 37.7 us  [the longest x1 27.6 us: on_device(): lax.all_to_all(jnp.broadcast_to(group_sums[None], (32, 128)), REST, 0, 0)]
  transfers between devices with their start and end apart: 48 -> 8, of which waited for: 12 -> 8; matrix products, arithmetic and copies ran while one was open for 0% -> 0% of each run, Pallas kernels for 0% -> 1%
where the time goes in v1:
time: 182 us; the launch traced here: 180 us
  blocking collectives  61.1 us (34%)
  starting transfers between devices  57.2 us (31%)
  Pallas kernels  42.7 us (23%)
  waiting for transfers between devices  13.6 us (7%)
  local copies, waits for them, and re-layouts  4.78 us (3%)
    all_to_all x5, blocking collectives, exchange(): received = lax.all_to_all(packed, GROUP, 0, 0)  61.1 us
    pallas_call x3, Pallas kernels, on_device(): pl.pallas_call(local_kernel, out_shape=(tile, sends_wide if last else sen...  31 us
    all_to_all x1, starting transfers between devices, on_device(): lax.all_to_all(jnp.broadcast_to(group_sums[None], (32, 128)), REST, 0, 0)  27.6 us
    ppermute x6, starting transfers between devices, exchange(): return (received, lax.ppermute(relay, AXES, pairs))  19.6 us
    all_to_all x1, starting transfers between devices, exchange(): received = lax.all_to_all(packed, GROUP, 0, 0)  10.1 us
    pallas_call x3, Pallas kernels, on_device(): pl.pallas_call(owner_kernel, out_shape=(tile,) if last else (tile, sends)...  8.34 us
    all_to_all x1, waiting for transfers between devices, exchange(): received = lax.all_to_all(packed, GROUP, 0, 0)  7.48 us
    ppermute x6, waiting for transfers between devices, exchange(): return (received, lax.ppermute(relay, AXES, pairs))  4.65 us
  transfers between devices with their start and end apart: 8, of which 8 were waited for; matrix products, arithmetic and copies ran while one was open for 0% of the time, Pallas kernels for 1%

profile of v1, /device:TPU:1, one launch (start us, length us, event | category | flops | bytes accessed | tf_op | source)
XLA Modules:
  0.0 180.2 jit_solution(3725865689705729324)
XLA Ops:
  0.6 1.7 first_lists.1
  2.4 10.1 %all-to-all-start = ((f32[16,4,128]{2,1,0:T(4,128)}), f32[16,4,128]{2,1,0:T(4,128)S(1)}, u32[]{:S(2)}, u32[]{:S(2)}) async-start(f32[16,4,128]{2,1,0:T(4,128)} %first_lists.1), calls=%async_computation | async-start | bytes 65536 | tf_op jit(solution)/shard_map/all_to_all | solution.py:366
  12.5 7.5 %all-to-all-done.received = f32[16,4,128]{2,1,0:T(4,128)S(1)} async-done(((f32[16,4,128]{2,1,0:T(4,128)}), f32[16,4,128]{2,1,0:T(4,128)S(1)}, u32[]{:S(2)}, u32[]{:S(2)}) %all-to-all-start) | async-done | bytes 32800 | tf_op jit(solution)/shard_map/all_to_all | solution.py:366
  20.0 1.5 collective-permute-start
  21.5 0.8 collective-permute-done.relayed
  22.8 10.3 %local_apply.3 = (f32[64,128]{1,0:T(8,128)}, f32[16,4,128]{2,1,0:T(4,128)}) custom-call(s32[1]{0:T(128)} %bitcast.place_ref, f32[64,128]{1,0:T(8,128)} %bitcast.9, f32[16,4,128]{2,1,0:T(4,128)} %copy-done.1, f32[4,4,128]{2,1,0:T(4,128)} %copy-done.10, s32[125,128]{1,0:T(8,128)} %slots_in.5, s32[1,128]{1,0:T(1,128)} %bitcast.19, s32[5,256]{1,0:T(8,128)} %masters_in.5, ...), custom_call_target="tpu_custom_call" | custom-call | tf_op jit(solution)/shard_map/local_apply/pallas_call | solution.py:383
  33.1 12.9 %all_to_all.38.received = f32[16,4,128]{2,1,0:T(4,128)S(1)} all-to-all(f32[16,4,128]{2,1,0:T(4,128)} %get-tuple-element.15), channel_id=1, replica_groups=mesh['gx'=8,'gy_0'=4,'gy_1'=8,'gy_2'=2] {'gy_1','gy_2'}, dimensions={0} | all-to-all | bytes 65536 | tf_op jit(solution)/shard_map/all_to_all | solution.py:366
  46.0 3.0 %collective-permute-start.1 = (f32[4,4,128]{2,1,0:T(4,128)S(1)}, f32[4,4,128]{2,1,0:T(4,128)S(1)}, u32[]{:S(2)}, u32[]{:S(2)}) collective-permute-start(f32[4,4,128]{2,1,0:T(4,128)S(1)} %constant_dynamic-slice_fusion.4), channel_id=1, source_target_pairs={{0,16},{1,17},{2,18},{3,19},{16,32},{28,12},{17,33},{29,13},{18,34... | collective-permute-start | bytes 24584 | tf_op jit(solution)/shard_map/ppermute | solution.py:369
  49.0 0.8 collective-permute-done.1.relayed
  50.4 2.9 %owner_sum.3 = (f32[64,128]{1,0:T(8,128)}, f32[16,4,128]{2,1,0:T(4,128)}) custom-call(s32[1]{0:T(128)} %bitcast.place_ref, f32[64,128]{1,0:T(8,128)} %get-tuple-element.14.own, f32[16,4,128]{2,1,0:T(4,128)} %copy-done.4, f32[4,4,128]{2,1,0:T(4,128)} %copy-done.11, s32[8,512]{1,0:T(8,128)} %lists.7), custom_call_target="tpu_custom_call" | custom-call | tf_op jit(solution)/shard_map/owner_sum/pallas_call | solution.py:415
  53.3 12.0 %all_to_all.39.received = f32[16,4,128]{2,1,0:T(4,128)S(1)} all-to-all(f32[16,4,128]{2,1,0:T(4,128)} %get-tuple-element.17), channel_id=1, replica_groups=mesh['gx'=8,'gy_0'=4,'gy_1'=8,'gy_2'=2] {'gy_1','gy_2'}, dimensions={0} | all-to-all | bytes 65536 | tf_op jit(solution)/shard_map/all_to_all | solution.py:366
  65.3 3.9 %collective-permute-start.2 = (f32[4,4,128]{2,1,0:T(4,128)S(1)}, f32[4,4,128]{2,1,0:T(4,128)S(1)}, u32[]{:S(2)}, u32[]{:S(2)}) collective-permute-start(f32[4,4,128]{2,1,0:T(4,128)S(1)} %constant_dynamic-slice_fusion.3), channel_id=1, source_target_pairs={{0,16},{1,17},{2,18},{3,19},{16,32},{28,12},{17,33},{29,13},{18,34... | collective-permute-start | bytes 24584 | tf_op jit(solution)/shard_map/ppermute | solution.py:369
  69.2 0.8 collective-permute-done.2.relayed
  70.5 10.3 %local_apply.4 = (f32[64,128]{1,0:T(8,128)}, f32[16,4,128]{2,1,0:T(4,128)}) custom-call(s32[1]{0:T(128)} %bitcast.place_ref, f32[64,128]{1,0:T(8,128)} %get-tuple-element.16.vector.rest_1_.refs_1_, f32[16,4,128]{2,1,0:T(4,128)} %copy-done.3, f32[4,4,128]{2,1,0:T(4,128)} %copy-done.8, s32[125,128]{1,0:T(8,128)} %slots_in.5, s32[1,128]{1,0:T(1,128)} %bitcast.20, ...), custom_call_target="tpu_custom_call" | custom-call | tf_op jit(solution)/shard_map/local_apply/pallas_call | solution.py:383
  80.8 12.0 %all_to_all.40.received = f32[16,4,128]{2,1,0:T(4,128)S(1)} all-to-all(f32[16,4,128]{2,1,0:T(4,128)} %get-tuple-element.19), channel_id=1, replica_groups=mesh['gx'=8,'gy_0'=4,'gy_1'=8,'gy_2'=2] {'gy_1','gy_2'}, dimensions={0} | all-to-all | bytes 65536 | tf_op jit(solution)/shard_map/all_to_all | solution.py:366
  92.8 3.9 %collective-permute-start.3 = (f32[4,4,128]{2,1,0:T(4,128)S(1)}, f32[4,4,128]{2,1,0:T(4,128)S(1)}, u32[]{:S(2)}, u32[]{:S(2)}) collective-permute-start(f32[4,4,128]{2,1,0:T(4,128)S(1)} %constant_dynamic-slice_fusion.2), channel_id=1, source_target_pairs={{0,16},{1,17},{2,18},{3,19},{16,32},{28,12},{17,33},{29,13},{18,34... | collective-permute-start | bytes 24584 | tf_op jit(solution)/shard_map/ppermute | solution.py:369
  96.7 0.8 collective-permute-done.3.relayed
  98.1 2.9 %owner_sum.4 = (f32[64,128]{1,0:T(8,128)}, f32[16,4,128]{2,1,0:T(4,128)}) custom-call(s32[1]{0:T(128)} %bitcast.place_ref, f32[64,128]{1,0:T(8,128)} %get-tuple-element.18.own, f32[16,4,128]{2,1,0:T(4,128)} %copy-done.5, f32[4,4,128]{2,1,0:T(4,128)} %copy-done.12, s32[8,512]{1,0:T(8,128)} %lists.7), custom_call_target="tpu_custom_call" | custom-call | tf_op jit(solution)/shard_map/owner_sum/pallas_call | solution.py:415
  101.0 12.0 %all_to_all.41.received = f32[16,4,128]{2,1,0:T(4,128)S(1)} all-to-all(f32[16,4,128]{2,1,0:T(4,128)} %get-tuple-element.21), channel_id=1, replica_groups=mesh['gx'=8,'gy_0'=4,'gy_1'=8,'gy_2'=2] {'gy_1','gy_2'}, dimensions={0} | all-to-all | bytes 65536 | tf_op jit(solution)/shard_map/all_to_all | solution.py:366
  113.0 4.1 %collective-permute-start.4 = (f32[4,4,128]{2,1,0:T(4,128)S(1)}, f32[4,4,128]{2,1,0:T(4,128)S(1)}, u32[]{:S(2)}, u32[]{:S(2)}) collective-permute-start(f32[4,4,128]{2,1,0:T(4,128)S(1)} %constant_dynamic-slice_fusion.1), channel_id=1, source_target_pairs={{0,16},{1,17},{2,18},{3,19},{16,32},{28,12},{17,33},{29,13},{18,34... | collective-permute-start | bytes 24584 | tf_op jit(solution)/shard_map/ppermute | solution.py:369
  117.1 0.8 collective-permute-done.4.relayed
  118.5 10.4 %local_apply.5 = (f32[64,128]{1,0:T(8,128)}, f32[16,8,128]{2,1,0:T(8,128)}) custom-call(s32[1]{0:T(128)} %bitcast.place_ref, f32[64,128]{1,0:T(8,128)} %get-tuple-element.20.vector.refs_2_, f32[16,4,128]{2,1,0:T(4,128)} %copy-done.2, f32[4,4,128]{2,1,0:T(4,128)} %copy-done.7, s32[125,128]{1,0:T(8,128)} %slots_in.5, s32[1,128]{1,0:T(1,128)} %bitcast.21, ...), custom_call_target="tpu_custom_call" | custom-call | tf_op jit(solution)/shard_map/local_apply/pallas_call | solution.py:383
  128.9 12.3 %all_to_all.42.received = f32[16,8,128]{2,1,0:T(8,128)S(1)} all-to-all(f32[16,8,128]{2,1,0:T(8,128)} %get-tuple-element.22), channel_id=1, replica_groups=mesh['gx'=8,'gy_0'=4,'gy_1'=8,'gy_2'=2] {'gy_1','gy_2'}, dimensions={0} | all-to-all | bytes 131072 | tf_op jit(solution)/shard_map/all_to_all | solution.py:366
  141.3 0.6 broadcast_in_dim.2
  141.9 27.6 %all-to-all-start.6 = ((f32[32,1,128]{2,1,0:T(1,128)}), f32[32,1,128]{2,1,0:T(1,128)S(1)}, u32[]{:S(2)}, u32[]{:S(2)}) async-start(f32[32,1,128]{2,1,0:T(1,128)} %broadcast_in_dim.2), calls=%async_computation.6 | async-start | bytes 32768 | tf_op jit(solution)/shard_map/all_to_all | solution.py:412
  169.5 3.1 %collective-permute-start.5 = (f32[4,4,128]{2,1,0:T(4,128)S(1)}, f32[4,4,128]{2,1,0:T(4,128)S(1)}, u32[]{:S(2)}, u32[]{:S(2)}) collective-permute-start(f32[4,4,128]{2,1,0:T(4,128)S(1)} %constant_dynamic-slice_fusion), channel_id=1, source_target_pairs={{0,16},{1,17},{2,18},{3,19},{16,32},{28,12},{17,33},{29,13},{18,34... | collective-permute-start | bytes 24584 | tf_op jit(solution)/shard_map/ppermute | solution.py:369
  172.6 0.8 collective-permute-done.5.relayed
  173.4 0.6 copy-done.9
  174.0 2.6 %owner_sum.5.refs_3_ = f32[64,128]{1,0:T(8,128)} custom-call(s32[1]{0:T(128)} %bitcast.place_ref, f32[64,128]{1,0:T(8,128)} %get-tuple-element.23.own, f32[16,8,128]{2,1,0:T(8,128)} %copy-done, f32[4,4,128]{2,1,0:T(4,128)} %copy-done.9, s32[8,512]{1,0:T(8,128)} %lists.7), custom_call_target="tpu_custom_call" | custom-call | tf_op jit(solution)/shard_map/owner_sum/pallas_call | solution.py:415
  176.5 1.4 all-to-all-done.6
  178.0 0.6 copy-done.6
  178.6 1.6 combine.1
  (31 shorter events, 3.0 us)
Async XLA Ops:
  2.4 17.6 %all-to-all-start = ((f32[16,4,128]{2,1,0:T(4,128)}), f32[16,4,128]{2,1,0:T(4,128)S(1)}, u32[]{:S(2)}, u32[]{:S(2)}) async-start(f32[16,4,128]{2,1,0:T(4,128)} %first_lists.1), calls=%async_computation | async-start | bytes 65536 | tf_op jit(solution)/shard_map/all_to_all | solution.py:366
  20.0 2.3 %copy-start.1 = (f32[16,4,128]{2,1,0:T(4,128)}, f32[16,4,128]{2,1,0:T(4,128)S(1)}, u32[]{:S(2)}) copy-start(f32[16,4,128]{2,1,0:T(4,128)S(1)} %all-to-all-done.received) | copy-start | bytes 98308
  20.0 2.3 %collective-permute-start = (f32[4,4,128]{2,1,0:T(4,128)S(1)}, f32[4,4,128]{2,1,0:T(4,128)S(1)}, u32[]{:S(2)}, u32[]{:S(2)}) collective-permute-start(f32[4,4,128]{2,1,0:T(4,128)S(1)} %constant_dynamic-slice_fusion.5), channel_id=1, source_target_pairs={{0,16},{1,17},{2,18},{3,19},{16,32},{28,12},{17,33},{29,13},{18,34... | collective-permute-start | bytes 24584 | tf_op jit(solution)/shard_map/ppermute | solution.py:369
  22.3 0.6 copy-start.10
  46.0 3.8 %copy-start.4 = (f32[16,4,128]{2,1,0:T(4,128)}, f32[16,4,128]{2,1,0:T(4,128)S(1)}, u32[]{:S(2)}) copy-start(f32[16,4,128]{2,1,0:T(4,128)S(1)} %all_to_all.38.received) | copy-start | bytes 98308
  46.0 3.8 %collective-permute-start.1 = (f32[4,4,128]{2,1,0:T(4,128)S(1)}, f32[4,4,128]{2,1,0:T(4,128)S(1)}, u32[]{:S(2)}, u32[]{:S(2)}) collective-permute-start(f32[4,4,128]{2,1,0:T(4,128)S(1)} %constant_dynamic-slice_fusion.4), channel_id=1, source_target_pairs={{0,16},{1,17},{2,18},{3,19},{16,32},{28,12},{17,33},{29,13},{18,34... | collective-permute-start | bytes 24584 | tf_op jit(solution)/shard_map/ppermute | solution.py:369
  49.8 0.6 copy-start.11
  65.3 4.7 %copy-start.3 = (f32[16,4,128]{2,1,0:T(4,128)}, f32[16,4,128]{2,1,0:T(4,128)S(1)}, u32[]{:S(2)}) copy-start(f32[16,4,128]{2,1,0:T(4,128)S(1)} %all_to_all.39.received) | copy-start | bytes 98308
  65.3 4.7 %collective-permute-start.2 = (f32[4,4,128]{2,1,0:T(4,128)S(1)}, f32[4,4,128]{2,1,0:T(4,128)S(1)}, u32[]{:S(2)}, u32[]{:S(2)}) collective-permute-start(f32[4,4,128]{2,1,0:T(4,128)S(1)} %constant_dynamic-slice_fusion.3), channel_id=1, source_target_pairs={{0,16},{1,17},{2,18},{3,19},{16,32},{28,12},{17,33},{29,13},{18,34... | collective-permute-start | bytes 24584 | tf_op jit(solution)/shard_map/ppermute | solution.py:369
  69.9 0.6 copy-start.8
  92.8 4.7 %copy-start.5 = (f32[16,4,128]{2,1,0:T(4,128)}, f32[16,4,128]{2,1,0:T(4,128)S(1)}, u32[]{:S(2)}) copy-start(f32[16,4,128]{2,1,0:T(4,128)S(1)} %all_to_all.40.received) | copy-start | bytes 98308
  92.8 4.7 %collective-permute-start.3 = (f32[4,4,128]{2,1,0:T(4,128)S(1)}, f32[4,4,128]{2,1,0:T(4,128)S(1)}, u32[]{:S(2)}, u32[]{:S(2)}) collective-permute-start(f32[4,4,128]{2,1,0:T(4,128)S(1)} %constant_dynamic-slice_fusion.2), channel_id=1, source_target_pairs={{0,16},{1,17},{2,18},{3,19},{16,32},{28,12},{17,33},{29,13},{18,34... | collective-permute-start | bytes 24584 | tf_op jit(solution)/shard_map/ppermute | solution.py:369
  97.5 0.6 copy-start.12
  112.9 4.9 %copy-start.2 = (f32[16,4,128]{2,1,0:T(4,128)}, f32[16,4,128]{2,1,0:T(4,128)S(1)}, u32[]{:S(2)}) copy-start(f32[16,4,128]{2,1,0:T(4,128)S(1)} %all_to_all.41.received) | copy-start | bytes 98308
  113.0 4.9 %collective-permute-start.4 = (f32[4,4,128]{2,1,0:T(4,128)S(1)}, f32[4,4,128]{2,1,0:T(4,128)S(1)}, u32[]{:S(2)}, u32[]{:S(2)}) collective-permute-start(f32[4,4,128]{2,1,0:T(4,128)S(1)} %constant_dynamic-slice_fusion.1), channel_id=1, source_target_pairs={{0,16},{1,17},{2,18},{3,19},{16,32},{28,12},{17,33},{29,13},{18,34... | collective-permute-start | bytes 24584 | tf_op jit(solution)/shard_map/ppermute | solution.py:369
  117.9 0.6 copy-start.7
  141.2 32.2 %copy-start = (f32[16,8,128]{2,1,0:T(8,128)}, f32[16,8,128]{2,1,0:T(8,128)S(1)}, u32[]{:S(2)}) copy-start(f32[16,8,128]{2,1,0:T(8,128)S(1)} %all_to_all.42.received) | copy-start | bytes 196612
  141.9 36.1 %all-to-all-start.6 = ((f32[32,1,128]{2,1,0:T(1,128)}), f32[32,1,128]{2,1,0:T(1,128)S(1)}, u32[]{:S(2)}, u32[]{:S(2)}) async-start(f32[32,1,128]{2,1,0:T(1,128)} %broadcast_in_dim.2), calls=%async_computation.6 | async-start | bytes 32768 | tf_op jit(solution)/shard_map/all_to_all | solution.py:412
  169.5 3.9 %collective-permute-start.5 = (f32[4,4,128]{2,1,0:T(4,128)S(1)}, f32[4,4,128]{2,1,0:T(4,128)S(1)}, u32[]{:S(2)}, u32[]{:S(2)}) collective-permute-start(f32[4,4,128]{2,1,0:T(4,128)S(1)} %constant_dynamic-slice_fusion), channel_id=1, source_target_pairs={{0,16},{1,17},{2,18},{3,19},{16,32},{28,12},{17,33},{29,13},{18,34... | collective-permute-start | bytes 24584 | tf_op jit(solution)/shard_map/ppermute | solution.py:369
  173.4 0.6 copy-start.9
  178.0 0.6 copy-start.6

commit v2 on v1

v2 whole, which is shorter than its diff:
```python
import jax
import jax.numpy as jnp
import numpy as np
from jax import lax
from jax.experimental import pallas as pl
from jax.experimental.pallas import tpu as pltpu
from jax.sharding import Mesh
from jax.sharding import PartitionSpec as P

F32 = jnp.float32
BF16 = jnp.bfloat16
I32 = jnp.int32
AXES = ("gx", "gy_0", "gy_1", "gy_2")
GROUP = ("gy_1", "gy_2")
REST = ("gx", "gy_0")
OFFSETS = (1, 2, 3, 4, -1, -2, -3, -4)
MEMBERS = 16
PARTS = 3
OWN_ROWS = 64
LOCAL_ROWS = 96
FULL_ROWS = 98
GHOST_ROWS = 48


def lagrange(node_list, points):
    node_count = len(node_list)
    values = np.ones((len(points), node_count))
    derivs = np.zeros((len(points), node_count))
    for basis_node in range(node_count):
        for other_node in range(node_count):
            if other_node != basis_node:
                values[:, basis_node] = (
                    values[:, basis_node]
                    * (points - node_list[other_node])
                    / (node_list[basis_node] - node_list[other_node])
                )
        for skipped in range(node_count):
            if skipped != basis_node:
                product_term = np.ones(len(points)) / (node_list[basis_node] - node_list[skipped])
                for other_node in range(node_count):
                    if other_node != basis_node and other_node != skipped:
                        product_term = (
                            product_term
                            * (points - node_list[other_node])
                            / (node_list[basis_node] - node_list[other_node])
                        )
                derivs[:, basis_node] = derivs[:, basis_node] + product_term
    return (values, derivs)


def tables():
    gll_offset = np.sqrt(3.0 / 7.0)
    lobatto = np.array([0.0, (1.0 - gll_offset) / 2.0, 0.5, (1.0 + gll_offset) / 2.0, 1.0])
    inner_point = np.sqrt(5.0 - 2.0 * np.sqrt(10.0 / 7.0)) / 3.0
    outer_point = np.sqrt(5.0 + 2.0 * np.sqrt(10.0 / 7.0)) / 3.0
    inner_weight = (322.0 + 13.0 * np.sqrt(70.0)) / 900.0
    outer_weight = (322.0 - 13.0 * np.sqrt(70.0)) / 900.0
    points = np.array([-outer_point, -inner_point, 0.0, inner_point, outer_point])
    gauss_weights = np.array(
        [outer_weight, inner_weight, 128.0 / 225.0, inner_weight, outer_weight]
    )
    points = (points + 1.0) / 2.0
    gauss_weights = gauss_weights / 2.0
    shapes, slopes = lagrange(lobatto, points)
    fine_points = np.concatenate([lobatto / 2.0, (1.0 + lobatto) / 2.0])
    interp, _ = lagrange(lobatto, fine_points)
    quad_weights = np.kron(gauss_weights, np.kron(gauss_weights, gauss_weights))
    grad_x = np.kron(slopes, np.kron(shapes, shapes))
    grad_y = np.kron(shapes, np.kron(slopes, shapes))
    grad_z = np.kron(shapes, np.kron(shapes, slopes))
    stiffness = np.zeros((128, 128))
    for gradient in (grad_x, grad_y, grad_z):
        stiffness[:125, :125] += gradient.T @ (quad_weights[:, None] * gradient)
    interp_wide = np.zeros((8, 128))
    interp_wide[:5, :10] = interp.T
    return (jnp.asarray(interp_wide, F32), jnp.asarray(stiffness, F32))


def lane_pick(rows, lanes):
    return jnp.take_along_axis(rows, lanes, axis=1, mode="promise_in_bounds")


def pick(table, slots, first, last, picked=None):
    row_of = lax.shift_right_logical(slots, 7)
    lane_of = lax.bitwise_and(slots, 127)
    if picked is None:
        picked = jnp.zeros(slots.shape, F32)
    for row in range(first, last):
        spread_row = jnp.broadcast_to(table[row : row + 1, :], slots.shape)
        picked = jnp.where(row_of == row, lane_pick(spread_row, lane_of), picked)
    return picked


def split(x):
    pieces = []
    for part in range(PARTS):
        piece = x.astype(BF16)
        pieces.append(piece)
        if part + 1 < PARTS:
            x = x - piece.astype(F32)
    return pieces


def scatter(entries, first, rows):
    row_ids = lax.broadcasted_iota(I32, (rows, 128), 0).astype(F32).astype(BF16)
    lane_ids = lax.broadcasted_iota(I32, (128, 128), 0).astype(F32).astype(BF16)
    none = jnp.zeros((rows, 128), BF16)
    total = None
    for start in range(0, len(entries), 16):
        row_values = []
        lane_hots = []
        for slots, values in entries[start : start + 16]:
            row_of = (lax.shift_right_logical(slots, 7) - first).astype(F32).astype(BF16)
            lane_of = lax.bitwise_and(slots, 127).astype(F32).astype(BF16)
            row_hot = row_ids == jnp.broadcast_to(row_of, (rows, 128))
            lane_hot = lane_ids == jnp.broadcast_to(lane_of, (128, 128))
            row_values.append(
                jnp.concatenate(
                    [
                        jnp.where(row_hot, jnp.broadcast_to(piece, (rows, 128)), none)
                        for piece in split(values)
                    ],
                    axis=0,
                )
            )
            lane_hots.append(
                jnp.where(lane_hot, jnp.ones((128, 128), BF16), jnp.zeros((128, 128), BF16))
            )
        part = lax.dot_general(
            jnp.concatenate(row_values, axis=1),
            jnp.concatenate(lane_hots, axis=1),
            (((1,), (1,)), ((), ())),
            preferred_element_type=F32,
        )
        total = part if total is None else total + part
    result = total[:rows, :]
    for part in range(1, PARTS):
        result = result + total[rows * part : rows * part + rows, :]
    return result


def place_sends(place, sign, sends, pull):
    for member in range(MEMBERS):
        sends[member] = jnp.zeros(sends.shape[1:], F32)
    for block, offset in enumerate(OFFSETS):
        position = place + sign * offset
        outside = (position < 0) | (position >= MEMBERS)
        member = lax.bitwise_xor(
            lax.bitwise_and(position, MEMBERS - 1), jnp.where(outside, 1, 0)
        )
        for quarter, row in enumerate(pull(block)):
            sends[member, quarter : quarter + 1, :] = row


def arrived(place, received, relayed, offset, quarter):
    position = place + offset
    member = lax.bitwise_and(position, MEMBERS - 1)
    outside = (position < 0) | (position >= MEMBERS)
    inner = received[member, quarter : quarter + 1, :]
    outer = relayed[lax.bitwise_and(member, 3), quarter : quarter + 1, :]
    return jnp.where(outside, outer, inner)


def pick_lists(place, vector, lists, sends):
    quarters = [
        pick(vector, lists[:, 128 * quarter : 128 * quarter + 128], 0, OWN_ROWS)
        for quarter in range(4)
    ]
    place_sends(
        place, 1, sends, lambda block: [quarter[block : block + 1, :] for quarter in quarters]
    )


def first_kernel(place_ref, vector, lists, sends):
    pick_lists(place_ref[0], vector, lists, sends)


def near_kernel(vector, slots_in, masters_in, cell_part, master_part, slots, masters):
    slots[120:128, :] = jnp.zeros((8, 128), I32)
    slots[0:125, :] = slots_in[...]
    masters[...] = jnp.zeros((8, 256), I32)
    masters[0:5, :] = masters_in[...]
    for half in range(2):
        lanes = slice(128 * half, 128 * half + 128)
        master_part[:, lanes] = pick(vector, masters[:, lanes], 0, OWN_ROWS)
    for group in range(16):
        group_rows = slice(8 * group, 8 * group + 8)
        cell_part[group_rows, :] = pick(vector, slots[group_rows, :], 0, OWN_ROWS)


def con_weights(con_row, interp):
    return [
        lane_pick(
            interp[...],
            jnp.broadcast_to(con_row[:, 128 * half : 128 * half + 128], (8, 128)),
        )
        for half in range(2)
    ]


def cell_products(
    place,
    received,
    relayed,
    cell_part,
    master_part,
    slots,
    level,
    masters,
    con_row,
    interp,
    stiffness,
    table,
    cell_values,
    products,
):
    for block, offset in enumerate(OFFSETS):
        for quarter in range(4):
            row = OWN_ROWS + 4 * block + quarter
            table[row : row + 1, :] = arrived(place, received, relayed, -offset, quarter)
    for half, weight in enumerate(con_weights(con_row, interp)):
        lanes = slice(128 * half, 128 * half + 128)
        resolved = weight * pick(
            table, masters[:, lanes], OWN_ROWS, LOCAL_ROWS, master_part[:, lanes]
        )
        table[LOCAL_ROWS + half : LOCAL_ROWS + half + 1, :] = jnp.sum(
            resolved, axis=0, keepdims=True
        )
    for group in range(16):
        group_rows = slice(8 * group, 8 * group + 8)
        cell_values[group_rows, :] = pick(
            table, slots[group_rows, :], OWN_ROWS, FULL_ROWS, cell_part[group_rows, :]
        )
    products[...] = jnp.dot(
        stiffness[...],
        cell_values[...],
        precision=lax.Precision.HIGHEST,
        preferred_element_type=F32,
    ) * jnp.exp2(-level[...].astype(F32))


def cell_entries(slots, products):
    return [(slots[row : row + 1, :], products[row : row + 1, :]) for row in range(125)]


def con_entries(masters, back):
    return [
        (
            masters[node : node + 1, 128 * half : 128 * half + 128],
            back[node : node + 1, 128 * half : 128 * half + 128],
        )
        for node in range(5)
        for half in range(2)
    ]


def ghost_sums(place, slots, masters, con_row, interp, products, sends, back):
    spread = scatter(cell_entries(slots, products), OWN_ROWS, GHOST_ROWS)
    con_first = LOCAL_ROWS - OWN_ROWS
    for half, weight in enumerate(con_weights(con_row, interp)):
        sums = spread[con_first + half : con_first + half + 1, :]
        back[:, 128 * half : 128 * half + 128] = weight * jnp.broadcast_to(sums, (8, 128))
    spread = spread + scatter(con_entries(masters, back), OWN_ROWS, GHOST_ROWS)
    place_sends(
        place,
        -1,
        sends,
        lambda block: [spread[row : row + 1, :] for row in range(4 * block, 4 * block + 4)],
    )


def local_kernel(
    place_ref,
    received,
    relayed,
    cell_part,
    master_part,
    slots,
    level,
    masters,
    con_row,
    interp,
    stiffness,
    products,
    sends,
    back,
    table,
    cell_values,
):
    place = place_ref[0]
    cell_products(
        place,
        received,
        relayed,
        cell_part,
        master_part,
        slots,
        level,
        masters,
        con_row,
        interp,
        stiffness,
        table,
        cell_values,
        products,
    )
    ghost_sums(place, slots, masters, con_row, interp, products, sends, back)


def last_local_kernel(
    place_ref,
    received,
    relayed,
    cell_part,
    master_part,
    slots,
    level,
    masters,
    con_row,
    interp,
    stiffness,
    reaction,
    first,
    second,
    third,
    products,
    sends,
    back,
    table,
    cell_values,
):
    local_kernel(
        place_ref,
        received,
        relayed,
        cell_part,
        master_part,
        slots,
        level,
        masters,
        con_row,
        interp,
        stiffness,
        products,
        sends,
        back,
        table,
        cell_values,
    )
    vectors = [ref[...] for ref in (first, second, third)]
    sums = [jnp.sum(vectors[degree // 2] * vectors[(degree + 1) // 2]) for degree in range(5)]
    sums.append(
        jnp.sum(products[...] * cell_values[...])
        + jnp.sum(reaction[...] * vectors[2] * vectors[2])
    )
    lane = lax.broadcasted_iota(I32, (1, 128), 1)
    packed = jnp.zeros((1, 128), F32)
    for degree, value in enumerate(sums):
        packed = jnp.where(lane == degree, value, packed)
    for member in range(MEMBERS):
        sends[member, 4:5, :] = packed


def own_kernel(slots, masters, products, back, reaction, vector, own):
    spread = scatter(cell_entries(slots, products) + con_entries(masters, back), 0, OWN_ROWS)
    own[...] = spread + reaction[...] * vector[...]


def owner_sum(place, own, received, relayed, lists, vector):
    entries = [
        (
            lists[block : block + 1, 128 * quarter : 128 * quarter + 128],
            arrived(place, received, relayed, offset, quarter),
        )
        for block, offset in enumerate(OFFSETS)
        for quarter in range(4)
    ]
    vector[...] = own[...] + scatter(entries, 0, OWN_ROWS)


def owner_kernel(place_ref, own, received, relayed, lists, vector, sends):
    place = place_ref[0]
    owner_sum(place, own, received, relayed, lists, vector)
    pick_lists(place, vector, lists, sends)


def final_owner_kernel(place_ref, own, received, relayed, lists, vector):
    owner_sum(place_ref[0], own, received, relayed, lists, vector)


def last_kernel(moments, first, second, third, fourth, solution, residual):
    v = [ref[...] for ref in (first, second, third, fourth)]
    sums = moments[0]
    for member in range(1, moments.shape[0]):
        sums = sums + moments[member]
    lane = lax.broadcasted_iota(I32, (1, 128), 1)
    mu = [
        jnp.sum(jnp.where(lane == degree, sums, 0.0), axis=1, keepdims=True)
        for degree in range(6)
    ]
    zero = jnp.zeros((1, 1), F32)
    one = jnp.ones((1, 1), F32)

    def form(p, q, shift):
        value = zero
        for i, left in enumerate(p):
            for k, right in enumerate(q):
                value = value + left * right * mu[i + k + shift]
        return value

    res = [one]
    direction = [one]
    sol = [zero]
    rr = mu[0]
    for iteration in range(3):
        step = rr / form(direction, direction, 1)
        applied = [zero] + direction
        sol = [
            (sol[i] if i < len(sol) else zero) + step * direction[i]
            for i in range(len(direction))
        ]
        res = [
            (res[i] if i < len(res) else zero) - step * applied[i] for i in range(len(applied))
        ]
        if iteration < 2:
            rr_next = form(res, res, 0)
            ratio = rr_next / rr
            direction = [
                res[i] + (ratio * direction[i] if i < len(direction) else zero)
                for i in range(len(res))
            ]
            rr = rr_next
    solution[...] = sol[0] * v[0] + sol[1] * v[1] + sol[2] * v[2]
    residual[...] = res[0] * v[0] + res[1] * v[1] + res[2] * v[2] + res[3] * v[3]


def relay_pairs():
    pairs = []
    for group in range(32):
        for member in range(4):
            if group + 1 < 32:
                source = MEMBERS * group + member
                pairs.append((source, (source + MEMBERS) ^ 1))
            if group > 0:
                source = MEMBERS * group + 12 + member
                pairs.append((source, (source - MEMBERS) ^ 1))
    return pairs


def on_device(right_side, reaction, cell_slots, cell_level, con_masters, con_rows, send_lists):
    interp, stiffness = tables()
    place = lax.axis_index(GROUP).astype(I32)
    place_ref = place.reshape(1)
    whole = pl.BlockSpec(memory_space=pltpu.VMEM)
    scalar = pl.BlockSpec(memory_space=pltpu.SMEM)
    tile = jax.ShapeDtypeStruct((OWN_ROWS, 128), F32)
    sends = jax.ShapeDtypeStruct((MEMBERS, 4, 128), F32)
    vector = right_side.reshape(OWN_ROWS, 128)
    reaction = reaction.reshape(OWN_ROWS, 128)
    level = cell_level.reshape(1, 128)
    con_row = con_rows.reshape(1, 256)
    pairs = relay_pairs()

    def relay(received):
        first = jnp.where(place < 4, 12, 0)
        rows = lax.dynamic_slice(received, (first, 0, 0), (4, 4, 128))
        return lax.ppermute(rows, AXES, pairs)

    def kernel(body, outs, operands, scratch=()):
        return pl.pallas_call(
            body,
            out_shape=outs,
            in_specs=[scalar if operand is place_ref else whole for operand in operands],
            out_specs=jax.tree.map(lambda out: whole, outs),
            scratch_shapes=scratch,
        )(*operands)

    padded = jax.ShapeDtypeStruct((128, 128), F32)
    con_padded = jax.ShapeDtypeStruct((8, 256), F32)
    work = [pltpu.VMEM((104, 128), F32), pltpu.VMEM((128, 128), F32)]
    packed = kernel(first_kernel, sends, (place_ref, vector, send_lists))
    vectors = [vector]
    for step in range(3):
        vector = vectors[-1]
        received = lax.all_to_all(packed, GROUP, 0, 0)
        cell_part, master_part, slots, masters = kernel(
            near_kernel,
            (
                padded,
                con_padded,
                jax.ShapeDtypeStruct((128, 128), I32),
                jax.ShapeDtypeStruct((8, 256), I32),
            ),
            (vector, cell_slots, con_masters),
        )
        relayed = relay(received)
        operands = (
            place_ref,
            received,
            relayed,
            cell_part,
            master_part,
            slots,
            level,
            masters,
            con_row,
            interp,
            stiffness,
        )
        if step < 2:
            products, packed, back = kernel(
                local_kernel, (padded, sends, con_padded), operands, work
            )
        else:
            products, packed, back = kernel(
                last_local_kernel,
                (padded, jax.ShapeDtypeStruct((MEMBERS, 8, 128), F32), con_padded),
                operands + (reaction,) + tuple(vectors),
                work,
            )
        received = lax.all_to_all(packed, GROUP, 0, 0)
        own = kernel(own_kernel, tile, (slots, masters, products, back, reaction, vector))
        relayed = relay(received)
        if step < 2:
            vector, packed = kernel(
                owner_kernel, (tile, sends), (place_ref, own, received, relayed, send_lists)
            )
            vectors.append(vector)
        else:
            sums = jnp.broadcast_to(jnp.sum(received[:, 4:5, :], axis=0)[None], (32, 1, 128))
            moments = lax.all_to_all(sums, REST, 0, 0)
            vector = kernel(
                final_owner_kernel, tile, (place_ref, own, received, relayed, send_lists)
            )
            vectors.append(vector)
    solution_rows, residual_rows = kernel(last_kernel, (tile, tile), (moments, *vectors))
    return (solution_rows.reshape(-1), residual_rows.reshape(-1))


def solution(mesh):
    torus = Mesh(mesh.devices.reshape(mesh.shape["gx"], 4, 8, 2), AXES)
    placed = (
        P(AXES),
        P(AXES),
        P(None, AXES),
        P(AXES),
        P(None, AXES),
        P(AXES),
        P(None, AXES),
    )
    return jax.shard_map(
        on_device, mesh=torus, in_specs=placed, out_specs=(P(AXES), P(AXES)), check_vma=False
    )
```

time: 182 us -> 164 us (0.901)
  starting transfers between devices: 57.2 us -> 50 us
  blocking collectives: 61.1 us -> 54.6 us
  waiting for transfers between devices: 13.6 us -> 7.5 us
  Pallas kernels: 42.7 us -> 44.7 us
    all_to_all x2, starting transfers between devices: 37.7 us -> 29.1 us  [the longest x1 19 us: on_device(): moments = lax.all_to_all(sums, REST, 0, 0)]
    all_to_all x5, blocking collectives: 61.1 us -> 54.6 us  [on_device(): received = lax.all_to_all(packed, GROUP, 0, 0)]
    ppermute x6, waiting for transfers between devices: 4.65 us -> 0.02 us  [relay(): return lax.ppermute(rows, AXES, pairs)]
    pallas_call x8 -> x14, Pallas kernels: 42.7 us -> 44.7 us  [kernel(): pl.pallas_call(body, out_shape=outs, in_specs=[scalar if operand is place...]
  transfers between devices with their start and end apart: 8 -> 8, of which waited for: 8 -> 1; matrix products, arithmetic and copies ran while one was open for 0% -> 0% of each run, Pallas kernels for 1% -> 13%
where the time goes in v2:
time: 164 us; the launch traced here: 162 us
  blocking collectives  54.6 us (33%)
  starting transfers between devices  50 us (30%)
  Pallas kernels  44.7 us (27%)
  waiting for transfers between devices  7.5 us (5%)
  local copies, waits for them, and re-layouts  4.79 us (3%)
    all_to_all x5, blocking collectives, on_device(): received = lax.all_to_all(packed, GROUP, 0, 0)  54.6 us
    pallas_call x14, Pallas kernels, kernel(): pl.pallas_call(body, out_shape=outs, in_specs=[scalar if operand is place...  44.7 us
    ppermute x6, starting transfers between devices, relay(): return lax.ppermute(rows, AXES, pairs)  20.9 us
    all_to_all x1, starting transfers between devices, on_device(): moments = lax.all_to_all(sums, REST, 0, 0)  19 us
    all_to_all x1, starting transfers between devices, on_device(): received = lax.all_to_all(packed, GROUP, 0, 0)  10.1 us
    all_to_all x1, waiting for transfers between devices, on_device(): received = lax.all_to_all(packed, GROUP, 0, 0)  7.48 us
    unnamed x26, local copies, waits for them, and re-layouts  4.16 us
  transfers between devices with their start and end apart: 8, of which 1 were waited for; matrix products, arithmetic and copies ran while one was open for 0% of the time, Pallas kernels for 13%

profile of v2, /device:TPU:1, one launch (start us, length us, event | category | flops | bytes accessed | tf_op | source)
XLA Modules:
  0.0 162.4 jit_solution(16783978590770538551)
XLA Ops:
  0.6 1.7 %shard_map.105 = f32[16,4,128]{2,1,0:T(4,128)} custom-call(s32[1]{0:T(128)} %bitcast.place_ref, f32[64,128]{1,0:T(8,128)} %bitcast.7, s32[8,512]{1,0:T(8,128)} %lists.7), custom_call_target="tpu_custom_call" | custom-call | tf_op jit(solution)/shard_map/pallas_call | solution.py:470
  2.4 10.1 %all-to-all-start = ((f32[16,4,128]{2,1,0:T(4,128)}), f32[16,4,128]{2,1,0:T(4,128)S(1)}, u32[]{:S(2)}, u32[]{:S(2)}) async-start(f32[16,4,128]{2,1,0:T(4,128)} %shard_map.105), calls=%async_computation | async-start | bytes 65536 | tf_op jit(solution)/shard_map/all_to_all | solution.py:485
  12.5 7.5 %all-to-all-done.received = f32[16,4,128]{2,1,0:T(4,128)S(1)} async-done(((f32[16,4,128]{2,1,0:T(4,128)}), f32[16,4,128]{2,1,0:T(4,128)S(1)}, u32[]{:S(2)}, u32[]{:S(2)}) %all-to-all-start) | async-done | bytes 32800 | tf_op jit(solution)/shard_map/all_to_all | solution.py:485
  20.0 1.8 %collective-permute-start = (f32[4,4,128]{2,1,0:T(4,128)S(1)}, f32[4,4,128]{2,1,0:T(4,128)S(1)}, u32[]{:S(2)}, u32[]{:S(2)}) collective-permute-start(f32[4,4,128]{2,1,0:T(4,128)S(1)} %constant_dynamic-slice_fusion.5), channel_id=1, source_target_pairs={{0,17},{1,16},{2,19},{3,18},{16,33},{28,13},{17,32},{29,12},{18,35... | collective-permute-start | bytes 24584 | tf_op jit(solution)/shard_map/ppermute | solution.py:467
  21.8 2.8 %shard_map.104 = (f32[128,128]{1,0:T(8,128)}, f32[8,256]{1,0:T(8,128)}, s32[128,128]{1,0:T(8,128)}, s32[8,256]{1,0:T(8,128)}) custom-call(f32[64,128]{1,0:T(8,128)} %bitcast.8, s32[125,128]{1,0:T(8,128)} %slots_in.5, s32[5,256]{1,0:T(8,128)} %masters_in.5), custom_call_target="tpu_custom_call" | custom-call | tf_op jit(solution)/shard_map/pallas_call | solution.py:470
  25.2 5.2 %shard_map.106 = (f32[128,128]{1,0:T(8,128)}, f32[16,4,128]{2,1,0:T(4,128)}, f32[8,256]{1,0:T(8,128)}) custom-call(s32[1]{0:T(128)} %bitcast.place_ref, f32[16,4,128]{2,1,0:T(4,128)} %copy-done.4, f32[4,4,128]{2,1,0:T(4,128)} %copy-done.9, f32[128,128]{1,0:T(8,128)} %get-tuple-element.31.cell_part, f32[8,256]{1,0:T(8,128)} %get-tuple-element.32.master_part, ...), custom_call_target="tpu_custom_call" | custom-call | tf_op jit(solution)/shard_map/pallas_call | solution.py:470
  30.4 10.9 %all_to_all.35.received = f32[16,4,128]{2,1,0:T(4,128)S(1)} all-to-all(f32[16,4,128]{2,1,0:T(4,128)} %get-tuple-element.35), channel_id=1, replica_groups=mesh['gx'=8,'gy_0'=4,'gy_1'=8,'gy_2'=2] {'gy_1','gy_2'}, dimensions={0} | all-to-all | bytes 65536 | tf_op jit(solution)/shard_map/all_to_all | solution.py:521
  41.3 3.4 %collective-permute-start.1 = (f32[4,4,128]{2,1,0:T(4,128)S(1)}, f32[4,4,128]{2,1,0:T(4,128)S(1)}, u32[]{:S(2)}, u32[]{:S(2)}) collective-permute-start(f32[4,4,128]{2,1,0:T(4,128)S(1)} %constant_dynamic-slice_fusion.4), channel_id=1, source_target_pairs={{0,17},{1,16},{2,19},{3,18},{16,33},{28,13},{17,32},{29,12},{18,35... | collective-permute-start | bytes 24584 | tf_op jit(solution)/shard_map/ppermute | solution.py:467
  44.7 3.5 %shard_map.107.own = f32[64,128]{1,0:T(8,128)} custom-call(s32[128,128]{1,0:T(8,128)} %get-tuple-element.29.slots, s32[8,256]{1,0:T(8,128)} %get-tuple-element.30.masters, f32[128,128]{1,0:T(8,128)} %get-tuple-element.33.products, f32[8,256]{1,0:T(8,128)} %get-tuple-element.34.back, f32[64,128]{1,0:T(8,128)} %bitcast.12, f32[64,128]{1,0:T(8,128)} %bitcast.9), custom_call_target="tpu_custom_call" | custom-call | tf_op jit(solution)/shard_map/pallas_call | solution.py:470
  48.1 0.6 copy-done.11
  48.7 2.4 %shard_map.108 = (f32[64,128]{1,0:T(8,128)}, f32[16,4,128]{2,1,0:T(4,128)}) custom-call(s32[1]{0:T(128)} %bitcast.place_ref, f32[64,128]{1,0:T(8,128)} %shard_map.107.own, f32[16,4,128]{2,1,0:T(4,128)} %copy-done.2, f32[4,4,128]{2,1,0:T(4,128)} %copy-done.11, s32[8,512]{1,0:T(8,128)} %lists.7), custom_call_target="tpu_custom_call" | custom-call | tf_op jit(solution)/shard_map/pallas_call | solution.py:470
  51.1 10.8 %all_to_all.36.received = f32[16,4,128]{2,1,0:T(4,128)S(1)} all-to-all(f32[16,4,128]{2,1,0:T(4,128)} %get-tuple-element.39), channel_id=1, replica_groups=mesh['gx'=8,'gy_0'=4,'gy_1'=8,'gy_2'=2] {'gy_1','gy_2'}, dimensions={0} | all-to-all | bytes 65536 | tf_op jit(solution)/shard_map/all_to_all | solution.py:485
  62.0 3.1 %collective-permute-start.2 = (f32[4,4,128]{2,1,0:T(4,128)S(1)}, f32[4,4,128]{2,1,0:T(4,128)S(1)}, u32[]{:S(2)}, u32[]{:S(2)}) collective-permute-start(f32[4,4,128]{2,1,0:T(4,128)S(1)} %constant_dynamic-slice_fusion.3), channel_id=1, source_target_pairs={{0,17},{1,16},{2,19},{3,18},{16,33},{28,13},{17,32},{29,12},{18,35... | collective-permute-start | bytes 24584 | tf_op jit(solution)/shard_map/ppermute | solution.py:467
  65.0 2.8 %shard_map.109 = (f32[128,128]{1,0:T(8,128)}, f32[8,256]{1,0:T(8,128)}, s32[128,128]{1,0:T(8,128)}, s32[8,256]{1,0:T(8,128)}) custom-call(f32[64,128]{1,0:T(8,128)} %get-tuple-element.36.vector.second, s32[125,128]{1,0:T(8,128)} %slots_in.5, s32[5,256]{1,0:T(8,128)} %masters_in.5), custom_call_target="tpu_custom_call" | custom-call | tf_op jit(solution)/shard_map/pallas_call | solution.py:470
  68.5 5.2 %shard_map.110 = (f32[128,128]{1,0:T(8,128)}, f32[16,4,128]{2,1,0:T(4,128)}, f32[8,256]{1,0:T(8,128)}) custom-call(s32[1]{0:T(128)} %bitcast.place_ref, f32[16,4,128]{2,1,0:T(4,128)} %copy-done.5, f32[4,4,128]{2,1,0:T(4,128)} %copy-done.8, f32[128,128]{1,0:T(8,128)} %get-tuple-element.40.cell_part, f32[8,256]{1,0:T(8,128)} %get-tuple-element.41.master_part, ...), custom_call_target="tpu_custom_call" | custom-call | tf_op jit(solution)/shard_map/pallas_call | solution.py:470
  73.7 10.9 %all_to_all.37.received = f32[16,4,128]{2,1,0:T(4,128)S(1)} all-to-all(f32[16,4,128]{2,1,0:T(4,128)} %get-tuple-element.44), channel_id=1, replica_groups=mesh['gx'=8,'gy_0'=4,'gy_1'=8,'gy_2'=2] {'gy_1','gy_2'}, dimensions={0} | all-to-all | bytes 65536 | tf_op jit(solution)/shard_map/all_to_all | solution.py:521
  84.6 4.4 %collective-permute-start.3 = (f32[4,4,128]{2,1,0:T(4,128)S(1)}, f32[4,4,128]{2,1,0:T(4,128)S(1)}, u32[]{:S(2)}, u32[]{:S(2)}) collective-permute-start(f32[4,4,128]{2,1,0:T(4,128)S(1)} %constant_dynamic-slice_fusion.2), channel_id=1, source_target_pairs={{0,17},{1,16},{2,19},{3,18},{16,33},{28,13},{17,32},{29,12},{18,35... | collective-permute-start | bytes 24584 | tf_op jit(solution)/shard_map/ppermute | solution.py:467
  89.0 3.5 %shard_map.111.own = f32[64,128]{1,0:T(8,128)} custom-call(s32[128,128]{1,0:T(8,128)} %get-tuple-element.37.slots, s32[8,256]{1,0:T(8,128)} %get-tuple-element.38.masters, f32[128,128]{1,0:T(8,128)} %get-tuple-element.42.products, f32[8,256]{1,0:T(8,128)} %get-tuple-element.43.back, f32[64,128]{1,0:T(8,128)} %bitcast.13, ...), custom_call_target="tpu_custom_call" | custom-call | tf_op jit(solution)/shard_map/pallas_call | solution.py:470
  93.0 2.4 %shard_map.112 = (f32[64,128]{1,0:T(8,128)}, f32[16,4,128]{2,1,0:T(4,128)}) custom-call(s32[1]{0:T(128)} %bitcast.place_ref, f32[64,128]{1,0:T(8,128)} %shard_map.111.own, f32[16,4,128]{2,1,0:T(4,128)} %copy-done.3, f32[4,4,128]{2,1,0:T(4,128)} %copy-done.12, s32[8,512]{1,0:T(8,128)} %lists.7), custom_call_target="tpu_custom_call" | custom-call | tf_op jit(solution)/shard_map/pallas_call | solution.py:470
  95.4 10.8 %all_to_all.38.received = f32[16,4,128]{2,1,0:T(4,128)S(1)} all-to-all(f32[16,4,128]{2,1,0:T(4,128)} %get-tuple-element.45), channel_id=1, replica_groups=mesh['gx'=8,'gy_0'=4,'gy_1'=8,'gy_2'=2] {'gy_1','gy_2'}, dimensions={0} | all-to-all | bytes 65536 | tf_op jit(solution)/shard_map/all_to_all | solution.py:485
  106.2 4.5 %collective-permute-start.4 = (f32[4,4,128]{2,1,0:T(4,128)S(1)}, f32[4,4,128]{2,1,0:T(4,128)S(1)}, u32[]{:S(2)}, u32[]{:S(2)}) collective-permute-start(f32[4,4,128]{2,1,0:T(4,128)S(1)} %constant_dynamic-slice_fusion.1), channel_id=1, source_target_pairs={{0,17},{1,16},{2,19},{3,18},{16,33},{28,13},{17,32},{29,12},{18,35... | collective-permute-start | bytes 24584 | tf_op jit(solution)/shard_map/ppermute | solution.py:467
  110.8 2.8 %shard_map.113 = (f32[128,128]{1,0:T(8,128)}, f32[8,256]{1,0:T(8,128)}, s32[128,128]{1,0:T(8,128)}, s32[8,256]{1,0:T(8,128)}) custom-call(f32[64,128]{1,0:T(8,128)} %get-tuple-element.46.vector.third, s32[125,128]{1,0:T(8,128)} %slots_in.5, s32[5,256]{1,0:T(8,128)} %masters_in.5), custom_call_target="tpu_custom_call" | custom-call | tf_op jit(solution)/shard_map/pallas_call | solution.py:470
  113.6 0.6 copy-done.7
  114.2 5.3 %shard_map.114 = (f32[128,128]{1,0:T(8,128)}, f32[16,8,128]{2,1,0:T(8,128)}, f32[8,256]{1,0:T(8,128)}) custom-call(s32[1]{0:T(128)} %bitcast.place_ref, f32[16,4,128]{2,1,0:T(4,128)} %copy-done.1, f32[4,4,128]{2,1,0:T(4,128)} %copy-done.7, f32[128,128]{1,0:T(8,128)} %get-tuple-element.47.cell_part, f32[8,256]{1,0:T(8,128)} %get-tuple-element.48.master_part, ...), custom_call_target="tpu_custom_call" | custom-call | tf_op jit(solution)/shard_map/pallas_call | solution.py:470
  119.4 11.2 %all_to_all.39.received = f32[16,8,128]{2,1,0:T(8,128)S(1)} all-to-all(f32[16,8,128]{2,1,0:T(8,128)} %get-tuple-element.51), channel_id=1, replica_groups=mesh['gx'=8,'gy_0'=4,'gy_1'=8,'gy_2'=2] {'gy_1','gy_2'}, dimensions={0} | all-to-all | bytes 131072 | tf_op jit(solution)/shard_map/all_to_all | solution.py:521
  130.7 0.6 broadcast_in_dim.2
  131.3 19.0 %all-to-all-start.6 = ((f32[32,1,128]{2,1,0:T(1,128)}), f32[32,1,128]{2,1,0:T(1,128)S(1)}, u32[]{:S(2)}, u32[]{:S(2)}) async-start(f32[32,1,128]{2,1,0:T(1,128)} %broadcast_in_dim.2), calls=%async_computation.6 | async-start | bytes 32768 | tf_op jit(solution)/shard_map/all_to_all | solution.py:531
  150.3 3.7 %collective-permute-start.5 = (f32[4,4,128]{2,1,0:T(4,128)S(1)}, f32[4,4,128]{2,1,0:T(4,128)S(1)}, u32[]{:S(2)}, u32[]{:S(2)}) collective-permute-start(f32[4,4,128]{2,1,0:T(4,128)S(1)} %constant_dynamic-slice_fusion), channel_id=1, source_target_pairs={{0,17},{1,16},{2,19},{3,18},{16,33},{28,13},{17,32},{29,12},{18,35... | collective-permute-start | bytes 24584 | tf_op jit(solution)/shard_map/ppermute | solution.py:467
  154.1 3.5 %shard_map.115.own = f32[64,128]{1,0:T(8,128)} custom-call(s32[128,128]{1,0:T(8,128)} %get-tuple-element.49.slots, s32[8,256]{1,0:T(8,128)} %get-tuple-element.50.masters, f32[128,128]{1,0:T(8,128)} %get-tuple-element.52.products, f32[8,256]{1,0:T(8,128)} %get-tuple-element.53.back, f32[64,128]{1,0:T(8,128)} %bitcast.15, ...), custom_call_target="tpu_custom_call" | custom-call | tf_op jit(solution)/shard_map/pallas_call | solution.py:470
  158.1 2.0 %shard_map.116.fourth = f32[64,128]{1,0:T(8,128)} custom-call(s32[1]{0:T(128)} %bitcast.place_ref, f32[64,128]{1,0:T(8,128)} %shard_map.115.own, f32[16,8,128]{2,1,0:T(8,128)} %copy-done, f32[4,4,128]{2,1,0:T(4,128)} %copy-done.10, s32[8,512]{1,0:T(8,128)} %lists.7), custom_call_target="tpu_custom_call" | custom-call | tf_op jit(solution)/shard_map/pallas_call | solution.py:470
  160.2 0.6 copy-done.6
  160.8 1.6 %shard_map.117 = (f32[64,128]{1,0:T(8,128)}, f32[64,128]{1,0:T(8,128)}) custom-call(f32[32,1,128]{2,1,0:T(1,128)} %copy-done.6, f32[64,128]{1,0:T(8,128)} %bitcast.11, f32[64,128]{1,0:T(8,128)} %get-tuple-element.36.vector.second, f32[64,128]{1,0:T(8,128)} %get-tuple-element.46.vector.third, f32[64,128]{1,0:T(8,128)} %shard_map.116.fourth), custom_call_target="tpu_custom_call" | custom-call | tf_op jit(solution)/shard_map/pallas_call | solution.py:470
  (37 shorter events, 2.5 us)
Async XLA Ops:
  2.4 17.6 %all-to-all-start = ((f32[16,4,128]{2,1,0:T(4,128)}), f32[16,4,128]{2,1,0:T(4,128)S(1)}, u32[]{:S(2)}, u32[]{:S(2)}) async-start(f32[16,4,128]{2,1,0:T(4,128)} %shard_map.105), calls=%async_computation | async-start | bytes 65536 | tf_op jit(solution)/shard_map/all_to_all | solution.py:485
  20.0 4.6 %copy-start.4 = (f32[16,4,128]{2,1,0:T(4,128)}, f32[16,4,128]{2,1,0:T(4,128)S(1)}, u32[]{:S(2)}) copy-start(f32[16,4,128]{2,1,0:T(4,128)S(1)} %all-to-all-done.received) | copy-start | bytes 98308
  20.0 4.6 %collective-permute-start = (f32[4,4,128]{2,1,0:T(4,128)S(1)}, f32[4,4,128]{2,1,0:T(4,128)S(1)}, u32[]{:S(2)}, u32[]{:S(2)}) collective-permute-start(f32[4,4,128]{2,1,0:T(4,128)S(1)} %constant_dynamic-slice_fusion.5), channel_id=1, source_target_pairs={{0,17},{1,16},{2,19},{3,18},{16,33},{28,13},{17,32},{29,12},{18,35... | collective-permute-start | bytes 24584 | tf_op jit(solution)/shard_map/ppermute | solution.py:467
  24.6 0.6 copy-start.9
  41.3 6.9 %copy-start.2 = (f32[16,4,128]{2,1,0:T(4,128)}, f32[16,4,128]{2,1,0:T(4,128)S(1)}, u32[]{:S(2)}) copy-start(f32[16,4,128]{2,1,0:T(4,128)S(1)} %all_to_all.35.received) | copy-start | bytes 98308
  41.3 6.9 %collective-permute-start.1 = (f32[4,4,128]{2,1,0:T(4,128)S(1)}, f32[4,4,128]{2,1,0:T(4,128)S(1)}, u32[]{:S(2)}, u32[]{:S(2)}) collective-permute-start(f32[4,4,128]{2,1,0:T(4,128)S(1)} %constant_dynamic-slice_fusion.4), channel_id=1, source_target_pairs={{0,17},{1,16},{2,19},{3,18},{16,33},{28,13},{17,32},{29,12},{18,35... | collective-permute-start | bytes 24584 | tf_op jit(solution)/shard_map/ppermute | solution.py:467
  48.1 0.6 copy-start.11
  62.0 5.9 %copy-start.5 = (f32[16,4,128]{2,1,0:T(4,128)}, f32[16,4,128]{2,1,0:T(4,128)S(1)}, u32[]{:S(2)}) copy-start(f32[16,4,128]{2,1,0:T(4,128)S(1)} %all_to_all.36.received) | copy-start | bytes 98308
  62.0 5.9 %collective-permute-start.2 = (f32[4,4,128]{2,1,0:T(4,128)S(1)}, f32[4,4,128]{2,1,0:T(4,128)S(1)}, u32[]{:S(2)}, u32[]{:S(2)}) collective-permute-start(f32[4,4,128]{2,1,0:T(4,128)S(1)} %constant_dynamic-slice_fusion.3), channel_id=1, source_target_pairs={{0,17},{1,16},{2,19},{3,18},{16,33},{28,13},{17,32},{29,12},{18,35... | collective-permute-start | bytes 24584 | tf_op jit(solution)/shard_map/ppermute | solution.py:467
  67.9 0.6 copy-start.8
  84.6 7.8 %copy-start.3 = (f32[16,4,128]{2,1,0:T(4,128)}, f32[16,4,128]{2,1,0:T(4,128)S(1)}, u32[]{:S(2)}) copy-start(f32[16,4,128]{2,1,0:T(4,128)S(1)} %all_to_all.37.received) | copy-start | bytes 98308
  84.6 7.8 %collective-permute-start.3 = (f32[4,4,128]{2,1,0:T(4,128)S(1)}, f32[4,4,128]{2,1,0:T(4,128)S(1)}, u32[]{:S(2)}, u32[]{:S(2)}) collective-permute-start(f32[4,4,128]{2,1,0:T(4,128)S(1)} %constant_dynamic-slice_fusion.2), channel_id=1, source_target_pairs={{0,17},{1,16},{2,19},{3,18},{16,33},{28,13},{17,32},{29,12},{18,35... | collective-permute-start | bytes 24584 | tf_op jit(solution)/shard_map/ppermute | solution.py:467
  92.4 0.6 copy-start.12
  106.2 7.3 %copy-start.1 = (f32[16,4,128]{2,1,0:T(4,128)}, f32[16,4,128]{2,1,0:T(4,128)S(1)}, u32[]{:S(2)}) copy-start(f32[16,4,128]{2,1,0:T(4,128)S(1)} %all_to_all.38.received) | copy-start | bytes 98308
  106.2 7.3 %collective-permute-start.4 = (f32[4,4,128]{2,1,0:T(4,128)S(1)}, f32[4,4,128]{2,1,0:T(4,128)S(1)}, u32[]{:S(2)}, u32[]{:S(2)}) collective-permute-start(f32[4,4,128]{2,1,0:T(4,128)S(1)} %constant_dynamic-slice_fusion.1), channel_id=1, source_target_pairs={{0,17},{1,16},{2,19},{3,18},{16,33},{28,13},{17,32},{29,12},{18,35... | collective-permute-start | bytes 24584 | tf_op jit(solution)/shard_map/ppermute | solution.py:467
  113.6 0.6 copy-start.7
  130.6 26.9 %copy-start = (f32[16,8,128]{2,1,0:T(8,128)}, f32[16,8,128]{2,1,0:T(8,128)S(1)}, u32[]{:S(2)}) copy-start(f32[16,8,128]{2,1,0:T(8,128)S(1)} %all_to_all.39.received) | copy-start | bytes 196612
  131.3 28.9 %all-to-all-start.6 = ((f32[32,1,128]{2,1,0:T(1,128)}), f32[32,1,128]{2,1,0:T(1,128)S(1)}, u32[]{:S(2)}, u32[]{:S(2)}) async-start(f32[32,1,128]{2,1,0:T(1,128)} %broadcast_in_dim.2), calls=%async_computation.6 | async-start | bytes 32768 | tf_op jit(solution)/shard_map/all_to_all | solution.py:531
  150.3 7.2 %collective-permute-start.5 = (f32[4,4,128]{2,1,0:T(4,128)S(1)}, f32[4,4,128]{2,1,0:T(4,128)S(1)}, u32[]{:S(2)}, u32[]{:S(2)}) collective-permute-start(f32[4,4,128]{2,1,0:T(4,128)S(1)} %constant_dynamic-slice_fusion), channel_id=1, source_target_pairs={{0,17},{1,16},{2,19},{3,18},{16,33},{28,13},{17,32},{29,12},{18,35... | collective-permute-start | bytes 24584 | tf_op jit(solution)/shard_map/ppermute | solution.py:467
  157.5 0.6 copy-start.10
  160.2 0.6 copy-start.6

commit v3 on v2

--- a/solution.py
+++ b/solution.py
@@ -466,14 +466,22 @@
         rows = lax.dynamic_slice(received, (first, 0, 0), (4, 4, 128))
         return lax.ppermute(rows, AXES, pairs)
 
-    def kernel(body, outs, operands, scratch=()):
+    def kernel(body, outs, operands, scratch=(), outs_in_vmem=True):
+        in_vmem = [
+            operand
+            if operand is place_ref
+            else pltpu.with_memory_space_constraint(operand, pltpu.VMEM)
+            for operand in operands
+        ]
         return pl.pallas_call(
             body,
-            out_shape=outs,
+            out_shape=jax.tree.map(lambda out: pltpu.VMEM(out.shape, out.dtype), outs)
+            if outs_in_vmem
+            else outs,
             in_specs=[scalar if operand is place_ref else whole for operand in operands],
             out_specs=jax.tree.map(lambda out: whole, outs),
             scratch_shapes=scratch,
-        )(*operands)
+        )(*in_vmem)
 
     padded = jax.ShapeDtypeStruct((128, 128), F32)
     con_padded = jax.ShapeDtypeStruct((8, 256), F32)
@@ -533,7 +541,9 @@
                 final_owner_kernel, tile, (place_ref, own, received, relayed, send_lists)
             )
             vectors.append(vector)
-    solution_rows, residual_rows = kernel(last_kernel, (tile, tile), (moments, *vectors))
+    solution_rows, residual_rows = kernel(
+        last_kernel, (tile, tile), (moments, *vectors), outs_in_vmem=False
+    )
     return (solution_rows.reshape(-1), residual_rows.reshape(-1))
 
 

time: 164 us -> 147 us (0.90)
  Pallas kernels: 44.7 us -> 25 us
  starting transfers between devices: 50 us -> 56.2 us
  blocking collectives: 54.6 us -> 51.5 us
  waiting for transfers between devices: 7.5 us -> 9.71 us
  local copies, waits for them, and re-layouts: 4.79 us -> 2.79 us
    pallas_call x14, Pallas kernels: 44.7 us -> 25 us  [kernel(): pl.pallas_call(body, out_shape=jax.tree.map(lambda out: pltpu.VMEM(out.sh...]
    all_to_all x1, starting transfers between devices: 19 us -> 24.9 us  [on_device(): moments = lax.all_to_all(sums, REST, 0, 0)]
    all_to_all x5, blocking collectives: 54.6 us -> 51.5 us  [on_device(): received = lax.all_to_all(packed, GROUP, 0, 0)]
    all_to_all x1, waiting for transfers between devices: 0.01 us -> 2.24 us  [on_device(): moments = lax.all_to_all(sums, REST, 0, 0)]
    unnamed x26 -> x20, local copies, waits for them, and re-layouts: 4.16 us -> 2.15 us
  transfers between devices with their start and end apart: 8 -> 8, of which waited for: 1 -> 2; matrix products, arithmetic and copies ran while one was open for 0% -> 0% of each run, Pallas kernels for 13% -> 7%
where the time goes in v3:
time: 147 us; the launch traced here: 146 us
  starting transfers between devices  56.2 us (38%)
  blocking collectives  51.5 us (35%)
  Pallas kernels  25 us (17%)
  waiting for transfers between devices  9.71 us (7%)
  local copies, waits for them, and re-layouts  2.79 us (2%)
    all_to_all x5, blocking collectives, on_device(): received = lax.all_to_all(packed, GROUP, 0, 0)  51.5 us
    pallas_call x14, Pallas kernels, kernel(): pl.pallas_call(body, out_shape=jax.tree.map(lambda out: pltpu.VMEM(out.sh...  25 us
    all_to_all x1, starting transfers between devices, on_device(): moments = lax.all_to_all(sums, REST, 0, 0)  24.9 us
    ppermute x6, starting transfers between devices, relay(): return lax.ppermute(rows, AXES, pairs)  21.1 us
    all_to_all x1, starting transfers between devices, on_device(): received = lax.all_to_all(packed, GROUP, 0, 0)  10.1 us
    all_to_all x1, waiting for transfers between devices, on_device(): received = lax.all_to_all(packed, GROUP, 0, 0)  7.46 us
  transfers between devices with their start and end apart: 8, of which 2 were waited for; matrix products, arithmetic and copies ran while one was open for 0% of the time, Pallas kernels for 7%

profile of v3, /device:TPU:1, one launch (start us, length us, event | category | flops | bytes accessed | tf_op | source)
XLA Modules:
  0.0 146.2 jit_solution(3148987030259897417)
XLA Ops:
  0.6 0.7 copy-done.5
  1.4 0.8 copy-done
  2.1 1.0 shard_map.105
  3.1 10.1 %all-to-all-start = ((f32[16,4,128]{2,1,0:T(4,128)}), f32[16,4,128]{2,1,0:T(4,128)S(1)}, u32[]{:S(2)}, u32[]{:S(2)}) async-start(f32[16,4,128]{2,1,0:T(4,128)} %shard_map.105), calls=%async_computation | async-start | bytes 65536 | tf_op jit(solution)/shard_map/all_to_all | solution.py:493
  13.2 7.5 %all-to-all-done.received = f32[16,4,128]{2,1,0:T(4,128)S(1)} async-done(((f32[16,4,128]{2,1,0:T(4,128)}), f32[16,4,128]{2,1,0:T(4,128)S(1)}, u32[]{:S(2)}, u32[]{:S(2)}) %all-to-all-start) | async-done | bytes 32800 | tf_op jit(solution)/shard_map/all_to_all | solution.py:493
  20.7 1.8 %collective-permute-start = (f32[4,4,128]{2,1,0:T(4,128)S(1)}, f32[4,4,128]{2,1,0:T(4,128)S(1)}, u32[]{:S(2)}, u32[]{:S(2)}) collective-permute-start(f32[4,4,128]{2,1,0:T(4,128)S(1)} %constant_dynamic-slice_fusion.5), channel_id=1, source_target_pairs={{0,17},{1,16},{2,19},{3,18},{16,33},{28,13},{17,32},{29,12},{18,35... | collective-permute-start | bytes 24584 | tf_op jit(solution)/shard_map/ppermute | solution.py:467
  22.5 1.3 shard_map.104
  23.9 0.6 copy-done.7
  24.6 3.6 %shard_map.106 = (f32[128,128]{1,0:T(8,128)S(1)}, f32[16,4,128]{2,1,0:T(4,128)S(1)}, f32[8,256]{1,0:T(8,128)S(1)}) custom-call(s32[1]{0:T(128)} %bitcast.place_ref, f32[16,4,128]{2,1,0:T(4,128)S(1)} %all-to-all-done.received, f32[4,4,128]{2,1,0:T(4,128)S(1)} %collective-permute-done.relayed, f32[128,128]{1,0:T(8,128)S(1)} %get-tuple-element.31.cell_part, ...), custom_call_target="tpu_custom_call" | custom-call | tf_op jit(solution)/shard_map/pallas_call | solution.py:476
  28.2 11.2 %all_to_all.35.received = f32[16,4,128]{2,1,0:T(4,128)S(1)} all-to-all(f32[16,4,128]{2,1,0:T(4,128)S(1)} %get-tuple-element.35), channel_id=1, replica_groups=mesh['gx'=8,'gy_0'=4,'gy_1'=8,'gy_2'=2] {'gy_1','gy_2'}, dimensions={0} | all-to-all | bytes 65536 | tf_op jit(solution)/shard_map/all_to_all | solution.py:529
  39.4 2.6 %collective-permute-start.1 = (f32[4,4,128]{2,1,0:T(4,128)S(1)}, f32[4,4,128]{2,1,0:T(4,128)S(1)}, u32[]{:S(2)}, u32[]{:S(2)}) collective-permute-start(f32[4,4,128]{2,1,0:T(4,128)S(1)} %constant_dynamic-slice_fusion.4), channel_id=1, source_target_pairs={{0,17},{1,16},{2,19},{3,18},{16,33},{28,13},{17,32},{29,12},{18,35... | collective-permute-start | bytes 24584 | tf_op jit(solution)/shard_map/ppermute | solution.py:467
  42.1 1.9 %shard_map.107.own = f32[64,128]{1,0:T(8,128)S(1)} custom-call(s32[128,128]{1,0:T(8,128)S(1)} %get-tuple-element.29.slots, s32[8,256]{1,0:T(8,128)S(1)} %get-tuple-element.30.masters, f32[128,128]{1,0:T(8,128)S(1)} %get-tuple-element.33.products, f32[8,256]{1,0:T(8,128)S(1)} %get-tuple-element.34.back, f32[64,128]{1,0:T(8,128)S(1)} %bitcast.12, ...), custom_call_target="tpu_custom_call" | custom-call | tf_op jit(solution)/shard_map/pallas_call | solution.py:476
  44.0 1.0 shard_map.108
  45.0 10.0 %all_to_all.36.received = f32[16,4,128]{2,1,0:T(4,128)S(1)} all-to-all(f32[16,4,128]{2,1,0:T(4,128)S(1)} %get-tuple-element.39), channel_id=1, replica_groups=mesh['gx'=8,'gy_0'=4,'gy_1'=8,'gy_2'=2] {'gy_1','gy_2'}, dimensions={0} | all-to-all | bytes 65536 | tf_op jit(solution)/shard_map/all_to_all | solution.py:493
  55.0 3.4 %collective-permute-start.2 = (f32[4,4,128]{2,1,0:T(4,128)S(1)}, f32[4,4,128]{2,1,0:T(4,128)S(1)}, u32[]{:S(2)}, u32[]{:S(2)}) collective-permute-start(f32[4,4,128]{2,1,0:T(4,128)S(1)} %constant_dynamic-slice_fusion.3), channel_id=1, source_target_pairs={{0,17},{1,16},{2,19},{3,18},{16,33},{28,13},{17,32},{29,12},{18,35... | collective-permute-start | bytes 24584 | tf_op jit(solution)/shard_map/ppermute | solution.py:467
  58.4 1.3 shard_map.109
  59.7 3.6 %shard_map.110 = (f32[128,128]{1,0:T(8,128)S(1)}, f32[16,4,128]{2,1,0:T(4,128)S(1)}, f32[8,256]{1,0:T(8,128)S(1)}) custom-call(s32[1]{0:T(128)} %bitcast.place_ref, f32[16,4,128]{2,1,0:T(4,128)S(1)} %all_to_all.36.received, f32[4,4,128]{2,1,0:T(4,128)S(1)} %collective-permute-done.2.relayed, f32[128,128]{1,0:T(8,128)S(1)} %get-tuple-element.40.cell_part, ...), custom_call_target="tpu_custom_call" | custom-call | tf_op jit(solution)/shard_map/pallas_call | solution.py:476
  63.4 10.0 %all_to_all.37.received = f32[16,4,128]{2,1,0:T(4,128)S(1)} all-to-all(f32[16,4,128]{2,1,0:T(4,128)S(1)} %get-tuple-element.44), channel_id=1, replica_groups=mesh['gx'=8,'gy_0'=4,'gy_1'=8,'gy_2'=2] {'gy_1','gy_2'}, dimensions={0} | all-to-all | bytes 65536 | tf_op jit(solution)/shard_map/all_to_all | solution.py:529
  73.4 4.6 %collective-permute-start.3 = (f32[4,4,128]{2,1,0:T(4,128)S(1)}, f32[4,4,128]{2,1,0:T(4,128)S(1)}, u32[]{:S(2)}, u32[]{:S(2)}) collective-permute-start(f32[4,4,128]{2,1,0:T(4,128)S(1)} %constant_dynamic-slice_fusion.2), channel_id=1, source_target_pairs={{0,17},{1,16},{2,19},{3,18},{16,33},{28,13},{17,32},{29,12},{18,35... | collective-permute-start | bytes 24584 | tf_op jit(solution)/shard_map/ppermute | solution.py:467
  78.0 1.9 %shard_map.111.own = f32[64,128]{1,0:T(8,128)S(1)} custom-call(s32[128,128]{1,0:T(8,128)S(1)} %get-tuple-element.37.slots, s32[8,256]{1,0:T(8,128)S(1)} %get-tuple-element.38.masters, f32[128,128]{1,0:T(8,128)S(1)} %get-tuple-element.42.products, f32[8,256]{1,0:T(8,128)S(1)} %get-tuple-element.43.back, f32[64,128]{1,0:T(8,128)S(1)} %bitcast.13, ...), custom_call_target="tpu_custom_call" | custom-call | tf_op jit(solution)/shard_map/pallas_call | solution.py:476
  79.9 1.0 shard_map.112
  80.9 10.0 %all_to_all.38.received = f32[16,4,128]{2,1,0:T(4,128)S(1)} all-to-all(f32[16,4,128]{2,1,0:T(4,128)S(1)} %get-tuple-element.45), channel_id=1, replica_groups=mesh['gx'=8,'gy_0'=4,'gy_1'=8,'gy_2'=2] {'gy_1','gy_2'}, dimensions={0} | all-to-all | bytes 65536 | tf_op jit(solution)/shard_map/all_to_all | solution.py:493
  90.9 5.0 %collective-permute-start.4 = (f32[4,4,128]{2,1,0:T(4,128)S(1)}, f32[4,4,128]{2,1,0:T(4,128)S(1)}, u32[]{:S(2)}, u32[]{:S(2)}) collective-permute-start(f32[4,4,128]{2,1,0:T(4,128)S(1)} %constant_dynamic-slice_fusion.1), channel_id=1, source_target_pairs={{0,17},{1,16},{2,19},{3,18},{16,33},{28,13},{17,32},{29,12},{18,35... | collective-permute-start | bytes 24584 | tf_op jit(solution)/shard_map/ppermute | solution.py:467
  95.9 1.3 shard_map.113
  97.2 3.6 %shard_map.114 = (f32[128,128]{1,0:T(8,128)S(1)}, f32[16,8,128]{2,1,0:T(8,128)S(1)}, f32[8,256]{1,0:T(8,128)S(1)}) custom-call(s32[1]{0:T(128)} %bitcast.place_ref, f32[16,4,128]{2,1,0:T(4,128)S(1)} %all_to_all.38.received, f32[4,4,128]{2,1,0:T(4,128)S(1)} %collective-permute-done.4.relayed, f32[128,128]{1,0:T(8,128)S(1)} %get-tuple-element.47.cell_part, ...), custom_call_target="tpu_custom_call" | custom-call | tf_op jit(solution)/shard_map/pallas_call | solution.py:476
  100.9 10.3 %all_to_all.39.received = f32[16,8,128]{2,1,0:T(8,128)S(1)} all-to-all(f32[16,8,128]{2,1,0:T(8,128)S(1)} %get-tuple-element.51), channel_id=1, replica_groups=mesh['gx'=8,'gy_0'=4,'gy_1'=8,'gy_2'=2] {'gy_1','gy_2'}, dimensions={0} | all-to-all | bytes 131072 | tf_op jit(solution)/shard_map/all_to_all | solution.py:529
  111.3 0.6 broadcast_in_dim.2
  111.9 24.9 %all-to-all-start.6 = ((f32[32,1,128]{2,1,0:T(1,128)}), f32[32,1,128]{2,1,0:T(1,128)S(1)}, u32[]{:S(2)}, u32[]{:S(2)}) async-start(f32[32,1,128]{2,1,0:T(1,128)} %broadcast_in_dim.2), calls=%async_computation.6 | async-start | bytes 32768 | tf_op jit(solution)/shard_map/all_to_all | solution.py:539
  136.8 3.7 %collective-permute-start.5 = (f32[4,4,128]{2,1,0:T(4,128)S(1)}, f32[4,4,128]{2,1,0:T(4,128)S(1)}, u32[]{:S(2)}, u32[]{:S(2)}) collective-permute-start(f32[4,4,128]{2,1,0:T(4,128)S(1)} %constant_dynamic-slice_fusion), channel_id=1, source_target_pairs={{0,17},{1,16},{2,19},{3,18},{16,33},{28,13},{17,32},{29,12},{18,35... | collective-permute-start | bytes 24584 | tf_op jit(solution)/shard_map/ppermute | solution.py:467
  140.6 1.9 %shard_map.115.own = f32[64,128]{1,0:T(8,128)S(1)} custom-call(s32[128,128]{1,0:T(8,128)S(1)} %get-tuple-element.49.slots, s32[8,256]{1,0:T(8,128)S(1)} %get-tuple-element.50.masters, f32[128,128]{1,0:T(8,128)S(1)} %get-tuple-element.52.products, f32[8,256]{1,0:T(8,128)S(1)} %get-tuple-element.53.back, f32[64,128]{1,0:T(8,128)S(1)} %bitcast.15, ...), custom_call_target="tpu_custom_call" | custom-call | tf_op jit(solution)/shard_map/pallas_call | solution.py:476
  143.1 2.2 %all-to-all-done.6.moments = f32[32,1,128]{2,1,0:T(1,128)S(1)} async-done(((f32[32,1,128]{2,1,0:T(1,128)}), f32[32,1,128]{2,1,0:T(1,128)S(1)}, u32[]{:S(2)}, u32[]{:S(2)}) %all-to-all-start.6) | async-done | bytes 16416 | tf_op jit(solution)/shard_map/all_to_all | solution.py:539
  145.4 0.8 shard_map.117
  (31 shorter events, 0.7 us)
Async XLA Ops:
  0.6 0.7 copy-start.5
  1.3 0.8 copy-start
  2.1 20.4 %copy-start.2 = (s32[125,128]{1,0:T(8,128)S(1)}, s32[125,128]{1,0:T(8,128)}, u32[]{:S(2)}) copy-start(s32[125,128]{1,0:T(8,128)} %slots_in.5) | copy-start | bytes 192004
  3.1 17.6 %all-to-all-start = ((f32[16,4,128]{2,1,0:T(4,128)}), f32[16,4,128]{2,1,0:T(4,128)S(1)}, u32[]{:S(2)}, u32[]{:S(2)}) async-start(f32[16,4,128]{2,1,0:T(4,128)} %shard_map.105), calls=%async_computation | async-start | bytes 65536 | tf_op jit(solution)/shard_map/all_to_all | solution.py:493
  13.2 9.3 %copy-start.6 = (s32[5,256]{1,0:T(8,128)S(1)}, s32[5,256]{1,0:T(8,128)}, u32[]{:S(2)}) copy-start(s32[5,256]{1,0:T(8,128)} %masters_in.5) | copy-start | bytes 15364
  13.2 10.7 %copy-start.3 = (f32[128,128]{1,0:T(8,128)S(1)}, f32[128,128]{1,0:T(8,128)}, u32[]{:S(2)}) copy-start(f32[128,128]{1,0:T(8,128)} %constant.25.clone.stiffness) | copy-start | bytes 196612
  20.7 3.2 %collective-permute-start = (f32[4,4,128]{2,1,0:T(4,128)S(1)}, f32[4,4,128]{2,1,0:T(4,128)S(1)}, u32[]{:S(2)}, u32[]{:S(2)}) collective-permute-start(f32[4,4,128]{2,1,0:T(4,128)S(1)} %constant_dynamic-slice_fusion.5), channel_id=1, source_target_pairs={{0,17},{1,16},{2,19},{3,18},{16,33},{28,13},{17,32},{29,12},{18,35... | collective-permute-start | bytes 24584 | tf_op jit(solution)/shard_map/ppermute | solution.py:467
  23.9 0.7 copy-start.7
  23.9 0.7 copy-start.8
  23.9 0.7 copy-start.9
  28.2 13.9 %copy-start.1 = (f32[8192]{0:T(1024)S(1)}, f32[8192]{0:T(1024)}, u32[]{:S(2)}) copy-start(f32[8192]{0:T(1024)} %param.9) | copy-start | bytes 98308
  28.2 13.9 %copy-start.4 = (f32[8192]{0:T(1024)S(1)}, f32[8192]{0:T(1024)}, u32[]{:S(2)}) copy-start(f32[8192]{0:T(1024)} %param.10) | copy-start | bytes 98308
  39.4 4.6 %collective-permute-start.1 = (f32[4,4,128]{2,1,0:T(4,128)S(1)}, f32[4,4,128]{2,1,0:T(4,128)S(1)}, u32[]{:S(2)}, u32[]{:S(2)}) collective-permute-start(f32[4,4,128]{2,1,0:T(4,128)S(1)} %constant_dynamic-slice_fusion.4), channel_id=1, source_target_pairs={{0,17},{1,16},{2,19},{3,18},{16,33},{28,13},{17,32},{29,12},{18,35... | collective-permute-start | bytes 24584 | tf_op jit(solution)/shard_map/ppermute | solution.py:467
  55.0 4.8 %collective-permute-start.2 = (f32[4,4,128]{2,1,0:T(4,128)S(1)}, f32[4,4,128]{2,1,0:T(4,128)S(1)}, u32[]{:S(2)}, u32[]{:S(2)}) collective-permute-start(f32[4,4,128]{2,1,0:T(4,128)S(1)} %constant_dynamic-slice_fusion.3), channel_id=1, source_target_pairs={{0,17},{1,16},{2,19},{3,18},{16,33},{28,13},{17,32},{29,12},{18,35... | collective-permute-start | bytes 24584 | tf_op jit(solution)/shard_map/ppermute | solution.py:467
  73.4 6.5 %collective-permute-start.3 = (f32[4,4,128]{2,1,0:T(4,128)S(1)}, f32[4,4,128]{2,1,0:T(4,128)S(1)}, u32[]{:S(2)}, u32[]{:S(2)}) collective-permute-start(f32[4,4,128]{2,1,0:T(4,128)S(1)} %constant_dynamic-slice_fusion.2), channel_id=1, source_target_pairs={{0,17},{1,16},{2,19},{3,18},{16,33},{28,13},{17,32},{29,12},{18,35... | collective-permute-start | bytes 24584 | tf_op jit(solution)/shard_map/ppermute | solution.py:467
  90.9 6.3 %collective-permute-start.4 = (f32[4,4,128]{2,1,0:T(4,128)S(1)}, f32[4,4,128]{2,1,0:T(4,128)S(1)}, u32[]{:S(2)}, u32[]{:S(2)}) collective-permute-start(f32[4,4,128]{2,1,0:T(4,128)S(1)} %constant_dynamic-slice_fusion.1), channel_id=1, source_target_pairs={{0,17},{1,16},{2,19},{3,18},{16,33},{28,13},{17,32},{29,12},{18,35... | collective-permute-start | bytes 24584 | tf_op jit(solution)/shard_map/ppermute | solution.py:467
  111.9 33.5 %all-to-all-start.6 = ((f32[32,1,128]{2,1,0:T(1,128)}), f32[32,1,128]{2,1,0:T(1,128)S(1)}, u32[]{:S(2)}, u32[]{:S(2)}) async-start(f32[32,1,128]{2,1,0:T(1,128)} %broadcast_in_dim.2), calls=%async_computation.6 | async-start | bytes 32768 | tf_op jit(solution)/shard_map/all_to_all | solution.py:539
  136.8 5.7 %collective-permute-start.5 = (f32[4,4,128]{2,1,0:T(4,128)S(1)}, f32[4,4,128]{2,1,0:T(4,128)S(1)}, u32[]{:S(2)}, u32[]{:S(2)}) collective-permute-start(f32[4,4,128]{2,1,0:T(4,128)S(1)} %constant_dynamic-slice_fusion), channel_id=1, source_target_pairs={{0,17},{1,16},{2,19},{3,18},{16,33},{28,13},{17,32},{29,12},{18,35... | collective-permute-start | bytes 24584 | tf_op jit(solution)/shard_map/ppermute | solution.py:467

commit v4 on v3

--- a/solution.py
+++ b/solution.py
@@ -18,8 +18,7 @@
 PARTS = 3
 OWN_ROWS = 64
 LOCAL_ROWS = 96
-FULL_ROWS = 98
-GHOST_ROWS = 48
+GHOST_ROWS = 34
 
 
 def lagrange(node_list, points):
@@ -80,14 +79,14 @@
     return jnp.take_along_axis(rows, lanes, axis=1, mode="promise_in_bounds")
 
 
-def pick(table, slots, first, last, picked=None):
+def pick(table, slots, first, last, picked=None, base=0):
     row_of = lax.shift_right_logical(slots, 7)
     lane_of = lax.bitwise_and(slots, 127)
     if picked is None:
         picked = jnp.zeros(slots.shape, F32)
     for row in range(first, last):
         spread_row = jnp.broadcast_to(table[row : row + 1, :], slots.shape)
-        picked = jnp.where(row_of == row, lane_pick(spread_row, lane_of), picked)
+        picked = jnp.where(row_of == base + row, lane_pick(spread_row, lane_of), picked)
     return picked
 
 
@@ -101,10 +100,34 @@
     return pieces
 
 
+def stacked(pieces, rows, tall):
+    blocks = []
+    for base in range(0, tall, 16):
+        low = min(base // rows, PARTS - 1)
+        high = min((base + 15) // rows, PARTS - 1)
+        block = jnp.broadcast_to(pieces[low], (16, 128))
+        if high > low:
+            ids = lax.broadcasted_iota(I32, (16, 128), 0).astype(F32).astype(BF16)
+            block = jnp.where(
+                ids < jnp.full((16, 128), high * rows - base, BF16),
+                block,
+                jnp.broadcast_to(pieces[high], (16, 128)),
+            )
+        blocks.append(block)
+    return jnp.concatenate(blocks, axis=0)
+
+
 def scatter(entries, first, rows):
-    row_ids = lax.broadcasted_iota(I32, (rows, 128), 0).astype(F32).astype(BF16)
+    tall = -(-PARTS * rows // 16) * 16
+    row_ids = lax.broadcasted_iota(I32, (tall, 128), 0)
+    row_ids = jnp.where(
+        row_ids >= PARTS * rows,
+        -256,
+        row_ids - jnp.where(row_ids >= 2 * rows, 2 * rows, jnp.where(row_ids >= rows, rows, 0)),
+    )
+    row_ids = row_ids.astype(F32).astype(BF16)
     lane_ids = lax.broadcasted_iota(I32, (128, 128), 0).astype(F32).astype(BF16)
-    none = jnp.zeros((rows, 128), BF16)
+    none = jnp.zeros((tall, 128), BF16)
     total = None
     for start in range(0, len(entries), 16):
         row_values = []
@@ -112,17 +135,9 @@
         for slots, values in entries[start : start + 16]:
             row_of = (lax.shift_right_logical(slots, 7) - first).astype(F32).astype(BF16)
             lane_of = lax.bitwise_and(slots, 127).astype(F32).astype(BF16)
-            row_hot = row_ids == jnp.broadcast_to(row_of, (rows, 128))
+            row_hot = row_ids == jnp.broadcast_to(row_of, (tall, 128))
             lane_hot = lane_ids == jnp.broadcast_to(lane_of, (128, 128))
-            row_values.append(
-                jnp.concatenate(
-                    [
-                        jnp.where(row_hot, jnp.broadcast_to(piece, (rows, 128)), none)
-                        for piece in split(values)
-                    ],
-                    axis=0,
-                )
-            )
+            row_values.append(jnp.where(row_hot, stacked(split(values), rows, tall), none))
             lane_hots.append(
                 jnp.where(lane_hot, jnp.ones((128, 128), BF16), jnp.zeros((128, 128), BF16))
             )
@@ -171,31 +186,56 @@
     )
 
 
-def first_kernel(place_ref, vector, lists, sends):
-    pick_lists(place_ref[0], vector, lists, sends)
-
-
-def near_kernel(vector, slots_in, masters_in, cell_part, master_part, slots, masters):
+def first_kernel(
+    place_ref,
+    vector_in,
+    lists,
+    slots_in,
+    masters_in,
+    con_row,
+    level,
+    interp,
+    stiffness_in,
+    reaction_in,
+    sends,
+    vector,
+    slots,
+    masters,
+    weights,
+    scale,
+    stiffness,
+    reaction,
+):
+    vector[...] = vector_in[...]
+    pick_lists(place_ref[0], vector_in, lists, sends)
     slots[120:128, :] = jnp.zeros((8, 128), I32)
     slots[0:125, :] = slots_in[...]
     masters[...] = jnp.zeros((8, 256), I32)
     masters[0:5, :] = masters_in[...]
     for half in range(2):
         lanes = slice(128 * half, 128 * half + 128)
-        master_part[:, lanes] = pick(vector, masters[:, lanes], 0, OWN_ROWS)
+        weights[:, lanes] = lane_pick(
+            interp[...], jnp.broadcast_to(con_row[:, lanes], (8, 128))
+        )
+    scale[...] = jnp.exp2(-level[...].astype(F32))
+    stiffness[...] = stiffness_in[...]
+    reaction[...] = reaction_in[...]
+
+
+def near_kernel(place_ref, vector, received, slots, masters, cell_part, master_part, table):
+    place = place_ref[0]
+    table[0:OWN_ROWS, :] = vector[...]
+    for block, offset in enumerate(OFFSETS):
+        member = lax.bitwise_and(place - offset, MEMBERS - 1)
+        for quarter in range(4):
+            row = OWN_ROWS + 4 * block + quarter
+            table[row : row + 1, :] = received[member, quarter : quarter + 1, :]
+    for half in range(2):
+        lanes = slice(128 * half, 128 * half + 128)
+        master_part[:, lanes] = pick(table, masters[:, lanes], 0, LOCAL_ROWS)
     for group in range(16):
         group_rows = slice(8 * group, 8 * group + 8)
-        cell_part[group_rows, :] = pick(vector, slots[group_rows, :], 0, OWN_ROWS)
-
-
-def con_weights(con_row, interp):
-    return [
-        lane_pick(
-            interp[...],
-            jnp.broadcast_to(con_row[:, 128 * half : 128 * half + 128], (8, 128)),
-        )
-        for half in range(2)
-    ]
+        cell_part[group_rows, :] = pick(table, slots[group_rows, :], 0, LOCAL_ROWS)
 
 
 def cell_products(
@@ -205,38 +245,38 @@
     cell_part,
     master_part,
     slots,
-    level,
+    scale,
     masters,
-    con_row,
-    interp,
+    weights,
     stiffness,
     table,
     cell_values,
     products,
 ):
-    for block, offset in enumerate(OFFSETS):
+    forward = place < 8
+    base = jnp.where(forward, OWN_ROWS, OWN_ROWS + 16)
+    for block in range(4):
+        offset = jnp.where(forward, block + 1, -(block + 1))
         for quarter in range(4):
-            row = OWN_ROWS + 4 * block + quarter
+            row = 4 * block + quarter
             table[row : row + 1, :] = arrived(place, received, relayed, -offset, quarter)
-    for half, weight in enumerate(con_weights(con_row, interp)):
+    for half in range(2):
         lanes = slice(128 * half, 128 * half + 128)
-        resolved = weight * pick(
-            table, masters[:, lanes], OWN_ROWS, LOCAL_ROWS, master_part[:, lanes]
-        )
-        table[LOCAL_ROWS + half : LOCAL_ROWS + half + 1, :] = jnp.sum(
-            resolved, axis=0, keepdims=True
-        )
+        resolved = weights[:, lanes] * pick(
+            table, masters[:, lanes], 0, 16, master_part[:, lanes], base
+        )
+        table[16 + half : 17 + half, :] = jnp.sum(resolved, axis=0, keepdims=True)
     for group in range(16):
         group_rows = slice(8 * group, 8 * group + 8)
-        cell_values[group_rows, :] = pick(
-            table, slots[group_rows, :], OWN_ROWS, FULL_ROWS, cell_part[group_rows, :]
-        )
+        at = slots[group_rows, :]
+        values = pick(table, at, 0, 16, cell_part[group_rows, :], base)
+        cell_values[group_rows, :] = pick(table, at, 16, 18, values, LOCAL_ROWS - 16)
     products[...] = jnp.dot(
         stiffness[...],
         cell_values[...],
         precision=lax.Precision.HIGHEST,
         preferred_element_type=F32,
-    ) * jnp.exp2(-level[...].astype(F32))
+    ) * scale[...]
 
 
 def cell_entries(slots, products):
@@ -254,12 +294,13 @@
     ]
 
 
-def ghost_sums(place, slots, masters, con_row, interp, products, sends, back):
+def ghost_sums(place, slots, masters, weights, products, sends, back):
     spread = scatter(cell_entries(slots, products), OWN_ROWS, GHOST_ROWS)
     con_first = LOCAL_ROWS - OWN_ROWS
-    for half, weight in enumerate(con_weights(con_row, interp)):
+    for half in range(2):
+        lanes = slice(128 * half, 128 * half + 128)
         sums = spread[con_first + half : con_first + half + 1, :]
-        back[:, 128 * half : 128 * half + 128] = weight * jnp.broadcast_to(sums, (8, 128))
+        back[:, lanes] = weights[:, lanes] * jnp.broadcast_to(sums, (8, 128))
     spread = spread + scatter(con_entries(masters, back), OWN_ROWS, GHOST_ROWS)
     place_sends(
         place,
@@ -276,10 +317,9 @@
     cell_part,
     master_part,
     slots,
-    level,
+    scale,
     masters,
-    con_row,
-    interp,
+    weights,
     stiffness,
     products,
     sends,
@@ -295,16 +335,15 @@
         cell_part,
         master_part,
         slots,
-        level,
+        scale,
         masters,
-        con_row,
-        interp,
+        weights,
         stiffness,
         table,
         cell_values,
         products,
     )
-    ghost_sums(place, slots, masters, con_row, interp, products, sends, back)
+    ghost_sums(place, slots, masters, weights, products, sends, back)
 
 
 def last_local_kernel(
@@ -314,10 +353,9 @@
     cell_part,
     master_part,
     slots,
-    level,
+    scale,
     masters,
-    con_row,
-    interp,
+    weights,
     stiffness,
     reaction,
     first,
@@ -336,10 +374,9 @@
         cell_part,
         master_part,
         slots,
-        level,
+        scale,
         masters,
-        con_row,
-        interp,
+        weights,
         stiffness,
         products,
         sends,
@@ -361,31 +398,59 @@
         sends[member, 4:5, :] = packed
 
 
-def own_kernel(slots, masters, products, back, reaction, vector, own):
-    spread = scatter(cell_entries(slots, products) + con_entries(masters, back), 0, OWN_ROWS)
-    own[...] = spread + reaction[...] * vector[...]
-
-
-def owner_sum(place, own, received, relayed, lists, vector):
-    entries = [
-        (
-            lists[block : block + 1, 128 * quarter : 128 * quarter + 128],
-            arrived(place, received, relayed, offset, quarter),
-        )
-        for block, offset in enumerate(OFFSETS)
-        for quarter in range(4)
-    ]
+def own_kernel(
+    place_ref, slots, masters, products, back, reaction, vector, received, lists, own
+):
+    place = place_ref[0]
+    entries = cell_entries(slots, products) + con_entries(masters, back)
+    for block, offset in enumerate(OFFSETS):
+        position = place + offset
+        inside = (position >= 0) & (position < MEMBERS)
+        member = lax.bitwise_and(position, MEMBERS - 1)
+        for quarter in range(4):
+            row = received[member, quarter : quarter + 1, :]
+            entries.append(
+                (
+                    lists[block : block + 1, 128 * quarter : 128 * quarter + 128],
+                    jnp.where(inside, row, 0.0),
+                )
+            )
+    own[...] = scatter(entries, 0, OWN_ROWS) + reaction[...] * vector[...]
+
+
+def owner_sum(place, own, relayed, lists, vector):
+    entries = []
+    back = place < 8
+    for block in range(4):
+        position = jnp.where(back, place - (block + 1), place + block + 1)
+        outside = (position < 0) | (position >= MEMBERS)
+        member = lax.bitwise_and(position, 3)
+        for quarter in range(4):
+            lanes = slice(128 * quarter, 128 * quarter + 128)
+            slots = jnp.where(
+                back, lists[block + 4 : block + 5, lanes], lists[block : block + 1, lanes]
+            )
+            row = relayed[member, quarter : quarter + 1, :]
+            entries.append((slots, jnp.where(outside, row, 0.0)))
     vector[...] = own[...] + scatter(entries, 0, OWN_ROWS)
 
 
-def owner_kernel(place_ref, own, received, relayed, lists, vector, sends):
+def owner_kernel(place_ref, own, relayed, lists, vector, sends):
     place = place_ref[0]
-    owner_sum(place, own, received, relayed, lists, vector)
+    owner_sum(place, own, relayed, lists, vector)
     pick_lists(place, vector, lists, sends)
 
 
-def final_owner_kernel(place_ref, own, received, relayed, lists, vector):
-    owner_sum(place_ref[0], own, received, relayed, lists, vector)
+def final_owner_kernel(place_ref, own, relayed, lists, vector):
+    owner_sum(place_ref[0], own, relayed, lists, vector)
+
+
+def group_kernel(received, sums):
+    total = received[0, 4:5, :]
+    for member in range(1, MEMBERS):
+        total = total + received[member, 4:5, :]
+    for member in range(sums.shape[0]):
+        sums[member] = total
 
 
 def last_kernel(moments, first, second, third, fourth, solution, residual):
@@ -450,7 +515,9 @@
 def on_device(right_side, reaction, cell_slots, cell_level, con_masters, con_rows, send_lists):
     interp, stiffness = tables()
     place = lax.axis_index(GROUP).astype(I32)
-    place_ref = place.reshape(1)
+    place_ref, relay_first = lax.optimization_barrier(
+        (place.reshape(1), jnp.where(place < 4, 12, 0).astype(I32))
+    )
     whole = pl.BlockSpec(memory_space=pltpu.VMEM)
     scalar = pl.BlockSpec(memory_space=pltpu.SMEM)
     tile = jax.ShapeDtypeStruct((OWN_ROWS, 128), F32)
@@ -462,14 +529,13 @@
     pairs = relay_pairs()
 
     def relay(received):
-        first = jnp.where(place < 4, 12, 0)
-        rows = lax.dynamic_slice(received, (first, 0, 0), (4, 4, 128))
+        rows = lax.dynamic_slice(received, (relay_first, 0, 0), (4, 4, 128))
         return lax.ppermute(rows, AXES, pairs)
 
-    def kernel(body, outs, operands, scratch=(), outs_in_vmem=True):
+    def kernel(body, outs, operands, scratch=(), ins_in_vmem=True, outs_in_vmem=True):
         in_vmem = [
             operand
-            if operand is place_ref
+            if operand is place_ref or not ins_in_vmem
             else pltpu.with_memory_space_constraint(operand, pltpu.VMEM)
             for operand in operands
         ]
@@ -485,21 +551,42 @@
 
     padded = jax.ShapeDtypeStruct((128, 128), F32)
     con_padded = jax.ShapeDtypeStruct((8, 256), F32)
-    work = [pltpu.VMEM((104, 128), F32), pltpu.VMEM((128, 128), F32)]
-    packed = kernel(first_kernel, sends, (place_ref, vector, send_lists))
+    work = [pltpu.VMEM((24, 128), F32), pltpu.VMEM((128, 128), F32)]
+    packed, vector, slots, masters, weights, scale, stiffness, reaction = kernel(
+        first_kernel,
+        (
+            sends,
+            tile,
+            jax.ShapeDtypeStruct((128, 128), I32),
+            jax.ShapeDtypeStruct((8, 256), I32),
+            con_padded,
+            jax.ShapeDtypeStruct((1, 128), F32),
+            padded,
+            tile,
+        ),
+        (
+            place_ref,
+            vector,
+            send_lists,
+            cell_slots,
+            con_masters,
+            con_row,
+            level,
+            interp,
+            stiffness,
+            reaction,
+        ),
+        ins_in_vmem=False,
+    )
     vectors = [vector]
     for step in range(3):
         vector = vectors[-1]
         received = lax.all_to_all(packed, GROUP, 0, 0)
-        cell_part, master_part, slots, masters = kernel(
+        cell_part, master_part = kernel(
             near_kernel,
-            (
-                padded,
-                con_padded,
-                jax.ShapeDtypeStruct((128, 128), I32),
-                jax.ShapeDtypeStruct((8, 256), I32),
-            ),
-            (vector, cell_slots, con_masters),
+            (padded, con_padded),
+            (place_ref, vector, received, slots, masters),
+            [pltpu.VMEM((LOCAL_ROWS, 128), F32)],
         )
         relayed = relay(received)
         operands = (
@@ -509,10 +596,9 @@
             cell_part,
             master_part,
             slots,
-            level,
+            scale,
             masters,
-            con_row,
-            interp,
+            weights,
             stiffness,
         )
         if step < 2:
@@ -527,19 +613,21 @@
                 work,
             )
         received = lax.all_to_all(packed, GROUP, 0, 0)
-        own = kernel(own_kernel, tile, (slots, masters, products, back, reaction, vector))
+        own = kernel(
+            own_kernel,
+            tile,
+            (place_ref, slots, masters, products, back, reaction, vector, received, send_lists),
+        )
         relayed = relay(received)
         if step < 2:
             vector, packed = kernel(
-                owner_kernel, (tile, sends), (place_ref, own, received, relayed, send_lists)
+                owner_kernel, (tile, sends), (place_ref, own, relayed, send_lists)
             )
             vectors.append(vector)
         else:
-            sums = jnp.broadcast_to(jnp.sum(received[:, 4:5, :], axis=0)[None], (32, 1, 128))
+            sums = kernel(group_kernel, jax.ShapeDtypeStruct((32, 1, 128), F32), (received,))
             moments = lax.all_to_all(sums, REST, 0, 0)
-            vector = kernel(
-                final_owner_kernel, tile, (place_ref, own, received, relayed, send_lists)
-            )
+            vector = kernel(final_owner_kernel, tile, (place_ref, own, relayed, send_lists))
             vectors.append(vector)
     solution_rows, residual_rows = kernel(
         last_kernel, (tile, tile), (moments, *vectors), outs_in_vmem=False

time: 147 us -> 142 us (0.966)
  local copies, waits for them, and re-layouts: 2.79 us -> 0.02 us
  starting transfers between devices: 56.2 us -> 54.3 us
    unnamed x20 -> x2, local copies, waits for them, and re-layouts: 2.15 us -> 0.01 us
    all_to_all x1, starting transfers between devices: 24.9 us -> 22.9 us  [on_device(): moments = lax.all_to_all(sums, REST, 0, 0)]
    pallas_call x14 -> x15, Pallas kernels: 25 us -> 26.2 us  [kernel(): pl.pallas_call(body, out_shape=jax.tree.map(lambda out: pltpu.VMEM(out.sh...]
  transfers between devices with their start and end apart: 8 -> 8, of which waited for: 2 -> 2; matrix products, arithmetic and copies ran while one was open for 0% -> 0% of each run, Pallas kernels for 7% -> 9%
where the time goes in v4:
time: 142 us
  starting transfers between devices  54.3 us (38%)
  blocking collectives  50.9 us (36%)
  Pallas kernels  26.2 us (18%)
  waiting for transfers between devices  9.53 us (7%)
    all_to_all x5, blocking collectives, on_device(): received = lax.all_to_all(packed, GROUP, 0, 0)  50.9 us
    pallas_call x15, Pallas kernels, kernel(): pl.pallas_call(body, out_shape=jax.tree.map(lambda out: pltpu.VMEM(out.sh...  26.2 us
    all_to_all x1, starting transfers between devices, on_device(): moments = lax.all_to_all(sums, REST, 0, 0)  22.9 us
    ppermute x6, starting transfers between devices, relay(): return lax.ppermute(rows, AXES, pairs)  21.2 us
    all_to_all x1, starting transfers between devices, on_device(): received = lax.all_to_all(packed, GROUP, 0, 0)  10.1 us
    all_to_all x1, waiting for transfers between devices, on_device(): received = lax.all_to_all(packed, GROUP, 0, 0)  7.48 us
  transfers between devices with their start and end apart: 8, of which 2 were waited for; matrix products, arithmetic and copies ran while one was open for 0% of the time, Pallas kernels for 9%

profile of v4, /device:TPU:1, one launch (start us, length us, event | category | flops | bytes accessed | tf_op | source)
XLA Modules:
  0.0 141.8 jit_solution(15038531263782167537)
XLA Ops:
  0.6 1.9 %shard_map.104 = (f32[16,4,128]{2,1,0:T(4,128)}, f32[64,128]{1,0:T(8,128)S(1)}, s32[128,128]{1,0:T(8,128)S(1)}, s32[8,256]{1,0:T(8,128)S(1)}, f32[8,256]{1,0:T(8...) custom-call(s32[1]{0:T(128)} %bitcast.place_ref, f32[64,128]{1,0:T(8,128)} %bitcast.7, ...), custom_call_target="tpu_custom_call" | custom-call | tf_op jit(solution)/shard_map/pallas_call | solution.py:542
  2.6 10.1 %all-to-all-start = ((f32[16,4,128]{2,1,0:T(4,128)}), f32[16,4,128]{2,1,0:T(4,128)S(1)}, u32[]{:S(2)}, u32[]{:S(2)}) async-start(f32[16,4,128]{2,1,0:T(4,128)} %get-tuple-element.36), calls=%async_computation | async-start | bytes 65536 | tf_op jit(solution)/shard_map/all_to_all | solution.py:584
  12.7 7.5 %all-to-all-done.received = f32[16,4,128]{2,1,0:T(4,128)S(1)} async-done(((f32[16,4,128]{2,1,0:T(4,128)}), f32[16,4,128]{2,1,0:T(4,128)S(1)}, u32[]{:S(2)}, u32[]{:S(2)}) %all-to-all-start) | async-done | bytes 32800 | tf_op jit(solution)/shard_map/all_to_all | solution.py:584
  20.2 1.8 %collective-permute-start = (f32[4,4,128]{2,1,0:T(4,128)S(1)}, f32[4,4,128]{2,1,0:T(4,128)S(1)}, u32[]{:S(2)}, u32[]{:S(2)}) collective-permute-start(f32[4,4,128]{2,1,0:T(4,128)S(1)} %constant_dynamic-slice_fusion.5), channel_id=1, source_target_pairs={{0,17},{1,16},{2,19},{3,18},{16,33},{28,13},{17,32},{29,12},{18,35... | collective-permute-start | bytes 24584 | tf_op jit(solution)/shard_map/ppermute | solution.py:533
  22.0 1.9 %shard_map.105 = (f32[128,128]{1,0:T(8,128)S(1)}, f32[8,256]{1,0:T(8,128)S(1)}) custom-call(s32[1]{0:T(128)} %bitcast.place_ref, f32[64,128]{1,0:T(8,128)S(1)} %get-tuple-element.38.vector.first, f32[16,4,128]{2,1,0:T(4,128)S(1)} %all-to-all-done.received, s32[128,128]{1,0:T(8,128)S(1)} %get-tuple-element.34.slots, s32[8,256]{1,0:T(8,128)S(1)} %get-tuple-element.35.masters), custom_call_target="tpu_custom_call" | custom-call | tf_op jit(solution)/shard_map/pallas_call | solution.py:542
  23.9 2.7 %shard_map.106 = (f32[128,128]{1,0:T(8,128)S(1)}, f32[16,4,128]{2,1,0:T(4,128)S(1)}, f32[8,256]{1,0:T(8,128)S(1)}) custom-call(s32[1]{0:T(128)} %bitcast.place_ref, f32[16,4,128]{2,1,0:T(4,128)S(1)} %all-to-all-done.received, f32[4,4,128]{2,1,0:T(4,128)S(1)} %collective-permute-done.relayed, f32[128,128]{1,0:T(8,128)S(1)} %get-tuple-element.39.cell_part, ...), custom_call_target="tpu_custom_call" | custom-call | tf_op jit(solution)/shard_map/pallas_call | solution.py:542
  26.6 10.6 %all_to_all.35.received = f32[16,4,128]{2,1,0:T(4,128)S(1)} all-to-all(f32[16,4,128]{2,1,0:T(4,128)S(1)} %get-tuple-element.47), channel_id=1, replica_groups=mesh['gx'=8,'gy_0'=4,'gy_1'=8,'gy_2'=2] {'gy_1','gy_2'}, dimensions={0} | all-to-all | bytes 65536 | tf_op jit(solution)/shard_map/all_to_all | solution.py:615
  37.2 2.9 %collective-permute-start.1 = (f32[4,4,128]{2,1,0:T(4,128)S(1)}, f32[4,4,128]{2,1,0:T(4,128)S(1)}, u32[]{:S(2)}, u32[]{:S(2)}) collective-permute-start(f32[4,4,128]{2,1,0:T(4,128)S(1)} %constant_dynamic-slice_fusion.4), channel_id=1, source_target_pairs={{0,17},{1,16},{2,19},{3,18},{16,33},{28,13},{17,32},{29,12},{18,35... | collective-permute-start | bytes 24584 | tf_op jit(solution)/shard_map/ppermute | solution.py:533
  40.1 2.3 %shard_map.107.own = f32[64,128]{1,0:T(8,128)S(1)} custom-call(s32[1]{0:T(128)} %bitcast.place_ref, s32[128,128]{1,0:T(8,128)S(1)} %get-tuple-element.34.slots, s32[8,256]{1,0:T(8,128)S(1)} %get-tuple-element.35.masters, f32[128,128]{1,0:T(8,128)S(1)} %get-tuple-element.44.products, f32[8,256]{1,0:T(8,128)S(1)} %get-tuple-element.45.back, ...), custom_call_target="tpu_custom_call" | custom-call | tf_op jit(solution)/shard_map/pallas_call | solution.py:542
  42.5 0.8 shard_map.108
  43.3 10.0 %all_to_all.36.received = f32[16,4,128]{2,1,0:T(4,128)S(1)} all-to-all(f32[16,4,128]{2,1,0:T(4,128)S(1)} %get-tuple-element.48), channel_id=1, replica_groups=mesh['gx'=8,'gy_0'=4,'gy_1'=8,'gy_2'=2] {'gy_1','gy_2'}, dimensions={0} | all-to-all | bytes 65536 | tf_op jit(solution)/shard_map/all_to_all | solution.py:584
  53.3 3.3 %collective-permute-start.2 = (f32[4,4,128]{2,1,0:T(4,128)S(1)}, f32[4,4,128]{2,1,0:T(4,128)S(1)}, u32[]{:S(2)}, u32[]{:S(2)}) collective-permute-start(f32[4,4,128]{2,1,0:T(4,128)S(1)} %constant_dynamic-slice_fusion.3), channel_id=1, source_target_pairs={{0,17},{1,16},{2,19},{3,18},{16,33},{28,13},{17,32},{29,12},{18,35... | collective-permute-start | bytes 24584 | tf_op jit(solution)/shard_map/ppermute | solution.py:533
  56.5 1.9 %shard_map.109 = (f32[128,128]{1,0:T(8,128)S(1)}, f32[8,256]{1,0:T(8,128)S(1)}) custom-call(s32[1]{0:T(128)} %bitcast.place_ref, f32[64,128]{1,0:T(8,128)S(1)} %get-tuple-element.49.vector.second, f32[16,4,128]{2,1,0:T(4,128)S(1)} %all_to_all.36.received, s32[128,128]{1,0:T(8,128)S(1)} %get-tuple-element.34.slots, s32[8,256]{1,0:T(8,128)S(1)} %get-tuple-element.35.masters), custom_call_target="tpu_custom_call" | custom-call | tf_op jit(solution)/shard_map/pallas_call | solution.py:542
  58.5 0.0 collective-permute-done.2.relayed
  58.5 2.7 %shard_map.110 = (f32[128,128]{1,0:T(8,128)S(1)}, f32[16,4,128]{2,1,0:T(4,128)S(1)}, f32[8,256]{1,0:T(8,128)S(1)}) custom-call(s32[1]{0:T(128)} %bitcast.place_ref, f32[16,4,128]{2,1,0:T(4,128)S(1)} %all_to_all.36.received, f32[4,4,128]{2,1,0:T(4,128)S(1)} %collective-permute-done.2.relayed, f32[128,128]{1,0:T(8,128)S(1)} %get-tuple-element.50.cell_part, ...), custom_call_target="tpu_custom_call" | custom-call | tf_op jit(solution)/shard_map/pallas_call | solution.py:542
  61.2 10.0 %all_to_all.37.received = f32[16,4,128]{2,1,0:T(4,128)S(1)} all-to-all(f32[16,4,128]{2,1,0:T(4,128)S(1)} %get-tuple-element.54), channel_id=1, replica_groups=mesh['gx'=8,'gy_0'=4,'gy_1'=8,'gy_2'=2] {'gy_1','gy_2'}, dimensions={0} | all-to-all | bytes 65536 | tf_op jit(solution)/shard_map/all_to_all | solution.py:615
  71.2 4.6 %collective-permute-start.3 = (f32[4,4,128]{2,1,0:T(4,128)S(1)}, f32[4,4,128]{2,1,0:T(4,128)S(1)}, u32[]{:S(2)}, u32[]{:S(2)}) collective-permute-start(f32[4,4,128]{2,1,0:T(4,128)S(1)} %constant_dynamic-slice_fusion.2), channel_id=1, source_target_pairs={{0,17},{1,16},{2,19},{3,18},{16,33},{28,13},{17,32},{29,12},{18,35... | collective-permute-start | bytes 24584 | tf_op jit(solution)/shard_map/ppermute | solution.py:533
  75.8 2.3 %shard_map.111.own = f32[64,128]{1,0:T(8,128)S(1)} custom-call(s32[1]{0:T(128)} %bitcast.place_ref, s32[128,128]{1,0:T(8,128)S(1)} %get-tuple-element.34.slots, s32[8,256]{1,0:T(8,128)S(1)} %get-tuple-element.35.masters, f32[128,128]{1,0:T(8,128)S(1)} %get-tuple-element.52.products, f32[8,256]{1,0:T(8,128)S(1)} %get-tuple-element.53.back, ...), custom_call_target="tpu_custom_call" | custom-call | tf_op jit(solution)/shard_map/pallas_call | solution.py:542
  78.1 0.0 collective-permute-done.3.relayed
  78.1 0.8 shard_map.112
  78.9 10.0 %all_to_all.38.received = f32[16,4,128]{2,1,0:T(4,128)S(1)} all-to-all(f32[16,4,128]{2,1,0:T(4,128)S(1)} %get-tuple-element.55), channel_id=1, replica_groups=mesh['gx'=8,'gy_0'=4,'gy_1'=8,'gy_2'=2] {'gy_1','gy_2'}, dimensions={0} | all-to-all | bytes 65536 | tf_op jit(solution)/shard_map/all_to_all | solution.py:584
  88.9 5.0 %collective-permute-start.4 = (f32[4,4,128]{2,1,0:T(4,128)S(1)}, f32[4,4,128]{2,1,0:T(4,128)S(1)}, u32[]{:S(2)}, u32[]{:S(2)}) collective-permute-start(f32[4,4,128]{2,1,0:T(4,128)S(1)} %constant_dynamic-slice_fusion.1), channel_id=1, source_target_pairs={{0,17},{1,16},{2,19},{3,18},{16,33},{28,13},{17,32},{29,12},{18,35... | collective-permute-start | bytes 24584 | tf_op jit(solution)/shard_map/ppermute | solution.py:533
  93.9 1.9 %shard_map.113 = (f32[128,128]{1,0:T(8,128)S(1)}, f32[8,256]{1,0:T(8,128)S(1)}) custom-call(s32[1]{0:T(128)} %bitcast.place_ref, f32[64,128]{1,0:T(8,128)S(1)} %get-tuple-element.56.vector.third, f32[16,4,128]{2,1,0:T(4,128)S(1)} %all_to_all.38.received, s32[128,128]{1,0:T(8,128)S(1)} %get-tuple-element.34.slots, s32[8,256]{1,0:T(8,128)S(1)} %get-tuple-element.35.masters), custom_call_target="tpu_custom_call" | custom-call | tf_op jit(solution)/shard_map/pallas_call | solution.py:542
  95.8 2.7 %shard_map.114 = (f32[128,128]{1,0:T(8,128)S(1)}, f32[16,8,128]{2,1,0:T(8,128)S(1)}, f32[8,256]{1,0:T(8,128)S(1)}) custom-call(s32[1]{0:T(128)} %bitcast.place_ref, f32[16,4,128]{2,1,0:T(4,128)S(1)} %all_to_all.38.received, f32[4,4,128]{2,1,0:T(4,128)S(1)} %collective-permute-done.4.relayed, f32[128,128]{1,0:T(8,128)S(1)} %get-tuple-element.57.cell_part, ...), custom_call_target="tpu_custom_call" | custom-call | tf_op jit(solution)/shard_map/pallas_call | solution.py:542
  98.5 10.3 %all_to_all.39.received = f32[16,8,128]{2,1,0:T(8,128)S(1)} all-to-all(f32[16,8,128]{2,1,0:T(8,128)S(1)} %get-tuple-element.59), channel_id=1, replica_groups=mesh['gx'=8,'gy_0'=4,'gy_1'=8,'gy_2'=2] {'gy_1','gy_2'}, dimensions={0} | all-to-all | bytes 131072 | tf_op jit(solution)/shard_map/all_to_all | solution.py:615
  108.9 0.6 shard_map.115
  109.5 22.9 %all-to-all-start.6 = ((f32[32,1,128]{2,1,0:T(1,128)}), f32[32,1,128]{2,1,0:T(1,128)S(1)}, u32[]{:S(2)}, u32[]{:S(2)}) async-start(f32[32,1,128]{2,1,0:T(1,128)} %shard_map.115), calls=%async_computation.6 | async-start | bytes 32768 | tf_op jit(solution)/shard_map/all_to_all | solution.py:629
  132.4 3.7 %collective-permute-start.5 = (f32[4,4,128]{2,1,0:T(4,128)S(1)}, f32[4,4,128]{2,1,0:T(4,128)S(1)}, u32[]{:S(2)}, u32[]{:S(2)}) collective-permute-start(f32[4,4,128]{2,1,0:T(4,128)S(1)} %constant_dynamic-slice_fusion), channel_id=1, source_target_pairs={{0,17},{1,16},{2,19},{3,18},{16,33},{28,13},{17,32},{29,12},{18,35... | collective-permute-start | bytes 24584 | tf_op jit(solution)/shard_map/ppermute | solution.py:533
  136.2 2.3 %shard_map.116.own = f32[64,128]{1,0:T(8,128)S(1)} custom-call(s32[1]{0:T(128)} %bitcast.place_ref, s32[128,128]{1,0:T(8,128)S(1)} %get-tuple-element.34.slots, s32[8,256]{1,0:T(8,128)S(1)} %get-tuple-element.35.masters, f32[128,128]{1,0:T(8,128)S(1)} %get-tuple-element.60.products, f32[8,256]{1,0:T(8,128)S(1)} %get-tuple-element.61.back, ...), custom_call_target="tpu_custom_call" | custom-call | tf_op jit(solution)/shard_map/pallas_call | solution.py:542
  138.5 0.4 shard_map.117.fourth
  138.9 2.0 %all-to-all-done.6.moments = f32[32,1,128]{2,1,0:T(1,128)S(1)} async-done(((f32[32,1,128]{2,1,0:T(1,128)}), f32[32,1,128]{2,1,0:T(1,128)S(1)}, u32[]{:S(2)}, u32[]{:S(2)}) %all-to-all-start.6) | async-done | bytes 16416 | tf_op jit(solution)/shard_map/all_to_all | solution.py:629
  141.0 0.8 shard_map.118
  (12 shorter events, 0.0 us)
Async XLA Ops:
  2.6 17.6 %all-to-all-start = ((f32[16,4,128]{2,1,0:T(4,128)}), f32[16,4,128]{2,1,0:T(4,128)S(1)}, u32[]{:S(2)}, u32[]{:S(2)}) async-start(f32[16,4,128]{2,1,0:T(4,128)} %get-tuple-element.36), calls=%async_computation | async-start | bytes 65536 | tf_op jit(solution)/shard_map/all_to_all | solution.py:584
  20.2 3.7 %collective-permute-start = (f32[4,4,128]{2,1,0:T(4,128)S(1)}, f32[4,4,128]{2,1,0:T(4,128)S(1)}, u32[]{:S(2)}, u32[]{:S(2)}) collective-permute-start(f32[4,4,128]{2,1,0:T(4,128)S(1)} %constant_dynamic-slice_fusion.5), channel_id=1, source_target_pairs={{0,17},{1,16},{2,19},{3,18},{16,33},{28,13},{17,32},{29,12},{18,35... | collective-permute-start | bytes 24584 | tf_op jit(solution)/shard_map/ppermute | solution.py:533
  37.2 2.9 %copy-start = (s32[8,512]{1,0:T(8,128)S(1)}, s32[8,512]{1,0:T(8,128)}, u32[]{:S(2)}) copy-start(s32[8,512]{1,0:T(8,128)} %lists.13) | copy-start | bytes 49156
  37.2 5.2 %collective-permute-start.1 = (f32[4,4,128]{2,1,0:T(4,128)S(1)}, f32[4,4,128]{2,1,0:T(4,128)S(1)}, u32[]{:S(2)}, u32[]{:S(2)}) collective-permute-start(f32[4,4,128]{2,1,0:T(4,128)S(1)} %constant_dynamic-slice_fusion.4), channel_id=1, source_target_pairs={{0,17},{1,16},{2,19},{3,18},{16,33},{28,13},{17,32},{29,12},{18,35... | collective-permute-start | bytes 24584 | tf_op jit(solution)/shard_map/ppermute | solution.py:533
  53.3 5.2 %collective-permute-start.2 = (f32[4,4,128]{2,1,0:T(4,128)S(1)}, f32[4,4,128]{2,1,0:T(4,128)S(1)}, u32[]{:S(2)}, u32[]{:S(2)}) collective-permute-start(f32[4,4,128]{2,1,0:T(4,128)S(1)} %constant_dynamic-slice_fusion.3), channel_id=1, source_target_pairs={{0,17},{1,16},{2,19},{3,18},{16,33},{28,13},{17,32},{29,12},{18,35... | collective-permute-start | bytes 24584 | tf_op jit(solution)/shard_map/ppermute | solution.py:533
  71.2 6.9 %collective-permute-start.3 = (f32[4,4,128]{2,1,0:T(4,128)S(1)}, f32[4,4,128]{2,1,0:T(4,128)S(1)}, u32[]{:S(2)}, u32[]{:S(2)}) collective-permute-start(f32[4,4,128]{2,1,0:T(4,128)S(1)} %constant_dynamic-slice_fusion.2), channel_id=1, source_target_pairs={{0,17},{1,16},{2,19},{3,18},{16,33},{28,13},{17,32},{29,12},{18,35... | collective-permute-start | bytes 24584 | tf_op jit(solution)/shard_map/ppermute | solution.py:533
  88.9 6.9 %collective-permute-start.4 = (f32[4,4,128]{2,1,0:T(4,128)S(1)}, f32[4,4,128]{2,1,0:T(4,128)S(1)}, u32[]{:S(2)}, u32[]{:S(2)}) collective-permute-start(f32[4,4,128]{2,1,0:T(4,128)S(1)} %constant_dynamic-slice_fusion.1), channel_id=1, source_target_pairs={{0,17},{1,16},{2,19},{3,18},{16,33},{28,13},{17,32},{29,12},{18,35... | collective-permute-start | bytes 24584 | tf_op jit(solution)/shard_map/ppermute | solution.py:533
  109.5 31.5 %all-to-all-start.6 = ((f32[32,1,128]{2,1,0:T(1,128)}), f32[32,1,128]{2,1,0:T(1,128)S(1)}, u32[]{:S(2)}, u32[]{:S(2)}) async-start(f32[32,1,128]{2,1,0:T(1,128)} %shard_map.115), calls=%async_computation.6 | async-start | bytes 32768 | tf_op jit(solution)/shard_map/all_to_all | solution.py:629
  132.4 6.1 %collective-permute-start.5 = (f32[4,4,128]{2,1,0:T(4,128)S(1)}, f32[4,4,128]{2,1,0:T(4,128)S(1)}, u32[]{:S(2)}, u32[]{:S(2)}) collective-permute-start(f32[4,4,128]{2,1,0:T(4,128)S(1)} %constant_dynamic-slice_fusion), channel_id=1, source_target_pairs={{0,17},{1,16},{2,19},{3,18},{16,33},{28,13},{17,32},{29,12},{18,35... | collective-permute-start | bytes 24584 | tf_op jit(solution)/shard_map/ppermute | solution.py:533

commit v5 on v4

--- a/solution.py
+++ b/solution.py
@@ -516,7 +516,7 @@
     interp, stiffness = tables()
     place = lax.axis_index(GROUP).astype(I32)
     place_ref, relay_first = lax.optimization_barrier(
-        (place.reshape(1), jnp.where(place < 4, 12, 0).astype(I32))
+        (place.reshape(1), jnp.where(place < 4, 12, 0).astype(jnp.uint32))
     )
     whole = pl.BlockSpec(memory_space=pltpu.VMEM)
     scalar = pl.BlockSpec(memory_space=pltpu.SMEM)
@@ -529,7 +529,9 @@
     pairs = relay_pairs()
 
     def relay(received):
-        rows = lax.dynamic_slice(received, (relay_first, 0, 0), (4, 4, 128))
+        rows = lax.dynamic_slice(
+            received, (relay_first, np.uint32(0), np.uint32(0)), (4, 4, 128)
+        )
         return lax.ppermute(rows, AXES, pairs)
 
     def kernel(body, outs, operands, scratch=(), ins_in_vmem=True, outs_in_vmem=True):

time: 142 us -> 142 us (level)
  blocking collectives: 50.9 us -> 66.9 us
  starting transfers between devices: 54.3 us -> 45.5 us
  waiting for transfers between devices: 9.53 us -> 2.05 us
    all_to_all x5 -> x6, blocking collectives: 50.9 us -> 66.9 us  [on_device(): received = lax.all_to_all(packed, GROUP, 0, 0)]
    all_to_all x1 -> x0, starting transfers between devices: 10.1 us -> none  [on_device(): received = lax.all_to_all(packed, GROUP, 0, 0)]
    all_to_all x1 -> x0, waiting for transfers between devices: 7.48 us -> none  [on_device(): received = lax.all_to_all(packed, GROUP, 0, 0)]
  transfers between devices with their start and end apart: 8 -> 7, of which waited for: 2 -> 1; matrix products, arithmetic and copies ran while one was open for 0% -> 0% of each run, Pallas kernels for 9% -> 9%
where the time goes in v5:
time: 142 us; the launch traced here: 141 us
  blocking collectives  66.9 us (47%)
  starting transfers between devices  45.5 us (32%)
  Pallas kernels  25.6 us (18%)
  waiting for transfers between devices  2.05 us (1%)
    all_to_all x6, blocking collectives, on_device(): received = lax.all_to_all(packed, GROUP, 0, 0)  66.9 us
    pallas_call x15, Pallas kernels, kernel(): pl.pallas_call(body, out_shape=jax.tree.map(lambda out: pltpu.VMEM(out.sh...  25.6 us
    all_to_all x1, starting transfers between devices, on_device(): moments = lax.all_to_all(sums, REST, 0, 0)  22.9 us
    ppermute x6, starting transfers between devices, relay(): return lax.ppermute(rows, AXES, pairs)  22.6 us
  transfers between devices with their start and end apart: 7, of which 1 were waited for; matrix products, arithmetic and copies ran while one was open for 0% of the time, Pallas kernels for 9%

profile of v5, /device:TPU:1, one launch (start us, length us, event | category | flops | bytes accessed | tf_op | source)
XLA Modules:
  0.0 141.0 jit_solution(13206683212743256253)
XLA Ops:
  0.6 1.3 shard_map.104
  2.0 16.7 %all_to_all.35.received = f32[16,4,128]{2,1,0:T(4,128)S(1)} all-to-all(f32[16,4,128]{2,1,0:T(4,128)S(1)} %get-tuple-element.36), channel_id=1, replica_groups=mesh['gx'=8,'gy_0'=4,'gy_1'=8,'gy_2'=2] {'gy_1','gy_2'}, dimensions={0} | all-to-all | bytes 65536 | tf_op jit(solution)/shard_map/all_to_all | solution.py:586
  18.7 2.5 %collective-permute-start = (f32[4,4,128]{2,1,0:T(4,128)S(1)}, f32[4,4,128]{2,1,0:T(4,128)S(1)}, u32[]{:S(2)}, u32[]{:S(2)}) collective-permute-start(f32[4,4,128]{2,1,0:T(4,128)S(1)} %constant_dynamic-slice_fusion.5), channel_id=1, source_target_pairs={{0,17},{1,16},{2,19},{3,18},{16,33},{28,13},{17,32},{29,12},{18,35... | collective-permute-start | bytes 24584 | tf_op jit(solution)/shard_map/ppermute | solution.py:535
  21.1 1.9 %shard_map.105 = (f32[128,128]{1,0:T(8,128)S(1)}, f32[8,256]{1,0:T(8,128)S(1)}) custom-call(s32[1]{0:T(128)} %bitcast.place_ref, f32[64,128]{1,0:T(8,128)S(1)} %get-tuple-element.38.vector.first, f32[16,4,128]{2,1,0:T(4,128)S(1)} %all_to_all.35.received, s32[128,128]{1,0:T(8,128)S(1)} %get-tuple-element.34.slots, s32[8,256]{1,0:T(8,128)S(1)} %get-tuple-element.35.masters), custom_call_target="tpu_custom_call" | custom-call | tf_op jit(solution)/shard_map/pallas_call | solution.py:544
  23.1 0.0 collective-permute-done.relayed
  23.1 2.7 %shard_map.106 = (f32[128,128]{1,0:T(8,128)S(1)}, f32[16,4,128]{2,1,0:T(4,128)S(1)}, f32[8,256]{1,0:T(8,128)S(1)}) custom-call(s32[1]{0:T(128)} %bitcast.place_ref, f32[16,4,128]{2,1,0:T(4,128)S(1)} %all_to_all.35.received, f32[4,4,128]{2,1,0:T(4,128)S(1)} %collective-permute-done.relayed, f32[128,128]{1,0:T(8,128)S(1)} %get-tuple-element.39.cell_part, ...), custom_call_target="tpu_custom_call" | custom-call | tf_op jit(solution)/shard_map/pallas_call | solution.py:544
  25.8 9.9 %all_to_all.36.received = f32[16,4,128]{2,1,0:T(4,128)S(1)} all-to-all(f32[16,4,128]{2,1,0:T(4,128)S(1)} %get-tuple-element.47), channel_id=1, replica_groups=mesh['gx'=8,'gy_0'=4,'gy_1'=8,'gy_2'=2] {'gy_1','gy_2'}, dimensions={0} | all-to-all | bytes 65536 | tf_op jit(solution)/shard_map/all_to_all | solution.py:617
  35.7 3.6 %collective-permute-start.1 = (f32[4,4,128]{2,1,0:T(4,128)S(1)}, f32[4,4,128]{2,1,0:T(4,128)S(1)}, u32[]{:S(2)}, u32[]{:S(2)}) collective-permute-start(f32[4,4,128]{2,1,0:T(4,128)S(1)} %constant_dynamic-slice_fusion.4), channel_id=1, source_target_pairs={{0,17},{1,16},{2,19},{3,18},{16,33},{28,13},{17,32},{29,12},{18,35... | collective-permute-start | bytes 24584 | tf_op jit(solution)/shard_map/ppermute | solution.py:535
  39.3 2.3 %shard_map.107.own = f32[64,128]{1,0:T(8,128)S(1)} custom-call(s32[1]{0:T(128)} %bitcast.place_ref, s32[128,128]{1,0:T(8,128)S(1)} %get-tuple-element.34.slots, s32[8,256]{1,0:T(8,128)S(1)} %get-tuple-element.35.masters, f32[128,128]{1,0:T(8,128)S(1)} %get-tuple-element.44.products, f32[8,256]{1,0:T(8,128)S(1)} %get-tuple-element.45.back, ...), custom_call_target="tpu_custom_call" | custom-call | tf_op jit(solution)/shard_map/pallas_call | solution.py:544
  41.6 0.8 shard_map.108
  42.5 10.0 %all_to_all.37.received = f32[16,4,128]{2,1,0:T(4,128)S(1)} all-to-all(f32[16,4,128]{2,1,0:T(4,128)S(1)} %get-tuple-element.48), channel_id=1, replica_groups=mesh['gx'=8,'gy_0'=4,'gy_1'=8,'gy_2'=2] {'gy_1','gy_2'}, dimensions={0} | all-to-all | bytes 65536 | tf_op jit(solution)/shard_map/all_to_all | solution.py:586
  52.4 3.3 %collective-permute-start.2 = (f32[4,4,128]{2,1,0:T(4,128)S(1)}, f32[4,4,128]{2,1,0:T(4,128)S(1)}, u32[]{:S(2)}, u32[]{:S(2)}) collective-permute-start(f32[4,4,128]{2,1,0:T(4,128)S(1)} %constant_dynamic-slice_fusion.3), channel_id=1, source_target_pairs={{0,17},{1,16},{2,19},{3,18},{16,33},{28,13},{17,32},{29,12},{18,35... | collective-permute-start | bytes 24584 | tf_op jit(solution)/shard_map/ppermute | solution.py:535
  55.7 1.9 %shard_map.109 = (f32[128,128]{1,0:T(8,128)S(1)}, f32[8,256]{1,0:T(8,128)S(1)}) custom-call(s32[1]{0:T(128)} %bitcast.place_ref, f32[64,128]{1,0:T(8,128)S(1)} %get-tuple-element.49.vector.second, f32[16,4,128]{2,1,0:T(4,128)S(1)} %all_to_all.37.received, s32[128,128]{1,0:T(8,128)S(1)} %get-tuple-element.34.slots, s32[8,256]{1,0:T(8,128)S(1)} %get-tuple-element.35.masters), custom_call_target="tpu_custom_call" | custom-call | tf_op jit(solution)/shard_map/pallas_call | solution.py:544
  57.7 0.0 collective-permute-done.2.relayed
  57.7 2.7 %shard_map.110 = (f32[128,128]{1,0:T(8,128)S(1)}, f32[16,4,128]{2,1,0:T(4,128)S(1)}, f32[8,256]{1,0:T(8,128)S(1)}) custom-call(s32[1]{0:T(128)} %bitcast.place_ref, f32[16,4,128]{2,1,0:T(4,128)S(1)} %all_to_all.37.received, f32[4,4,128]{2,1,0:T(4,128)S(1)} %collective-permute-done.2.relayed, f32[128,128]{1,0:T(8,128)S(1)} %get-tuple-element.50.cell_part, ...), custom_call_target="tpu_custom_call" | custom-call | tf_op jit(solution)/shard_map/pallas_call | solution.py:544
  60.4 10.0 %all_to_all.38.received = f32[16,4,128]{2,1,0:T(4,128)S(1)} all-to-all(f32[16,4,128]{2,1,0:T(4,128)S(1)} %get-tuple-element.54), channel_id=1, replica_groups=mesh['gx'=8,'gy_0'=4,'gy_1'=8,'gy_2'=2] {'gy_1','gy_2'}, dimensions={0} | all-to-all | bytes 65536 | tf_op jit(solution)/shard_map/all_to_all | solution.py:617
  70.4 4.6 %collective-permute-start.3 = (f32[4,4,128]{2,1,0:T(4,128)S(1)}, f32[4,4,128]{2,1,0:T(4,128)S(1)}, u32[]{:S(2)}, u32[]{:S(2)}) collective-permute-start(f32[4,4,128]{2,1,0:T(4,128)S(1)} %constant_dynamic-slice_fusion.2), channel_id=1, source_target_pairs={{0,17},{1,16},{2,19},{3,18},{16,33},{28,13},{17,32},{29,12},{18,35... | collective-permute-start | bytes 24584 | tf_op jit(solution)/shard_map/ppermute | solution.py:535
  75.0 2.3 %shard_map.111.own = f32[64,128]{1,0:T(8,128)S(1)} custom-call(s32[1]{0:T(128)} %bitcast.place_ref, s32[128,128]{1,0:T(8,128)S(1)} %get-tuple-element.34.slots, s32[8,256]{1,0:T(8,128)S(1)} %get-tuple-element.35.masters, f32[128,128]{1,0:T(8,128)S(1)} %get-tuple-element.52.products, f32[8,256]{1,0:T(8,128)S(1)} %get-tuple-element.53.back, ...), custom_call_target="tpu_custom_call" | custom-call | tf_op jit(solution)/shard_map/pallas_call | solution.py:544
  77.3 0.8 shard_map.112
  78.1 10.0 %all_to_all.39.received = f32[16,4,128]{2,1,0:T(4,128)S(1)} all-to-all(f32[16,4,128]{2,1,0:T(4,128)S(1)} %get-tuple-element.55), channel_id=1, replica_groups=mesh['gx'=8,'gy_0'=4,'gy_1'=8,'gy_2'=2] {'gy_1','gy_2'}, dimensions={0} | all-to-all | bytes 65536 | tf_op jit(solution)/shard_map/all_to_all | solution.py:586
  88.1 4.9 %collective-permute-start.4 = (f32[4,4,128]{2,1,0:T(4,128)S(1)}, f32[4,4,128]{2,1,0:T(4,128)S(1)}, u32[]{:S(2)}, u32[]{:S(2)}) collective-permute-start(f32[4,4,128]{2,1,0:T(4,128)S(1)} %constant_dynamic-slice_fusion.1), channel_id=1, source_target_pairs={{0,17},{1,16},{2,19},{3,18},{16,33},{28,13},{17,32},{29,12},{18,35... | collective-permute-start | bytes 24584 | tf_op jit(solution)/shard_map/ppermute | solution.py:535
  93.1 1.9 %shard_map.113 = (f32[128,128]{1,0:T(8,128)S(1)}, f32[8,256]{1,0:T(8,128)S(1)}) custom-call(s32[1]{0:T(128)} %bitcast.place_ref, f32[64,128]{1,0:T(8,128)S(1)} %get-tuple-element.56.vector.third, f32[16,4,128]{2,1,0:T(4,128)S(1)} %all_to_all.39.received, s32[128,128]{1,0:T(8,128)S(1)} %get-tuple-element.34.slots, s32[8,256]{1,0:T(8,128)S(1)} %get-tuple-element.35.masters), custom_call_target="tpu_custom_call" | custom-call | tf_op jit(solution)/shard_map/pallas_call | solution.py:544
  95.0 0.0 collective-permute-done.4.relayed
  95.0 2.7 %shard_map.114 = (f32[128,128]{1,0:T(8,128)S(1)}, f32[16,8,128]{2,1,0:T(8,128)S(1)}, f32[8,256]{1,0:T(8,128)S(1)}) custom-call(s32[1]{0:T(128)} %bitcast.place_ref, f32[16,4,128]{2,1,0:T(4,128)S(1)} %all_to_all.39.received, f32[4,4,128]{2,1,0:T(4,128)S(1)} %collective-permute-done.4.relayed, f32[128,128]{1,0:T(8,128)S(1)} %get-tuple-element.57.cell_part, ...), custom_call_target="tpu_custom_call" | custom-call | tf_op jit(solution)/shard_map/pallas_call | solution.py:544
  97.7 10.3 %all_to_all.40.received = f32[16,8,128]{2,1,0:T(8,128)S(1)} all-to-all(f32[16,8,128]{2,1,0:T(8,128)S(1)} %get-tuple-element.59), channel_id=1, replica_groups=mesh['gx'=8,'gy_0'=4,'gy_1'=8,'gy_2'=2] {'gy_1','gy_2'}, dimensions={0} | all-to-all | bytes 131072 | tf_op jit(solution)/shard_map/all_to_all | solution.py:617
  108.0 0.6 shard_map.115
  108.7 22.9 %all-to-all-start.6 = ((f32[32,1,128]{2,1,0:T(1,128)}), f32[32,1,128]{2,1,0:T(1,128)S(1)}, u32[]{:S(2)}, u32[]{:S(2)}) async-start(f32[32,1,128]{2,1,0:T(1,128)} %shard_map.115), calls=%async_computation.6 | async-start | bytes 32768 | tf_op jit(solution)/shard_map/all_to_all | solution.py:631
  131.6 3.7 %collective-permute-start.5 = (f32[4,4,128]{2,1,0:T(4,128)S(1)}, f32[4,4,128]{2,1,0:T(4,128)S(1)}, u32[]{:S(2)}, u32[]{:S(2)}) collective-permute-start(f32[4,4,128]{2,1,0:T(4,128)S(1)} %constant_dynamic-slice_fusion), channel_id=1, source_target_pairs={{0,17},{1,16},{2,19},{3,18},{16,33},{28,13},{17,32},{29,12},{18,35... | collective-permute-start | bytes 24584 | tf_op jit(solution)/shard_map/ppermute | solution.py:535
  135.4 2.3 %shard_map.116.own = f32[64,128]{1,0:T(8,128)S(1)} custom-call(s32[1]{0:T(128)} %bitcast.place_ref, s32[128,128]{1,0:T(8,128)S(1)} %get-tuple-element.34.slots, s32[8,256]{1,0:T(8,128)S(1)} %get-tuple-element.35.masters, f32[128,128]{1,0:T(8,128)S(1)} %get-tuple-element.60.products, f32[8,256]{1,0:T(8,128)S(1)} %get-tuple-element.61.back, ...), custom_call_target="tpu_custom_call" | custom-call | tf_op jit(solution)/shard_map/pallas_call | solution.py:544
  137.7 0.4 shard_map.117.fourth
  138.1 2.0 %all-to-all-done.6.moments = f32[32,1,128]{2,1,0:T(1,128)S(1)} async-done(((f32[32,1,128]{2,1,0:T(1,128)}), f32[32,1,128]{2,1,0:T(1,128)S(1)}, u32[]{:S(2)}, u32[]{:S(2)}) %all-to-all-start.6) | async-done | bytes 16416 | tf_op jit(solution)/shard_map/all_to_all | solution.py:631
  140.2 0.8 shard_map.118
  (11 shorter events, 0.0 us)
Async XLA Ops:
  18.7 4.4 %collective-permute-start = (f32[4,4,128]{2,1,0:T(4,128)S(1)}, f32[4,4,128]{2,1,0:T(4,128)S(1)}, u32[]{:S(2)}, u32[]{:S(2)}) collective-permute-start(f32[4,4,128]{2,1,0:T(4,128)S(1)} %constant_dynamic-slice_fusion.5), channel_id=1, source_target_pairs={{0,17},{1,16},{2,19},{3,18},{16,33},{28,13},{17,32},{29,12},{18,35... | collective-permute-start | bytes 24584 | tf_op jit(solution)/shard_map/ppermute | solution.py:535
  35.7 3.6 %copy-start = (s32[8,512]{1,0:T(8,128)S(1)}, s32[8,512]{1,0:T(8,128)}, u32[]{:S(2)}) copy-start(s32[8,512]{1,0:T(8,128)} %lists.13) | copy-start | bytes 49156
  35.7 5.9 %collective-permute-start.1 = (f32[4,4,128]{2,1,0:T(4,128)S(1)}, f32[4,4,128]{2,1,0:T(4,128)S(1)}, u32[]{:S(2)}, u32[]{:S(2)}) collective-permute-start(f32[4,4,128]{2,1,0:T(4,128)S(1)} %constant_dynamic-slice_fusion.4), channel_id=1, source_target_pairs={{0,17},{1,16},{2,19},{3,18},{16,33},{28,13},{17,32},{29,12},{18,35... | collective-permute-start | bytes 24584 | tf_op jit(solution)/shard_map/ppermute | solution.py:535
  52.4 5.2 %collective-permute-start.2 = (f32[4,4,128]{2,1,0:T(4,128)S(1)}, f32[4,4,128]{2,1,0:T(4,128)S(1)}, u32[]{:S(2)}, u32[]{:S(2)}) collective-permute-start(f32[4,4,128]{2,1,0:T(4,128)S(1)} %constant_dynamic-slice_fusion.3), channel_id=1, source_target_pairs={{0,17},{1,16},{2,19},{3,18},{16,33},{28,13},{17,32},{29,12},{18,35... | collective-permute-start | bytes 24584 | tf_op jit(solution)/shard_map/ppermute | solution.py:535
  70.4 6.9 %collective-permute-start.3 = (f32[4,4,128]{2,1,0:T(4,128)S(1)}, f32[4,4,128]{2,1,0:T(4,128)S(1)}, u32[]{:S(2)}, u32[]{:S(2)}) collective-permute-start(f32[4,4,128]{2,1,0:T(4,128)S(1)} %constant_dynamic-slice_fusion.2), channel_id=1, source_target_pairs={{0,17},{1,16},{2,19},{3,18},{16,33},{28,13},{17,32},{29,12},{18,35... | collective-permute-start | bytes 24584 | tf_op jit(solution)/shard_map/ppermute | solution.py:535
  88.1 6.9 %collective-permute-start.4 = (f32[4,4,128]{2,1,0:T(4,128)S(1)}, f32[4,4,128]{2,1,0:T(4,128)S(1)}, u32[]{:S(2)}, u32[]{:S(2)}) collective-permute-start(f32[4,4,128]{2,1,0:T(4,128)S(1)} %constant_dynamic-slice_fusion.1), channel_id=1, source_target_pairs={{0,17},{1,16},{2,19},{3,18},{16,33},{28,13},{17,32},{29,12},{18,35... | collective-permute-start | bytes 24584 | tf_op jit(solution)/shard_map/ppermute | solution.py:535
  108.7 31.5 %all-to-all-start.6 = ((f32[32,1,128]{2,1,0:T(1,128)}), f32[32,1,128]{2,1,0:T(1,128)S(1)}, u32[]{:S(2)}, u32[]{:S(2)}) async-start(f32[32,1,128]{2,1,0:T(1,128)} %shard_map.115), calls=%async_computation.6 | async-start | bytes 32768 | tf_op jit(solution)/shard_map/all_to_all | solution.py:631
  131.6 6.1 %collective-permute-start.5 = (f32[4,4,128]{2,1,0:T(4,128)S(1)}, f32[4,4,128]{2,1,0:T(4,128)S(1)}, u32[]{:S(2)}, u32[]{:S(2)}) collective-permute-start(f32[4,4,128]{2,1,0:T(4,128)S(1)} %constant_dynamic-slice_fusion), channel_id=1, source_target_pairs={{0,17},{1,16},{2,19},{3,18},{16,33},{28,13},{17,32},{29,12},{18,35... | collective-permute-start | bytes 24584 | tf_op jit(solution)/shard_map/ppermute | solution.py:535

commit v6 on v5

--- a/solution.py
+++ b/solution.py
@@ -218,7 +218,8 @@
             interp[...], jnp.broadcast_to(con_row[:, lanes], (8, 128))
         )
     scale[...] = jnp.exp2(-level[...].astype(F32))
-    stiffness[...] = stiffness_in[...]
+    one, two, three = split(stiffness_in[...])
+    stiffness[...] = jnp.concatenate([one, two, three, one, two, one], axis=1)
     reaction[...] = reaction_in[...]
 
 
@@ -271,10 +272,10 @@
         at = slots[group_rows, :]
         values = pick(table, at, 0, 16, cell_part[group_rows, :], base)
         cell_values[group_rows, :] = pick(table, at, 16, 18, values, LOCAL_ROWS - 16)
+    one, two, three = split(cell_values[...])
     products[...] = jnp.dot(
         stiffness[...],
-        cell_values[...],
-        precision=lax.Precision.HIGHEST,
+        jnp.concatenate([three, two, one, two, one, one], axis=0),
         preferred_element_type=F32,
     ) * scale[...]
 
@@ -563,7 +564,7 @@
             jax.ShapeDtypeStruct((8, 256), I32),
             con_padded,
             jax.ShapeDtypeStruct((1, 128), F32),
-            padded,
+            jax.ShapeDtypeStruct((128, 768), BF16),
             tile,
         ),
         (

time: 142 us -> 142 us (level)
  no operation moved by 1% of the time
where the time goes in v6:
time: 142 us; the launch traced here: 141 us
  blocking collectives  66.9 us (47%)
  starting transfers between devices  45.5 us (32%)
  Pallas kernels  25.6 us (18%)
  waiting for transfers between devices  2.05 us (1%)
    all_to_all x6, blocking collectives, on_device(): received = lax.all_to_all(packed, GROUP, 0, 0)  66.9 us
    pallas_call x15, Pallas kernels, kernel(): pl.pallas_call(body, out_shape=jax.tree.map(lambda out: pltpu.VMEM(out.sh...  25.6 us
    all_to_all x1, starting transfers between devices, on_device(): moments = lax.all_to_all(sums, REST, 0, 0)  22.9 us
    ppermute x6, starting transfers between devices, relay(): return lax.ppermute(rows, AXES, pairs)  22.6 us
  transfers between devices with their start and end apart: 7, of which 1 were waited for; matrix products, arithmetic and copies ran while one was open for 0% of the time, Pallas kernels for 9%

profile of v6, /device:TPU:1, one launch (start us, length us, event | category | flops | bytes accessed | tf_op | source)
XLA Modules:
  0.0 140.9 jit_solution(13194141318563882101)
XLA Ops:
  0.6 1.3 shard_map.104
  2.0 16.7 %all_to_all.35.received = f32[16,4,128]{2,1,0:T(4,128)S(1)} all-to-all(f32[16,4,128]{2,1,0:T(4,128)S(1)} %get-tuple-element.36), channel_id=1, replica_groups=mesh['gx'=8,'gy_0'=4,'gy_1'=8,'gy_2'=2] {'gy_1','gy_2'}, dimensions={0} | all-to-all | bytes 65536 | tf_op jit(solution)/shard_map/all_to_all | solution.py:587
  18.7 2.5 %collective-permute-start = (f32[4,4,128]{2,1,0:T(4,128)S(1)}, f32[4,4,128]{2,1,0:T(4,128)S(1)}, u32[]{:S(2)}, u32[]{:S(2)}) collective-permute-start(f32[4,4,128]{2,1,0:T(4,128)S(1)} %constant_dynamic-slice_fusion.5), channel_id=1, source_target_pairs={{0,17},{1,16},{2,19},{3,18},{16,33},{28,13},{17,32},{29,12},{18,35... | collective-permute-start | bytes 24584 | tf_op jit(solution)/shard_map/ppermute | solution.py:536
  21.1 1.9 %shard_map.105 = (f32[128,128]{1,0:T(8,128)S(1)}, f32[8,256]{1,0:T(8,128)S(1)}) custom-call(s32[1]{0:T(128)} %bitcast.place_ref, f32[64,128]{1,0:T(8,128)S(1)} %get-tuple-element.38.vector.first, f32[16,4,128]{2,1,0:T(4,128)S(1)} %all_to_all.35.received, s32[128,128]{1,0:T(8,128)S(1)} %get-tuple-element.34.slots, s32[8,256]{1,0:T(8,128)S(1)} %get-tuple-element.35.masters), custom_call_target="tpu_custom_call" | custom-call | tf_op jit(solution)/shard_map/pallas_call | solution.py:545
  23.1 0.0 collective-permute-done.relayed
  23.1 2.7 %shard_map.106 = (f32[128,128]{1,0:T(8,128)S(1)}, f32[16,4,128]{2,1,0:T(4,128)S(1)}, f32[8,256]{1,0:T(8,128)S(1)}) custom-call(s32[1]{0:T(128)} %bitcast.place_ref, f32[16,4,128]{2,1,0:T(4,128)S(1)} %all_to_all.35.received, f32[4,4,128]{2,1,0:T(4,128)S(1)} %collective-permute-done.relayed, f32[128,128]{1,0:T(8,128)S(1)} %get-tuple-element.39.cell_part, ...), custom_call_target="tpu_custom_call" | custom-call | tf_op jit(solution)/shard_map/pallas_call | solution.py:545
  25.8 9.9 %all_to_all.36.received = f32[16,4,128]{2,1,0:T(4,128)S(1)} all-to-all(f32[16,4,128]{2,1,0:T(4,128)S(1)} %get-tuple-element.47), channel_id=1, replica_groups=mesh['gx'=8,'gy_0'=4,'gy_1'=8,'gy_2'=2] {'gy_1','gy_2'}, dimensions={0} | all-to-all | bytes 65536 | tf_op jit(solution)/shard_map/all_to_all | solution.py:618
  35.7 3.6 %collective-permute-start.1 = (f32[4,4,128]{2,1,0:T(4,128)S(1)}, f32[4,4,128]{2,1,0:T(4,128)S(1)}, u32[]{:S(2)}, u32[]{:S(2)}) collective-permute-start(f32[4,4,128]{2,1,0:T(4,128)S(1)} %constant_dynamic-slice_fusion.4), channel_id=1, source_target_pairs={{0,17},{1,16},{2,19},{3,18},{16,33},{28,13},{17,32},{29,12},{18,35... | collective-permute-start | bytes 24584 | tf_op jit(solution)/shard_map/ppermute | solution.py:536
  39.3 2.3 %shard_map.107.own = f32[64,128]{1,0:T(8,128)S(1)} custom-call(s32[1]{0:T(128)} %bitcast.place_ref, s32[128,128]{1,0:T(8,128)S(1)} %get-tuple-element.34.slots, s32[8,256]{1,0:T(8,128)S(1)} %get-tuple-element.35.masters, f32[128,128]{1,0:T(8,128)S(1)} %get-tuple-element.44.products, f32[8,256]{1,0:T(8,128)S(1)} %get-tuple-element.45.back, ...), custom_call_target="tpu_custom_call" | custom-call | tf_op jit(solution)/shard_map/pallas_call | solution.py:545
  41.6 0.0 collective-permute-done.1.relayed
  41.7 0.8 shard_map.108
  42.5 10.0 %all_to_all.37.received = f32[16,4,128]{2,1,0:T(4,128)S(1)} all-to-all(f32[16,4,128]{2,1,0:T(4,128)S(1)} %get-tuple-element.48), channel_id=1, replica_groups=mesh['gx'=8,'gy_0'=4,'gy_1'=8,'gy_2'=2] {'gy_1','gy_2'}, dimensions={0} | all-to-all | bytes 65536 | tf_op jit(solution)/shard_map/all_to_all | solution.py:587
  52.4 3.3 %collective-permute-start.2 = (f32[4,4,128]{2,1,0:T(4,128)S(1)}, f32[4,4,128]{2,1,0:T(4,128)S(1)}, u32[]{:S(2)}, u32[]{:S(2)}) collective-permute-start(f32[4,4,128]{2,1,0:T(4,128)S(1)} %constant_dynamic-slice_fusion.3), channel_id=1, source_target_pairs={{0,17},{1,16},{2,19},{3,18},{16,33},{28,13},{17,32},{29,12},{18,35... | collective-permute-start | bytes 24584 | tf_op jit(solution)/shard_map/ppermute | solution.py:536
  55.7 1.9 %shard_map.109 = (f32[128,128]{1,0:T(8,128)S(1)}, f32[8,256]{1,0:T(8,128)S(1)}) custom-call(s32[1]{0:T(128)} %bitcast.place_ref, f32[64,128]{1,0:T(8,128)S(1)} %get-tuple-element.49.vector.second, f32[16,4,128]{2,1,0:T(4,128)S(1)} %all_to_all.37.received, s32[128,128]{1,0:T(8,128)S(1)} %get-tuple-element.34.slots, s32[8,256]{1,0:T(8,128)S(1)} %get-tuple-element.35.masters), custom_call_target="tpu_custom_call" | custom-call | tf_op jit(solution)/shard_map/pallas_call | solution.py:545
  57.7 0.0 collective-permute-done.2.relayed
  57.7 2.7 %shard_map.110 = (f32[128,128]{1,0:T(8,128)S(1)}, f32[16,4,128]{2,1,0:T(4,128)S(1)}, f32[8,256]{1,0:T(8,128)S(1)}) custom-call(s32[1]{0:T(128)} %bitcast.place_ref, f32[16,4,128]{2,1,0:T(4,128)S(1)} %all_to_all.37.received, f32[4,4,128]{2,1,0:T(4,128)S(1)} %collective-permute-done.2.relayed, f32[128,128]{1,0:T(8,128)S(1)} %get-tuple-element.50.cell_part, ...), custom_call_target="tpu_custom_call" | custom-call | tf_op jit(solution)/shard_map/pallas_call | solution.py:545
  60.3 10.0 %all_to_all.38.received = f32[16,4,128]{2,1,0:T(4,128)S(1)} all-to-all(f32[16,4,128]{2,1,0:T(4,128)S(1)} %get-tuple-element.54), channel_id=1, replica_groups=mesh['gx'=8,'gy_0'=4,'gy_1'=8,'gy_2'=2] {'gy_1','gy_2'}, dimensions={0} | all-to-all | bytes 65536 | tf_op jit(solution)/shard_map/all_to_all | solution.py:618
  70.3 4.6 %collective-permute-start.3 = (f32[4,4,128]{2,1,0:T(4,128)S(1)}, f32[4,4,128]{2,1,0:T(4,128)S(1)}, u32[]{:S(2)}, u32[]{:S(2)}) collective-permute-start(f32[4,4,128]{2,1,0:T(4,128)S(1)} %constant_dynamic-slice_fusion.2), channel_id=1, source_target_pairs={{0,17},{1,16},{2,19},{3,18},{16,33},{28,13},{17,32},{29,12},{18,35... | collective-permute-start | bytes 24584 | tf_op jit(solution)/shard_map/ppermute | solution.py:536
  74.9 2.3 %shard_map.111.own = f32[64,128]{1,0:T(8,128)S(1)} custom-call(s32[1]{0:T(128)} %bitcast.place_ref, s32[128,128]{1,0:T(8,128)S(1)} %get-tuple-element.34.slots, s32[8,256]{1,0:T(8,128)S(1)} %get-tuple-element.35.masters, f32[128,128]{1,0:T(8,128)S(1)} %get-tuple-element.52.products, f32[8,256]{1,0:T(8,128)S(1)} %get-tuple-element.53.back, ...), custom_call_target="tpu_custom_call" | custom-call | tf_op jit(solution)/shard_map/pallas_call | solution.py:545
  77.3 0.8 shard_map.112
  78.1 10.0 %all_to_all.39.received = f32[16,4,128]{2,1,0:T(4,128)S(1)} all-to-all(f32[16,4,128]{2,1,0:T(4,128)S(1)} %get-tuple-element.55), channel_id=1, replica_groups=mesh['gx'=8,'gy_0'=4,'gy_1'=8,'gy_2'=2] {'gy_1','gy_2'}, dimensions={0} | all-to-all | bytes 65536 | tf_op jit(solution)/shard_map/all_to_all | solution.py:587
  88.1 5.0 %collective-permute-start.4 = (f32[4,4,128]{2,1,0:T(4,128)S(1)}, f32[4,4,128]{2,1,0:T(4,128)S(1)}, u32[]{:S(2)}, u32[]{:S(2)}) collective-permute-start(f32[4,4,128]{2,1,0:T(4,128)S(1)} %constant_dynamic-slice_fusion.1), channel_id=1, source_target_pairs={{0,17},{1,16},{2,19},{3,18},{16,33},{28,13},{17,32},{29,12},{18,35... | collective-permute-start | bytes 24584 | tf_op jit(solution)/shard_map/ppermute | solution.py:536
  93.1 1.9 %shard_map.113 = (f32[128,128]{1,0:T(8,128)S(1)}, f32[8,256]{1,0:T(8,128)S(1)}) custom-call(s32[1]{0:T(128)} %bitcast.place_ref, f32[64,128]{1,0:T(8,128)S(1)} %get-tuple-element.56.vector.third, f32[16,4,128]{2,1,0:T(4,128)S(1)} %all_to_all.39.received, s32[128,128]{1,0:T(8,128)S(1)} %get-tuple-element.34.slots, s32[8,256]{1,0:T(8,128)S(1)} %get-tuple-element.35.masters), custom_call_target="tpu_custom_call" | custom-call | tf_op jit(solution)/shard_map/pallas_call | solution.py:545
  95.0 2.7 %shard_map.114 = (f32[128,128]{1,0:T(8,128)S(1)}, f32[16,8,128]{2,1,0:T(8,128)S(1)}, f32[8,256]{1,0:T(8,128)S(1)}) custom-call(s32[1]{0:T(128)} %bitcast.place_ref, f32[16,4,128]{2,1,0:T(4,128)S(1)} %all_to_all.39.received, f32[4,4,128]{2,1,0:T(4,128)S(1)} %collective-permute-done.4.relayed, f32[128,128]{1,0:T(8,128)S(1)} %get-tuple-element.57.cell_part, ...), custom_call_target="tpu_custom_call" | custom-call | tf_op jit(solution)/shard_map/pallas_call | solution.py:545
  97.7 10.3 %all_to_all.40.received = f32[16,8,128]{2,1,0:T(8,128)S(1)} all-to-all(f32[16,8,128]{2,1,0:T(8,128)S(1)} %get-tuple-element.59), channel_id=1, replica_groups=mesh['gx'=8,'gy_0'=4,'gy_1'=8,'gy_2'=2] {'gy_1','gy_2'}, dimensions={0} | all-to-all | bytes 131072 | tf_op jit(solution)/shard_map/all_to_all | solution.py:618
  108.1 0.6 shard_map.115
  108.7 22.9 %all-to-all-start.6 = ((f32[32,1,128]{2,1,0:T(1,128)}), f32[32,1,128]{2,1,0:T(1,128)S(1)}, u32[]{:S(2)}, u32[]{:S(2)}) async-start(f32[32,1,128]{2,1,0:T(1,128)} %shard_map.115), calls=%async_computation.6 | async-start | bytes 32768 | tf_op jit(solution)/shard_map/all_to_all | solution.py:632
  131.6 3.7 %collective-permute-start.5 = (f32[4,4,128]{2,1,0:T(4,128)S(1)}, f32[4,4,128]{2,1,0:T(4,128)S(1)}, u32[]{:S(2)}, u32[]{:S(2)}) collective-permute-start(f32[4,4,128]{2,1,0:T(4,128)S(1)} %constant_dynamic-slice_fusion), channel_id=1, source_target_pairs={{0,17},{1,16},{2,19},{3,18},{16,33},{28,13},{17,32},{29,12},{18,35... | collective-permute-start | bytes 24584 | tf_op jit(solution)/shard_map/ppermute | solution.py:536
  135.4 2.3 %shard_map.116.own = f32[64,128]{1,0:T(8,128)S(1)} custom-call(s32[1]{0:T(128)} %bitcast.place_ref, s32[128,128]{1,0:T(8,128)S(1)} %get-tuple-element.34.slots, s32[8,256]{1,0:T(8,128)S(1)} %get-tuple-element.35.masters, f32[128,128]{1,0:T(8,128)S(1)} %get-tuple-element.60.products, f32[8,256]{1,0:T(8,128)S(1)} %get-tuple-element.61.back, ...), custom_call_target="tpu_custom_call" | custom-call | tf_op jit(solution)/shard_map/pallas_call | solution.py:545
  137.7 0.4 shard_map.117.fourth
  138.1 2.0 %all-to-all-done.6.moments = f32[32,1,128]{2,1,0:T(1,128)S(1)} async-done(((f32[32,1,128]{2,1,0:T(1,128)}), f32[32,1,128]{2,1,0:T(1,128)S(1)}, u32[]{:S(2)}, u32[]{:S(2)}) %all-to-all-start.6) | async-done | bytes 16416 | tf_op jit(solution)/shard_map/all_to_all | solution.py:632
  140.1 0.8 shard_map.118
  (11 shorter events, 0.0 us)
Async XLA Ops:
  18.7 4.4 %collective-permute-start = (f32[4,4,128]{2,1,0:T(4,128)S(1)}, f32[4,4,128]{2,1,0:T(4,128)S(1)}, u32[]{:S(2)}, u32[]{:S(2)}) collective-permute-start(f32[4,4,128]{2,1,0:T(4,128)S(1)} %constant_dynamic-slice_fusion.5), channel_id=1, source_target_pairs={{0,17},{1,16},{2,19},{3,18},{16,33},{28,13},{17,32},{29,12},{18,35... | collective-permute-start | bytes 24584 | tf_op jit(solution)/shard_map/ppermute | solution.py:536
  35.7 3.6 %copy-start = (s32[8,512]{1,0:T(8,128)S(1)}, s32[8,512]{1,0:T(8,128)}, u32[]{:S(2)}) copy-start(s32[8,512]{1,0:T(8,128)} %lists.13) | copy-start | bytes 49156
  35.7 5.9 %collective-permute-start.1 = (f32[4,4,128]{2,1,0:T(4,128)S(1)}, f32[4,4,128]{2,1,0:T(4,128)S(1)}, u32[]{:S(2)}, u32[]{:S(2)}) collective-permute-start(f32[4,4,128]{2,1,0:T(4,128)S(1)} %constant_dynamic-slice_fusion.4), channel_id=1, source_target_pairs={{0,17},{1,16},{2,19},{3,18},{16,33},{28,13},{17,32},{29,12},{18,35... | collective-permute-start | bytes 24584 | tf_op jit(solution)/shard_map/ppermute | solution.py:536
  52.4 5.2 %collective-permute-start.2 = (f32[4,4,128]{2,1,0:T(4,128)S(1)}, f32[4,4,128]{2,1,0:T(4,128)S(1)}, u32[]{:S(2)}, u32[]{:S(2)}) collective-permute-start(f32[4,4,128]{2,1,0:T(4,128)S(1)} %constant_dynamic-slice_fusion.3), channel_id=1, source_target_pairs={{0,17},{1,16},{2,19},{3,18},{16,33},{28,13},{17,32},{29,12},{18,35... | collective-permute-start | bytes 24584 | tf_op jit(solution)/shard_map/ppermute | solution.py:536
  70.3 6.9 %collective-permute-start.3 = (f32[4,4,128]{2,1,0:T(4,128)S(1)}, f32[4,4,128]{2,1,0:T(4,128)S(1)}, u32[]{:S(2)}, u32[]{:S(2)}) collective-permute-start(f32[4,4,128]{2,1,0:T(4,128)S(1)} %constant_dynamic-slice_fusion.2), channel_id=1, source_target_pairs={{0,17},{1,16},{2,19},{3,18},{16,33},{28,13},{17,32},{29,12},{18,35... | collective-permute-start | bytes 24584 | tf_op jit(solution)/shard_map/ppermute | solution.py:536
  88.1 7.0 %collective-permute-start.4 = (f32[4,4,128]{2,1,0:T(4,128)S(1)}, f32[4,4,128]{2,1,0:T(4,128)S(1)}, u32[]{:S(2)}, u32[]{:S(2)}) collective-permute-start(f32[4,4,128]{2,1,0:T(4,128)S(1)} %constant_dynamic-slice_fusion.1), channel_id=1, source_target_pairs={{0,17},{1,16},{2,19},{3,18},{16,33},{28,13},{17,32},{29,12},{18,35... | collective-permute-start | bytes 24584 | tf_op jit(solution)/shard_map/ppermute | solution.py:536
  108.7 31.5 %all-to-all-start.6 = ((f32[32,1,128]{2,1,0:T(1,128)}), f32[32,1,128]{2,1,0:T(1,128)S(1)}, u32[]{:S(2)}, u32[]{:S(2)}) async-start(f32[32,1,128]{2,1,0:T(1,128)} %shard_map.115), calls=%async_computation.6 | async-start | bytes 32768 | tf_op jit(solution)/shard_map/all_to_all | solution.py:632
  131.6 6.1 %collective-permute-start.5 = (f32[4,4,128]{2,1,0:T(4,128)S(1)}, f32[4,4,128]{2,1,0:T(4,128)S(1)}, u32[]{:S(2)}, u32[]{:S(2)}) collective-permute-start(f32[4,4,128]{2,1,0:T(4,128)S(1)} %constant_dynamic-slice_fusion), channel_id=1, source_target_pairs={{0,17},{1,16},{2,19},{3,18},{16,33},{28,13},{17,32},{29,12},{18,35... | collective-permute-start | bytes 24584 | tf_op jit(solution)/shard_map/ppermute | solution.py:536
